TPU v7x, 32 devices: a whole 2x2x4 slice. The times are simulated.
32 devices in a mesh: rep: 8 (over y, x, core), shard: 4 (over z).
Axes of the slice: x: 2, y: 2, z: 4, core: 2. Of those that a mesh axis runs over, the one named last changes fastest.
Arguments:
- tokens: bfloat16 [32, 512, 2048], P(('rep', 'shard')), may hold values from -6 to 6
- segments: int32 [32, 512], P(('rep', 'shard')), may hold values from 0 to 7, never falling along the last dimension, each value on 1 to 256 neighbouring positions
- cotangent: bfloat16 [32, 512, 2048], P(('rep', 'shard')), may hold values from -6 to 6
- gain: float32 [2048], P('shard'), may hold values from 0.5 to 1.5
- w_query: float32 [2048, 1024], P('shard'), may hold values from -0.125 to 0.125
- w_key: float32 [2048, 256], P('shard'), may hold values from -0.125 to 0.125
- w_value: float32 [2048, 256], P('shard'), may hold values from -0.125 to 0.125
- w_outproj: float32 [1024, 2048], P('shard'), may hold values from -0.75 to 0.75
- moment_gain: float32 [2048], P('shard'), may hold values from -160 to 160
- moment_query: float32 [2048, 1024], P('shard'), may hold values from -224 to 224
- moment_key: float32 [2048, 256], P('shard'), may hold values from -224 to 224
- moment_value: float32 [2048, 256], P('shard'), may hold values from -384 to 384
- moment_outproj: float32 [1024, 2048], P('shard'), may hold values from -40 to 40
Outputs:
- output: bfloat16 [32, 512, 2048], P(('rep', 'shard'))
- grad_input: bfloat16 [32, 512, 2048], P(('rep', 'shard'))
- grad_gain: float32 [2048], P('shard')
- grad_query: float32 [2048, 1024], P('shard')
- grad_key: float32 [2048, 256], P('shard')
- grad_value: float32 [2048, 256], P('shard')
- grad_outproj: float32 [1024, 2048], P('shard')
- gain_next: float32 [2048], P('shard')
- query_next: float32 [2048, 1024], P('shard', 'rep')
- key_next: float32 [2048, 256], P('shard', 'rep')
- value_next: float32 [2048, 256], P('shard', 'rep')
- outproj_next: float32 [1024, 2048], P('shard', 'rep')
- moment_gain_next: float32 [2048], P('shard')
- moment_query_next: float32 [2048, 1024], P('shard')
- moment_key_next: float32 [2048, 256], P('shard')
- moment_value_next: float32 [2048, 256], P('shard')
- moment_outproj_next: float32 [1024, 2048], P('shard')
Inputs may be any that keep to these rules, and one draw needn't show every extreme that they name: `segments`: within a sequence ids never fall; every one of the 8 ids appears, each document has 1 to 256 tokens, and one has exactly 256.
All inputs are finite; a program needn't handle non-finite values.
Results may differ from a plain program's by a relative error of at most 0.012.
The roundings to bfloat16 on the way count: a program that leaves them out, or rounds other values in their place, can miss the bound.
Values may be sent and summed in bfloat16 or wider, within the bound.
A program may use at most 320 MiB of HBM per device.

v0:
```python
import math

import jax
import jax.numpy as jnp
from jax import lax
from jax.sharding import PartitionSpec as P

HEAD_SIZE = 64


norm_eps = 1e-05
rope_base = 500000.0
coef_a = 3.4445
coef_b = -4.775
coef_c = 2.0315
decay = 0.95
muon_rate = 0.02
gain_rate = 0.2


def from_root(block, axis, source):
    block = jnp.where(lax.axis_index(axis) == source, block, jnp.zeros_like(block))
    return lax.psum(block, axis)


def positions_of(seq_segments):
    sequence_length = seq_segments.shape[0]
    token_index = jnp.arange(sequence_length, dtype=jnp.int32)
    before = jnp.concatenate([seq_segments[:1] - 1, seq_segments[:-1]])
    starts = jnp.where(seq_segments != before, token_index, jnp.zeros_like(token_index))
    return token_index - lax.cummax(starts, axis=0)


def rope_tables(seq_segments, head_dim):
    position = positions_of(seq_segments).astype(jnp.float32)
    half_dim = head_dim // 2
    frequency = rope_base ** (-2.0 * jnp.arange(half_dim, dtype=jnp.float32) / head_dim)
    angles = position[:, None] * frequency[None, :]
    return (jnp.cos(angles)[:, None, :], jnp.sin(angles)[:, None, :])


def apply_rotary(values, cosine_table, sine_table):
    half_dim = values.shape[-1] // 2
    front_half = values[..., :half_dim]
    back_half = values[..., half_dim:]
    return jnp.concatenate(
        [
            front_half * cosine_table - back_half * sine_table,
            back_half * cosine_table + front_half * sine_table,
        ],
        -1,
    )


def unrotate(gradient, cosine_table, sine_table):
    half_dim = gradient.shape[-1] // 2
    front_half = gradient[..., :half_dim]
    back_half = gradient[..., half_dim:]
    return jnp.concatenate(
        [
            front_half * cosine_table + back_half * sine_table,
            back_half * cosine_table - front_half * sine_table,
        ],
        -1,
    )


def contract_rows(left, right):
    return lax.dot_general(
        left, right, (((0,), (0,)), ((), ())), preferred_element_type=jnp.float32
    )


def contract_cols(left, right):
    return lax.dot_general(
        left, right, (((1,), (1,)), ((), ())), preferred_element_type=jnp.float32
    )


def head_forward(q_head, k_head, v_head, allowed, score_scale):
    scores = (
        jnp.einsum("qgd,kd->gqk", q_head, k_head, preferred_element_type=jnp.float32) * score_scale
    )
    exponent = jnp.where(allowed[None], jnp.exp(scores), jnp.zeros_like(scores))
    denom_sum = jnp.sum(exponent, -1, keepdims=True)
    probabilities = (exponent / denom_sum).astype(jnp.bfloat16)
    attended = jnp.einsum("gqk,kd->qgd", probabilities, v_head, preferred_element_type=jnp.float32)
    return (attended, jnp.log(denom_sum))


def head_backward(q_head, k_head, v_head, log_sum, grad_head, allowed, score_scale):
    scores = (
        jnp.einsum("qgd,kd->gqk", q_head, k_head, preferred_element_type=jnp.float32) * score_scale
    )
    recomputed = jnp.where(allowed[None], jnp.exp(scores - log_sum), jnp.zeros_like(scores))
    rounded = recomputed.astype(jnp.bfloat16)
    value_grad = jnp.einsum("gqk,qgd->kd", rounded, grad_head, preferred_element_type=jnp.float32)
    prob_grad = jnp.einsum("qgd,kd->gqk", grad_head, v_head, preferred_element_type=jnp.float32)
    row_inner = jnp.sum(recomputed * prob_grad, -1, keepdims=True)
    score_grad = (recomputed * (prob_grad - row_inner) * score_scale).astype(jnp.bfloat16)
    query_grad = jnp.einsum("gqk,kd->qgd", score_grad, k_head, preferred_element_type=jnp.float32)
    key_grad = jnp.einsum("gqk,qgd->kd", score_grad, q_head, preferred_element_type=jnp.float32)
    return (query_grad, key_grad, value_grad)


def orthogonalize(matrix):
    is_tall = matrix.shape[0] > matrix.shape[1]
    iterate = matrix.T if is_tall else matrix
    iterate = iterate / (jnp.sqrt(jnp.sum(iterate * iterate)) + 1e-06)
    for sweep in range(5):
        square = jnp.dot(iterate, iterate.T, precision=lax.Precision.HIGHEST)
        polynomial = coef_b * square + coef_c * jnp.dot(
            square, square, precision=lax.Precision.HIGHEST
        )
        iterate = coef_a * iterate + jnp.dot(polynomial, iterate, precision=lax.Precision.HIGHEST)
    return iterate.T if is_tall else iterate


def column_block(matrix, rep_index, n_rep):
    block_width = matrix.shape[1] // n_rep
    return lax.dynamic_slice_in_dim(matrix, rep_index * block_width, block_width, 1)


def on_device(
    tokens,
    segments,
    cotangent,
    gain,
    w_query,
    w_key,
    w_value,
    w_outproj,
    moment_gain,
    moment_query,
    moment_key,
    moment_value,
    moment_outproj,
):
    n_rep = lax.axis_size("rep")
    n_shard = lax.axis_size("shard")
    rep_index = lax.axis_index("rep")
    shard_index = lax.axis_index("shard")
    sequence_length = tokens.shape[1]
    query_width = w_query.shape[1]
    kv_width = w_key.shape[1]
    query_heads = query_width // HEAD_SIZE
    kv_heads = kv_width // HEAD_SIZE
    group_width = query_heads // kv_heads
    score_scale = 1.0 / math.sqrt(HEAD_SIZE)
    total_tokens = tokens.shape[0] * sequence_length * n_rep * n_shard
    seq_tokens = tokens[0]
    seq_segments = segments[0]
    seq_cotangent = cotangent[0]
    w_in_bf = jnp.concatenate([w_query, w_key, w_value], 1).astype(jnp.bfloat16)
    gain_bf = gain.astype(jnp.bfloat16)
    w_out_bf = w_outproj.astype(jnp.bfloat16)
    tok_float = seq_tokens.astype(jnp.float32)
    inv_rms = lax.rsqrt(jnp.mean(tok_float * tok_float, -1, keepdims=True) + norm_eps)
    normed = tok_float * inv_rms
    w_piece = lax.all_gather(w_in_bf, "shard", axis=0, tiled=True)
    gain_piece = lax.all_gather(gain_bf, "shard", axis=0, tiled=True)
    columns = normed
    piece_norm = (columns * gain_piece.astype(jnp.float32)).astype(jnp.bfloat16)
    projected_rows = jnp.dot(piece_norm, w_piece, preferred_element_type=jnp.float32)
    cosine_table, sine_table = rope_tables(seq_segments, HEAD_SIZE)
    query_rows = apply_rotary(
        projected_rows[:, :query_width].reshape(sequence_length, query_heads, HEAD_SIZE),
        cosine_table,
        sine_table,
    ).astype(jnp.bfloat16)
    rotated_keys = apply_rotary(
        projected_rows[:, query_width : query_width + kv_width].reshape(
            sequence_length, kv_heads, HEAD_SIZE
        ),
        cosine_table,
        sine_table,
    ).astype(jnp.bfloat16)
    values_bfloat = (
        projected_rows[:, query_width + kv_width :]
        .reshape(sequence_length, kv_heads, HEAD_SIZE)
        .astype(jnp.bfloat16)
    )
    token_index = jnp.arange(sequence_length, dtype=jnp.int32)
    allowed = (token_index[None, :] <= token_index[:, None]) & (
        seq_segments[None, :] == seq_segments[:, None]
    )
    query_head_rows = query_rows.reshape(
        sequence_length, kv_heads, group_width, HEAD_SIZE
    ).transpose(1, 0, 2, 3)
    k_heads = rotated_keys.transpose(1, 0, 2)
    v_heads = values_bfloat.transpose(1, 0, 2)
    attended, log_sum = lax.map(
        lambda blocks: head_forward(blocks[0], blocks[1], blocks[2], allowed, score_scale),
        (query_head_rows, k_heads, v_heads),
    )
    attn_bf = (
        attended.transpose(1, 0, 2, 3).reshape(sequence_length, query_width).astype(jnp.bfloat16)
    )
    columns = attn_bf
    branch_out = jnp.dot(
        columns,
        lax.all_gather(w_out_bf, "shard", axis=0, tiled=True),
        preferred_element_type=jnp.float32,
    )
    result = (tok_float + branch_out).astype(jnp.bfloat16)
    w_in_all, gain_all, w_out_all = (
        lax.all_gather(w_in_bf, "shard", axis=0, tiled=True),
        lax.all_gather(gain_bf, "shard", axis=0, tiled=True),
        lax.all_gather(w_out_bf, "shard", axis=0, tiled=True),
    )
    norm_bf = (normed * gain_all.astype(jnp.float32)).astype(jnp.bfloat16)
    gain_cast = gain_all.astype(jnp.float32)
    columns = attn_bf
    grad_outproj_part = lax.psum_scatter(
        contract_rows(columns, seq_cotangent), "shard", scatter_dimension=0, tiled=True
    )
    attention_gradient = contract_cols(seq_cotangent, w_out_all).astype(jnp.bfloat16)
    head_gradients = attention_gradient.reshape(
        sequence_length, kv_heads, group_width, HEAD_SIZE
    ).transpose(1, 0, 2, 3)
    query_grad, key_grad, value_grad = lax.map(
        lambda blocks: head_backward(
            blocks[0], blocks[1], blocks[2], blocks[3], blocks[4], allowed, score_scale
        ),
        (query_head_rows, k_heads, v_heads, log_sum, head_gradients),
    )
    query_grad = unrotate(
        query_grad.transpose(1, 0, 2, 3).reshape(sequence_length, query_heads, HEAD_SIZE),
        cosine_table,
        sine_table,
    )
    key_grad = unrotate(key_grad.transpose(1, 0, 2), cosine_table, sine_table)
    grad_qkv = jnp.concatenate(
        [
            query_grad.reshape(sequence_length, query_width),
            key_grad.reshape(sequence_length, kv_width),
            value_grad.transpose(1, 0, 2).reshape(sequence_length, kv_width),
        ],
        1,
    ).astype(jnp.bfloat16)
    grad_in_local = contract_rows(norm_bf, grad_qkv)
    grad_normed = contract_cols(grad_qkv, w_in_all)
    grad_gain_local = jnp.sum(grad_normed * normed, 0)
    grad_hat = grad_normed * gain_cast
    grad_tokens = (
        seq_cotangent.astype(jnp.float32)
        + inv_rms * (grad_hat - normed * jnp.mean(grad_hat * normed, -1, keepdims=True))
    ).astype(jnp.bfloat16)
    grad_in_shard, grad_gain_shard = (
        lax.psum_scatter(grad_in_local, "shard", scatter_dimension=0, tiled=True),
        lax.psum_scatter(grad_gain_local, "shard", scatter_dimension=0, tiled=True),
    )
    grad_in_sum, grad_gain_sum, grad_outproj_sum = lax.psum(
        (grad_in_shard, grad_gain_shard, grad_outproj_part), "rep"
    )
    grad_query = grad_in_sum[:, :query_width]
    grad_key = grad_in_sum[:, query_width : query_width + kv_width]
    grad_value = grad_in_sum[:, query_width + kv_width :]
    moment_gain_next = decay * moment_gain + grad_gain_sum
    moment_query_next = decay * moment_query + grad_query
    moment_key_next = decay * moment_key + grad_key
    moment_value_next = decay * moment_value + grad_value
    moment_outproj_next = decay * moment_outproj + grad_outproj_sum
    gain_next = gain - gain_rate / math.sqrt(total_tokens) * moment_gain_next
    part_query = column_block(moment_query_next, rep_index, n_rep)
    part_key = column_block(moment_key_next, rep_index, n_rep)
    part_value = column_block(moment_value_next, rep_index, n_rep)
    part_outproj = column_block(moment_outproj_next, rep_index, n_rep)
    rows_query, rows_key, rows_value, rows_outproj = (
        lax.all_gather(part_query.astype(jnp.bfloat16), "shard", axis=0, tiled=True).astype(
            part_query.dtype
        ),
        lax.all_gather(part_key.astype(jnp.bfloat16), "shard", axis=0, tiled=True).astype(
            part_key.dtype
        ),
        lax.all_gather(part_value.astype(jnp.bfloat16), "shard", axis=0, tiled=True).astype(
            part_value.dtype
        ),
        lax.all_gather(part_outproj.astype(jnp.bfloat16), "shard", axis=0, tiled=True).astype(
            part_outproj.dtype
        ),
    )
    whole_query, whole_key, whole_value, whole_outproj = (
        lax.all_gather(rows_query.astype(jnp.bfloat16), "rep", axis=1, tiled=True).astype(
            rows_query.dtype
        ),
        lax.all_gather(rows_key.astype(jnp.bfloat16), "rep", axis=1, tiled=True).astype(
            rows_key.dtype
        ),
        lax.all_gather(rows_value.astype(jnp.bfloat16), "rep", axis=1, tiled=True).astype(
            rows_value.dtype
        ),
        lax.all_gather(rows_outproj.astype(jnp.bfloat16), "rep", axis=1, tiled=True).astype(
            rows_outproj.dtype
        ),
    )
    whole_mats = (whole_query, whole_key, whole_value, whole_outproj)
    moments_here = (moment_query_next, moment_key_next, moment_value_next, moment_outproj_next)
    weights_here = (w_query, w_key, w_value, w_outproj)
    my_linear = rep_index * n_shard + shard_index
    updated = []
    for matrix_slot in range(4):
        whole = whole_mats[matrix_slot]
        row_count = moments_here[matrix_slot].shape[0]
        owner_rep = matrix_slot % n_rep
        owner_shard = matrix_slot % n_shard
        owner_index = owner_rep * n_shard + owner_shard
        owned_result = lax.cond(my_linear == owner_index, orthogonalize, jnp.zeros_like, whole)
        ortho_whole = from_root(
            owned_result.astype(jnp.bfloat16), ("rep", "shard"), owner_index
        ).astype(owned_result.dtype)
        ortho_rows = lax.dynamic_slice_in_dim(ortho_whole, shard_index * row_count, row_count, 0)
        rate_factor = muon_rate * math.sqrt(max(whole.shape))
        weight_cols = column_block(weights_here[matrix_slot], rep_index, n_rep)
        ortho_cols = column_block(ortho_rows, rep_index, n_rep)
        updated.append(weight_cols - rate_factor * ortho_cols)
    return (
        result[None],
        grad_tokens[None],
        grad_gain_sum,
        grad_query,
        grad_key,
        grad_value,
        grad_outproj_sum,
        gain_next,
        updated[0],
        updated[1],
        updated[2],
        updated[3],
        moment_gain_next,
        moment_query_next,
        moment_key_next,
        moment_value_next,
        moment_outproj_next,
    )


def solution(mesh):
    in_specs = (
        P(("rep", "shard"), None, None),
        P(("rep", "shard"), None),
        P(("rep", "shard"), None, None),
        P("shard"),
        P("shard", None),
        P("shard", None),
        P("shard", None),
        P("shard", None),
        P("shard"),
        P("shard", None),
        P("shard", None),
        P("shard", None),
        P("shard", None),
    )
    out_specs = (
        P(("rep", "shard"), None, None),
        P(("rep", "shard"), None, None),
        P("shard"),
        P("shard", None),
        P("shard", None),
        P("shard", None),
        P("shard", None),
        P("shard"),
        P("shard", "rep"),
        P("shard", "rep"),
        P("shard", "rep"),
        P("shard", "rep"),
        P("shard"),
        P("shard", None),
        P("shard", None),
        P("shard", None),
        P("shard", None),
    )
    return jax.shard_map(
        on_device, mesh=mesh, in_specs=in_specs, out_specs=out_specs, check_vma=False
    )
```

profile of v0, /device:TPU:0, one launch (start us, length us, event | category | flops | bytes accessed | tf_op | source)
XLA Modules:
  0.0 1450.7 jit_solution(16184623670681157868)
XLA Ops:
  16.5 13.8 all-gather
  33.0 97.6 %all-gather.8.cloned.1.call-done = bf16[2048,1536]{1,0:T(8,128)(2,1)} async-done(((bf16[512,1536]{1,0:T(8,128)(2,1)}), bf16[2048,1536]{1,0:T(8,128)(2,1)}) %all-gather.8.cloned.1.call-update) | async-done | bytes 6291472 | tf_op jit(solution)/shard_map/all_gather | solution.py:160
  144.6 22.0 %while.30 = (s32[]{:T(128)}, bf16[4,512,4,64]{1,3,2,0:T(8,128)(2,1)}, f32[4,4,512,1]{2,1,3,0:T(4,128)}, bf16[4,512,64]{1,2,0:T(8,128)(2,1)}, bf16[4,512,64]{1,2,...) while((s32[]{:T(128)}, bf16[4,512,4,64]{1,3,2,0:T(8,128)(2,1)}, ...), condition=%wide.region_5.6_spmd.clone.clone, body=%wide.region_3.5_spmd.clone.sunk.clone | while | flops 276559872 | bytes 18518160 | solution.py:192
  166.6 7.5 fusion.249
  174.4 37.3 %all-gather.10.cloned.1.call-done = bf16[1024,2048]{1,0:T(8,128)(2,1)} async-done(((bf16[256,2048]{1,0:T(8,128)(2,1)}), bf16[1024,2048]{1,0:T(8,128)(2,1)}) %all-gather.10.cloned.1.call-update) | async-done | bytes 4194320 | tf_op jit(solution)/shard_map/all_gather | solution.py:202
  220.4 119.1 %while.31 = (s32[]{:T(128)}, f32[4,512,4,64]{1,3,2,0:T(8,128)}, f32[4,512,64]{1,2,0:T(8,128)}, bf16[4,512,64]{1,2,0:T(8,128)(2,1)}, bf16[4,512,64]{1,2,0:T(8,128...) while((s32[]{:T(128)}, f32[4,512,4,64]{1,3,2,0:T(8,128)}, ...), condition=%wide.region_8.9_spmd.clone.clone, body=%wide.region_6.8_spmd.clone.sunk.clone | while | flops 699143168 | bytes 49806448 | solution.py:221
  228.6 9.6 fusion.412
  238.2 8.1 fusion.413
  258.3 9.6 fusion.412
  267.9 8.2 fusion.413
  288.1 9.9 fusion.412
  297.9 8.1 fusion.413
  318.0 9.6 fusion.412
  327.6 8.0 fusion.413
  343.8 7.7 fusion.256
  357.2 214.7 %reduce-scatter.3.cloned.1.call-done = f32[512,1536]{1,0:T(8,128)} async-done(((f32[2048,1536]{1,0:T(8,128)}), f32[512,1536]{1,0:T(8,128)}) %reduce-scatter.3.cloned.1.call-update) | async-done | bytes 3145744 | tf_op jit(solution)/shard_map/reduce_scatter | solution.py:250
  572.0 96.6 %all-reduce.6.cloned.1.call-done = (f32[512,1536]{1,0:T(8,128)}, f32[256,2048]{1,0:T(8,128)}) async-done(((f32[512,1536]{1,0:T(8,128)}, f32[256,2048]{1,0:T(8,128)}), (f32[512,1536]{1,0:T(8,128)}, f32[256,2048]{1,0:T(8,128)})) %all-reduce.6.cloned.1.call-update) | async-done | bytes 5242896 | tf_op jit(solution)/shard_map/psum | solution.py:253
  671.9 15.5 %all_gather.43 = bf16[2048,32]{1,0:T(8,128)(2,1)S(1)} all-gather(bf16[512,32]{1,0:T(8,128)(2,1)S(1)} %dynamic-slice_convert_fusion.1), channel_id=1, replica_groups=mesh['rep'=8,'shard'=4] {'shard'}, dimensions={0}, use_global_device_ids=true | all-gather | bytes 163840 | tf_op jit(solution)/shard_map/all_gather | solution.py:276
  688.4 16.3 %all_gather.41 = bf16[2048,32]{1,0:T(8,128)(2,1)S(1)} all-gather(bf16[512,32]{1,0:T(8,128)(2,1)S(1)} %dynamic-slice_convert_fusion.2), channel_id=1, replica_groups=mesh['rep'=8,'shard'=4] {'shard'}, dimensions={0}, use_global_device_ids=true | all-gather | bytes 163840 | tf_op jit(solution)/shard_map/all_gather | solution.py:273
  711.4 16.7 %all_gather.39 = bf16[2048,128]{1,0:T(8,128)(2,1)} all-gather(bf16[512,128]{1,0:T(8,128)(2,1)S(1)} %dynamic-slice_convert_fusion.3), channel_id=1, replica_groups=mesh['rep'=8,'shard'=4] {'shard'}, dimensions={0}, use_global_device_ids=true | all-gather | bytes 655360 | tf_op jit(solution)/shard_map/all_gather | solution.py:270
  731.4 16.0 %all_gather.45 = bf16[1024,256]{1,0:T(8,128)(2,1)} all-gather(bf16[256,256]{1,0:T(8,128)(2,1)S(1)} %dynamic-slice_convert_fusion), channel_id=1, replica_groups=mesh['rep'=8,'shard'=4] {'shard'}, dimensions={0}, use_global_device_ids=true | all-gather | bytes 655360 | tf_op jit(solution)/shard_map/all_gather | solution.py:279
  749.0 9.1 conditional.6
  759.7 13.9 conditional.5
  777.9 6.5 convert_element_type.178
  784.4 427.3 %conditional.4 = (bf16[2048,1024]{1,0:T(8,128)(2,1)}) conditional(s32[]{:T(128)} %convert_element_type.176, () %tuple.50, f32[2048,1024]{1,0:T(8,128)} %convert_element_type.178), branch_computations={%region_17.18_spmd, %region_18.20_spmd} | conditional | flops 322220064768 | bytes 478150816 | solution.py:308
  784.4 9.2 copy.83
  800.4 32.3 %fusion.57 = f32[1024,1024]{1,0:T(8,128)S(1)} fusion(f32[2048,1024]{0,1:T(8,128)} %copy.83, f32[]{:T(128)S(6)} %add.210), kind=kOutput, calls=%fused_computation.63 | convolution fusion | flops 25771900928 | bytes 12582916 | tf_op jit(solution)/shard_map/cond/branch_1_fun/dot_general | solution.py:111
  832.7 13.9 fusion.274
  846.6 30.0 %fusion.26 = f32[1024,2048]{1,0:T(8,128)} fusion(f32[1024,1024]{1,0:T(8,128)S(1)} %fusion.274, f32[1024,1024]{1,0:T(8,128)S(1)} %fusion.57, f32[2048,1024]{0,1:T(8,128)S(1)} %copy-done.1, f32[]{:T(128)S(6)} %add.210), kind=kOutput, calls=%fused_computation.33 | convolution fusion | flops 25775046656 | bytes 25165828 | tf_op jit(solution)/shard_map/cond/branch_1_fun/dot_general | solution.py:115
  876.5 33.3 %fusion.56 = f32[1024,1024]{1,0:T(8,128)S(1)} fusion(f32[1024,2048]{1,0:T(8,128)} %fusion.26, f32[2048,1024]{0,1:T(8,128)S(1)} %copy-done.1, f32[]{:T(128)S(6)} %add.210), kind=kOutput, calls=%fused_computation.62 | convolution fusion | flops 25776095232 | bytes 20971524 | tf_op jit(solution)/shard_map/cond/branch_1_fun/dot_general | solution.py:111
  909.9 14.9 %fusion.275 = f32[1024,1024]{1,0:T(8,128)} fusion(f32[1024,1024]{1,0:T(8,128)S(1)} %fusion.56), kind=kOutput, calls=%fused_computation.348 | convolution fusion | flops 12884901888 | bytes 8388608 | tf_op jit(solution)/shard_map/cond/branch_1_fun/dot_general | solution.py:112
  924.8 37.9 %multiply_add_fusion.2 = (f32[1024,2048]{1,0:T(8,128)}, f32[1024,2048]{1,0:T(8,128)}) fusion(f32[1024,2048]{1,0:T(8,128)} %fusion.26, f32[2048,1024]{0,1:T(8,128)S(1)} %copy-done.1, f32[]{:T(128)S(6)} %add.210, f32[1024,1024]{1,0:T(8,128)} %fusion.275, f32[1024,1024]{1,0:T(8,128)S(1)} %fusion.56), kind=kOutput, calls=%fused_computation.15 | convolution fusion | flops 25789726720 | bytes 41943044 | tf_op jit(solution)/shard_map/cond/branch_1_fun/dot_general | solution.py:115
  962.7 32.3 %fusion.276 = f32[1024,1024]{1,0:T(8,128)S(1)} fusion(f32[1024,2048]{1,0:T(8,128)} %get-tuple-element.225), kind=kOutput, calls=%fused_computation.349 | convolution fusion | flops 25769803776 | bytes 12582912 | tf_op jit(solution)/shard_map/cond/branch_1_fun/dot_general | solution.py:111
  995.1 13.9 fusion.277
  1009.0 29.0 %fusion.18 = f32[1024,2048]{1,0:T(8,128)S(1)} fusion(f32[1024,2048]{1,0:T(8,128)S(1)} %copy-done.32, f32[1024,1024]{1,0:T(8,128)S(1)} %fusion.277, f32[1024,1024]{1,0:T(8,128)S(1)} %fusion.276), kind=kOutput, calls=%fused_computation.25 | convolution fusion | flops 25772949504 | bytes 25165824 | tf_op jit(solution)/shard_map/cond/branch_1_fun/dot_general | solution.py:115
  1038.0 30.3 %fusion.55 = f32[1024,1024]{1,0:T(8,128)S(1)} fusion(f32[1024,2048]{1,0:T(8,128)S(1)} %fusion.18, f32[1024,2048]{1,0:T(8,128)S(1)} %copy-done.32), kind=kOutput, calls=%fused_computation.61 | convolution fusion | flops 25773998080 | bytes 20971520 | tf_op jit(solution)/shard_map/cond/branch_1_fun/dot_general | solution.py:111
  1068.3 13.9 fusion.278
  1082.2 29.7 %fusion.14 = f32[1024,2048]{1,0:T(8,128)} fusion(f32[1024,1024]{1,0:T(8,128)S(1)} %fusion.278, f32[1024,1024]{1,0:T(8,128)S(1)} %fusion.55, f32[1024,2048]{1,0:T(8,128)S(1)} %fusion.18, f32[1024,2048]{1,0:T(8,128)S(1)} %copy-done.32), kind=kOutput, calls=%fused_computation.21 | convolution fusion | flops 25777143808 | bytes 33554432 | tf_op jit(solution)/shard_map/cond/branch_1_fun/dot_general | solution.py:115
  1111.9 33.9 %fusion.30 = f32[1024,1024]{1,0:T(8,128)S(1)} fusion(f32[1024,2048]{1,0:T(8,128)} %fusion.14, f32[1024,2048]{1,0:T(8,128)S(1)} %fusion.18, f32[1024,2048]{1,0:T(8,128)S(1)} %copy-done.32), kind=kOutput, calls=%fused_computation.38 | convolution fusion | flops 25778192384 | bytes 29360128 | tf_op jit(solution)/shard_map/cond/branch_1_fun/dot_general | solution.py:111
  1147.8 15.1 %fusion.279 = f32[1024,1024]{1,0:T(8,128)} fusion(f32[1024,1024]{1,0:T(8,128)S(1)} %fusion.30), kind=kOutput, calls=%fused_computation.352 | convolution fusion | flops 12884901888 | bytes 8388608 | tf_op jit(solution)/shard_map/cond/branch_1_fun/dot_general | solution.py:112
  1162.9 42.2 %fusion.6 = bf16[2048,1024]{0,1:T(8,128)(2,1)} fusion(f32[1024,2048]{1,0:T(8,128)} %fusion.14, f32[1024,2048]{1,0:T(8,128)} %copy-done.33, f32[1024,2048]{1,0:T(8,128)} %get-tuple-element.226, f32[1024,2048]{1,0:T(8,128)} %fusion.26, f32[1024,1024]{1,0:T(8,128)} %fusion.279, f32[1024,1024]{1,0:T(8,128)} %copy-done.34, f32[1024,2048]{1,0:T(8,128)} %get-tuple-element.225, ...), kind=kOutput, calls=%fused_computation.5 | convolution fusion | flops 25806503936 | bytes 62914564 | tf_op jit(solution)/shard_map/cond/branch_1_fun/dot_general | solution.py:115
  1205.1 6.4 copy.97
  1216.1 6.5 convert_element_type.190
  1222.7 9.5 conditional.7
  1239.1 9.7 fusion.244
  1248.7 9.3 all-reduce
  1258.1 12.0 psum.49
  1279.6 154.0 %all-reduce.8.cloned.1.call-done = (bf16[2048,1024]{1,0:T(8,128)(2,1)}, bf16[2048,256]{0,1:T(8,128)(2,1)}, bf16[2048,256]{0,1:T(8,128)(2,1)}, bf16[1024,2048]{1,0:T(8,128)(2,1)}) async-done(((bf16[2048,1024]{1,0:T(8,128)(2,1)}, bf16[2048,256]{0,1:T(8,128)(2,1)}, bf16[2048,256]{0,1:T(8,128)(2,1)}, bf16[1024,2048]{1,0:T(8,128)(2,1)}), (bf16[2048,1024]{1,0:T(8,128)(2,1)}, bf16[2048,256]{0,1:T(8,128)(2,1)}, ...) | async-done | bytes 10485776 | tf_op jit(solution)/shard_map/psum | solution.py:23
  (214 shorter events, 177.5 us)
Async XLA Ops:
  7.2 123.5 %all-gather.8.cloned.1.call-start = ((), (), s32[]{:S(2)}) async-start(), calls=%async_computation.2 | async-start | bytes 7864320 | tf_op jit(solution)/shard_map/all_gather | solution.py:160
  12.4 4.1 copy-start.24
  12.4 17.9 %copy-start.2 = (bf16[1,512,2048]{2,1,0:T(8,128)(2,1)S(1)}, bf16[1,512,2048]{2,1,0:T(8,128)(2,1)}, u32[]{:S(2)}) copy-start(bf16[1,512,2048]{2,1,0:T(8,128)(2,1)} %param.25) | copy-start | bytes 6291460
  12.4 18.4 %copy-start.15 = (s32[1,512]{1,0:T(1,128)S(1)}, s32[1,512]{1,0:T(1,128)}, u32[]{:S(2)}) copy-start(s32[1,512]{1,0:T(1,128)} %param.26) | copy-start | bytes 6148
  12.4 199.3 %all-gather.10.cloned.1.call-start = ((), (), s32[]{:S(2)}) async-start(), calls=%async_computation.3 | async-start | bytes 5242880 | tf_op jit(solution)/shard_map/all_gather | solution.py:202
  15.3 341.9 %reduce-scatter.5.cloned.1.call-start = ((), (), s32[]{:S(2)}) async-start(), calls=%async_computation.5 | async-start | bytes 10485760 | tf_op jit(solution)/shard_map/reduce_scatter | solution.py:214
  30.3 105.9 %copy-start.21 = (f32[4,1,512]{2,1,0:T(1,128)}, f32[4,1,512]{2,1,0:T(1,128)S(1)}, u32[]{:S(2)}) copy-start(f32[4,1,512]{2,1,0:T(1,128)S(1)} %convert_element_type.193) | copy-start | bytes 24580
  30.8 312.0 %copy-start.27 = (f32[512]{0:T(512)}, f32[512]{0:T(512)S(1)}, u32[]{:S(2)}) copy-start(f32[512]{0:T(512)S(1)} %add_rsqrt_fusion) | copy-start | bytes 6148
  144.6 2.4 copy-start.5
  149.1 1.0 copy-start.6
  150.1 2.4 copy-start.5
  154.6 1.0 copy-start.6
  155.6 2.4 copy-start.5
  160.1 1.0 copy-start.6
  161.1 2.4 copy-start.5
  165.6 1.0 copy-start.6
  174.1 397.9 %reduce-scatter.3.cloned.1.call-start = ((), (), s32[]{:S(2)}) async-start(), calls=%async_computation.4 | async-start | bytes 15728640 | tf_op jit(solution)/shard_map/reduce_scatter | solution.py:250
  339.5 4.2 copy-start.22
  339.5 4.2 copy-start.30
  340.7 10.7 copy-start.20
  351.4 317.2 %copy-start.18 = (f32[512,256]{1,0:T(8,128)S(1)}, f32[512,256]{1,0:T(8,128)}, u32[]{:S(2)}) copy-start(f32[512,256]{1,0:T(8,128)} %param.36) | copy-start | bytes 1572868
  351.5 317.2 %copy-start.19 = (f32[512,256]{1,0:T(8,128)S(1)}, f32[512,256]{1,0:T(8,128)}, u32[]{:S(2)}) copy-start(f32[512,256]{1,0:T(8,128)} %param.35) | copy-start | bytes 1572868
  351.5 317.2 %all-reduce.6.cloned.1.call-start = ((), (), s32[]{:S(2)}) async-start(), calls=%async_computation.10 | async-start | bytes 10485760 | tf_op jit(solution)/shard_map/psum | solution.py:253
  572.0 175.5 %all-gather.16.cloned.1.call-start = ((), (), s32[]{:S(2)}) async-start(), calls=%async_computation.8 | async-start | bytes 1179648 | tf_op jit(solution)/shard_map/all_gather | solution.py:290
  671.0 34.6 %copy-start.17 = (f32[512,256]{1,0:T(8,128)}, f32[512,256]{1,0:T(8,128)S(1)}, u32[]{:S(2)}) copy-start(f32[512,256]{1,0:T(8,128)S(1)} %get-tuple-element.465) | copy-start | bytes 1572868
  688.2 70.0 %all-gather.14.cloned.1.call-start = ((), (), s32[]{:S(2)}) async-start(), calls=%async_computation.7 | async-start | bytes 1179648 | tf_op jit(solution)/shard_map/all_gather | solution.py:287
  705.5 72.3 %all-gather.12.cloned.1.call-start = ((), (), s32[]{:S(2)}) async-start(), calls=%async_computation.6 | async-start | bytes 4718592 | tf_op jit(solution)/shard_map/all_gather | solution.py:284
  705.6 22.5 %copy-start.4 = (f32[256,2048]{1,0:T(8,128)S(1)}, f32[256,2048]{1,0:T(8,128)}, u32[]{:S(2)}) copy-start(f32[256,2048]{1,0:T(8,128)} %get-tuple-element.457) | copy-start | bytes 6291460
  710.0 1.3 copy-start.10
  728.0 488.1 %all-gather.18.cloned.1.call-start = ((), (), s32[]{:S(2)}) async-start(), calls=%async_computation.9 | async-start | bytes 4718592 | tf_op jit(solution)/shard_map/all_gather | solution.py:293
  730.0 1.3 copy-start.9
  747.4 686.2 %all-reduce.8.cloned.1.call-start = ((), (), s32[]{:S(2)}) async-start(), calls=%async_computation.11 | async-start | bytes 20971520 | tf_op jit(solution)/shard_map/psum | solution.py:23
  832.7 13.9 copy-start.1
  995.1 13.9 copy-start.32
  1038.0 73.9 %copy-start.33 = (f32[1024,2048]{1,0:T(8,128)}, f32[1024,2048]{1,0:T(8,128)S(1)}, u32[]{:S(2)}) copy-start(f32[1024,2048]{1,0:T(8,128)S(1)} %fusion.18) | copy-start | bytes 25165828 | tf_op jit(solution)/shard_map/cond
  1145.8 2.0 copy-start.34
  1234.4 1.0 copy-start.12
  1234.4 1.2 copy-start.13
  1234.4 3.3 copy-start.31
  1234.4 4.6 copy-start.3
  1234.4 4.6 copy-start.23
  1234.4 4.6 copy-start.28
  1239.0 31.1 %copy-start.25 = (f32[512]{0:T(512)S(1)}, f32[512]{0:T(512)}, u32[]{:S(2)}) copy-start(f32[512]{0:T(512)} %param.28) | copy-start | bytes 6148
  1239.0 31.1 %copy-start.29 = (f32[512]{0:T(512)S(1)}, f32[512]{0:T(512)}, u32[]{:S(2)}) copy-start(f32[512]{0:T(512)} %param.33) | copy-start | bytes 6148
  1239.0 31.7 %copy-start.7 = (bf16[4,512,4,64]{1,3,2,0:T(8,128)(2,1)S(1)}, bf16[4,512,4,64]{1,3,2,0:T(8,128)(2,1)}, u32[]{:S(2)}) copy-start(bf16[4,512,4,64]{1,3,2,0:T(8,128)(2,1)} %get-tuple-element.129) | copy-start | bytes 3145732
  1270.1 6.7 copy-start.26
  1270.7 6.1 copy-start.8
  1270.7 6.1 copy-start.11
  (2 other events, 1.8 us)
Sparse Core Ops, SparseCore 0:
  12.5 118.0 all-gather.7
  132.8 78.9 all-gather.9
  214.1 143.0 reduce-scatter.4
  359.4 212.4 reduce-scatter.2
  575.2 93.4 all-reduce.5
  688.3 24.3 all-gather.15
  715.2 23.3 all-gather.13
  740.5 37.3 all-gather.11
  779.7 37.3 all-gather.17
  1234.6 198.9 all-reduce.7
where the time goes:
time: 1460 us; the launch traced here: 1450 us
  waiting for transfers between devices  609 us (42%)
  matrix products  578 us (40%)
  blocking collectives  99.4 us (7%)
  other arithmetic  67.1 us (5%)
  local copies, waits for them, and re-layouts  50.2 us (3%)
  loops' own time  30 us (2%)
  between operations  16.5 us (1%)
    reduce_scatter x1, waiting for transfers between devices, on_device(): lax.psum_scatter(grad_in_local, 'shard', scatter_dimension=0, tiled=True)  215 us
    dot_general x5, matrix products, orthogonalize(): jnp.dot(polynomial, iterate, precision=lax.Precision.HIGHEST)  169 us
    dot_general x5, matrix products, orthogonalize(): square = jnp.dot(iterate, iterate.T, precision=lax.Precision.HIGHEST)  162 us
    psum x1, waiting for transfers between devices, from_root(): return lax.psum(block, axis)  154 us
    all_gather x1, waiting for transfers between devices, on_device(): w_piece = lax.all_gather(w_in_bf, 'shard', axis=0, tiled=True)  97.6 us
    psum x1, waiting for transfers between devices, on_device(): lax.psum((grad_in_shard, grad_gain_shard, grad_outproj_part), 'rep')  96.6 us
    dot_general x5, matrix products, orthogonalize(): jnp.dot(square, square, precision=lax.Precision.HIGHEST)  71.7 us
    dot_general x4, matrix products, head_backward(): jnp.einsum('gqk,kd->qgd', score_grad, k_head, preferred_element_type=jnp....  38.6 us
  transfers between devices with their start and end apart: 10, of which 7 were waited for; matrix products, arithmetic and copies ran while one was open for 45% of the time, Pallas kernels for 0%

commit v1 on v0

v1 whole, which is shorter than its diff:
```python
import functools
import math

import jax
import jax.numpy as jnp
from jax import lax
from jax.experimental import pallas as pl
from jax.experimental.pallas import tpu as pltpu
from jax.sharding import PartitionSpec as P

MESH = pl.DeviceIdType.MESH


class Links:
    def __init__(self, n_rep, n_shard):
        self.n_bits = n_rep.bit_length() - 1
        self.n_shard = n_shard
        self.rep = lax.axis_index("rep")
        self.shard = lax.axis_index("shard")
        self.bits = [lax.rem(lax.div(self.rep, 1 << b), 2) for b in range(self.n_bits)]
        far = list(range(1, self.n_bits))
        self.orders = (far, far[::-1])

    def flip(self, bit):
        return self.rep + (1 << bit) * (1 - 2 * self.bits[bit])

    def barrier(self, line):
        sem = pltpu.get_barrier_semaphore()
        count = self.n_bits
        for b in range(self.n_bits):
            pl.semaphore_signal(sem, 1, device_id=(self.flip(b), self.shard), device_id_type=MESH)
        if line:
            for step in (-1, 1):
                there = self.shard + step
                inside = jnp.logical_and(there >= 0, there < self.n_shard)

                @pl.when(inside)
                def _():
                    pl.semaphore_signal(sem, 1, device_id=(self.rep, there), device_id_type=MESH)

                count = count + inside.astype(jnp.int32)
        else:
            for k in range(1, self.n_shard):
                there = lax.rem(self.shard + k, self.n_shard)
                pl.semaphore_signal(sem, 1, device_id=(self.rep, there), device_id_type=MESH)
            count = count + self.n_shard - 1
        pl.semaphore_wait(sem, count)

    def where(self, fixed, free=()):
        return tuple(
            slice(None) if b in free else fixed.get(b, self.bits[b])
            for b in reversed(range(self.n_bits))
        )


def halves(ref):
    cols = ref.shape[-1]
    return (pl.ds(0, cols // 2), pl.ds(cols // 2, cols // 2))


def spread(links, full, q, half, step, send, recv):
    order = links.orders[half] + [0]
    bit, done = order[step], order[:step]
    view = full.at[(q, *links.where({}, done), slice(None), halves(full)[half])]
    return pltpu.make_async_remote_copy(
        view, view, send, recv, device_id=(links.flip(bit), links.shard), device_id_type=MESH
    )


def gather_kernel(n_rep, n_shard, n_arrays, *refs):
    local, row = refs[:n_arrays], refs[n_arrays]
    full, row_full = refs[n_arrays + 1 : 2 * n_arrays + 1], refs[2 * n_arrays + 1]
    keep_sem, line_send, line_recv, plane_send, plane_recv, row_send, row_recv = refs[2 * n_arrays + 2 :]
    links = Links(n_rep, n_shard)
    me = links.shard
    links.barrier(True)
    row_full[me] = row[...]

    def row_line(way, k):
        q, side = me - way * k, (way + 1) // 2
        return pltpu.make_async_remote_copy(
            row if k == 0 else row_full.at[q], row_full.at[q], row_send.at[side, k], row_recv.at[side, k],
            device_id=(links.rep, me + way), device_id_type=MESH,
        )

    def row_came(way, k):
        here, side = row_full.at[me - way * (k + 1)], (way + 1) // 2
        return pltpu.make_async_remote_copy(
            here, here, row_send.at[side, k], row_recv.at[side, k], device_id=(links.rep, me), device_id_type=MESH
        )
    keeps = [pltpu.make_async_copy(local[a], full[a].at[me], keep_sem.at[a]) for a in range(n_arrays)]

    def line(a, way, k):
        q = me - way * k
        here = links.where({})
        src = local[a].at[here] if k == 0 else full[a].at[(q, *here)]
        side = (way + 1) // 2
        return pltpu.make_async_remote_copy(
            src, full[a].at[(q, *here)], line_send.at[a, side, k], line_recv.at[a, side, k],
            device_id=(links.rep, me + way), device_id_type=MESH,
        )

    def came(a, way, k):
        q = me - way * (k + 1)
        here = full[a].at[(q, *links.where({}))]
        side = (way + 1) // 2
        return pltpu.make_async_remote_copy(
            here, here, line_send.at[a, side, k], line_recv.at[a, side, k],
            device_id=(links.rep, me), device_id_type=MESH,
        )

    def goes(way, k):
        q, there = me - way * k, me + way
        return (q >= 0) & (q < n_shard) & (there >= 0) & (there < n_shard)

    def comes(way, k):
        q = me - way * (k + 1)
        return (q >= 0) & (q < n_shard)

    ways = (1, -1)
    n_steps = links.n_bits
    for way in ways:
        @pl.when(goes(way, 0))
        def _():
            row_line(way, 0).start()
    for a in range(n_arrays):
        for way in ways:
            @pl.when(goes(way, 0))
            def _():
                line(a, way, 0).start()
    for keep in keeps:
        keep.start()

    def plane(a, way, k, half, step):
        q = me - way * (k + 1)
        side = (way + 1) // 2
        return spread(links, full[a], q, half, step,
                      plane_send.at[a, side, k, half, step], plane_recv.at[a, side, k, half, step])

    items = [(a, k) for a in range(n_arrays) for k in range(n_shard - 1)]
    for t in range(len(items) + n_steps):
        for i, (a, k) in enumerate(items):
            step = t - i
            if step < 0 or step > n_steps:
                continue
            for way in ways:
                @pl.when(comes(way, k))
                def _():
                    if step == 0 and a == 0:
                        row_came(way, k).wait_recv()
                        if k + 1 < n_shard - 1:
                            @pl.when(goes(way, k + 1))
                            def _():
                                row_line(way, k + 1).start()
                    if step == 0:
                        came(a, way, k).wait_recv()
                        if k + 1 < n_shard - 1:
                            @pl.when(goes(way, k + 1))
                            def _():
                                line(a, way, k + 1).start()
                    else:
                        for half in range(2):
                            plane(a, way, k, half, step - 1).wait_recv()
                    if step < n_steps:
                        for half in range(2):
                            plane(a, way, k, half, step).start()
    for keep in keeps:
        keep.wait()
    for way in ways:
        for k in range(n_shard - 1):
            @pl.when(goes(way, k))
            def _():
                row_line(way, k).wait_send()
    for a in range(n_arrays):
        for way in ways:
            for k in range(n_shard - 1):
                @pl.when(goes(way, k))
                def _():
                    line(a, way, k).wait_send()

                @pl.when(comes(way, k))
                def _():
                    for half in range(2):
                        for step in range(n_steps):
                            plane(a, way, k, half, step).wait_send()


def gather_all(blocks, row, n_rep, n_shard, collective_id):
    n_bits = n_rep.bit_length() - 1
    n = len(blocks)
    shaped = [b.reshape((2,) * n_bits + (b.shape[0] // n_rep, b.shape[1])) for b in blocks]
    steps = max(n_shard - 1, 1)
    out = pl.pallas_call(
        functools.partial(gather_kernel, n_rep, n_shard, n),
        out_shape=[jax.ShapeDtypeStruct((n_shard,) + s.shape, s.dtype) for s in shaped]
        + [jax.ShapeDtypeStruct((n_shard, 1) + row.shape, row.dtype)],
        in_specs=[pl.BlockSpec(memory_space=pltpu.VMEM)] * (n + 1),
        out_specs=[pl.BlockSpec(memory_space=pl.ANY)] * n + [pl.BlockSpec(memory_space=pltpu.VMEM)],
        scratch_shapes=[
            pltpu.SemaphoreType.DMA((n,)),
            pltpu.SemaphoreType.DMA((n, 2, steps)),
            pltpu.SemaphoreType.DMA((n, 2, steps)),
            pltpu.SemaphoreType.DMA((n, 2, steps, 2, n_bits)),
            pltpu.SemaphoreType.DMA((n, 2, steps, 2, n_bits)),
            pltpu.SemaphoreType.DMA((2, steps)),
            pltpu.SemaphoreType.DMA((2, steps)),
        ],
        compiler_params=pltpu.CompilerParams(collective_id=collective_id, has_side_effects=True),
        name="gather_all",
    )(*shaped, row[None])
    return [o.reshape(n_shard * b.shape[0], b.shape[1]) for o, b in zip(out, blocks)] + [out[n].reshape(-1)]


F32 = jnp.float32


class Sems:
    def __init__(self, send, recv):
        self.send, self.recv, self.names = send, recv, {}

    def pair(self, *name):
        i = self.names.setdefault(name, len(self.names))
        return self.send.at[i], self.recv.at[i]


def reduce_kernel(n_rep, n_shard, decay, n_sems, *refs):
    parts, gain, moments = refs[0:2], refs[2], refs[3:5]
    sums, wholes, gain_out = refs[5:7], refs[7:9], refs[9]
    rest = list(refs[10:])
    nb = n_rep.bit_length() - 1
    bufs = [[rest.pop(0) for _ in range(nb)] for _ in range(2)]
    zbuf = [rest.pop(0) for _ in range(2)]
    gpiece = [rest.pop(0) for _ in range(2)]
    mpiece = [rest.pop(0) for _ in range(2)]
    gacc, gcome, gz = rest.pop(0), rest.pop(0), rest.pop(0)
    keep_sem = rest.pop(0)
    sems = Sems(rest.pop(0), rest.pop(0))
    links = Links(n_rep, n_shard)
    me = links.shard
    links.barrier(False)

    def remote(src, dst, name, rep, shard):
        send, recv = sems.pair(*name)
        return pltpu.make_async_remote_copy(src, dst, send, recv, device_id=(rep, shard), device_id_type=MESH)

    def dest(k):
        return lax.rem(me + 1 + k, n_shard)

    def order(half):
        return [0] + links.orders[half]

    def pick(half, step, bit_value, fixed_lead):
        o = order(half)
        remaining = sorted(o[step:], reverse=True)
        return fixed_lead + tuple(bit_value if b == o[step] else slice(None) for b in remaining)

    def send_reduce(a, k, half, step):
        d, o = dest(k), order(half)
        bit = o[step]
        src = parts[a] if step == 0 else bufs[a][step - 1]
        cols = slice(None) if step == 0 else halves(parts[a])[half]
        view = src.at[pick(half, step, 1 - links.bits[bit], (d,)) + (slice(None), cols)]
        into = bufs[a][step].at[(d,) + (slice(None),) * (nb - step) + (cols,)]
        return remote(view, into, ("r", a, k, half, step), links.flip(bit), me)

    def add_reduce(a, k, half, step):
        d, o = dest(k), order(half)
        src = parts[a] if step == 0 else bufs[a][step - 1]
        n_left = nb - 1 - step
        cols = slice(None) if step == 0 else halves(parts[a])[half]
        mine = links.bits[o[step]]
        remaining = sorted(o[step:], reverse=True)

        def one(i, c):
            left = {}
            rest_bits = [b for b in remaining if b != o[step]]
            for pos, b in enumerate(rest_bits):
                left[b] = lax.rem(lax.div(i, 1 << (len(rest_bits) - 1 - pos)), 2)
            here = tuple(left[b] for b in rest_bits)
            there = tuple(mine if b == o[step] else left[b] for b in remaining)
            x = src[(d,) + there + (slice(None), cols)].astype(F32)
            y = bufs[a][step][(d,) + here + (slice(None), cols)].astype(F32)
            bufs[a][step][(d,) + here + (slice(None), cols)] = (x + y).astype(jnp.bfloat16)
            return c

        if n_left == 0:
            one(0, 0)
        else:
            lax.fori_loop(0, 1 << n_left, one, 0)

    def send_line(a, k):
        d = dest(k)
        return remote(bufs[a][nb - 1].at[d], zbuf[a].at[me], ("z", a, k), links.rep, d)

    def wait_line(a, k):
        q = lax.rem(me + n_shard - 1 - k, n_shard)
        return remote(zbuf[a].at[q], zbuf[a].at[q], ("z", a, k), links.rep, me)

    for a in (1, 0):
        for k in range(n_shard):
            send_reduce(a, k, 0, 0).start()

    def gain_send(b):
        return remote(gacc, gcome.at[b], ("gain", b), links.flip(b), me)

    def gain_line(k):
        d = dest(k)
        return remote(gacc.at[d], gz.at[me], ("gainz", k), links.rep, d)

    gacc[...] = gain[...]
    gain_send(0).start()

    def gain_step(b):
        gain_send(b).wait()
        gacc[...] = gacc[...] + gcome[b]
        if b + 1 < nb:
            gain_send(b + 1).start()
        else:
            for k in range(n_shard - 1):
                gain_line(k).start()

    def gain_end():
        acc = gacc[me]
        for k in range(n_shard - 1):
            gain_line(k).wait_send()
            q = lax.rem(me + n_shard - 1 - k, n_shard)
            remote(gz.at[q], gz.at[q], ("gainz", k), links.rep, me).wait_recv()
        for q in range(n_shard):
            acc = jnp.where(me == q, acc, acc + gz[q])
        gain_out[...] = acc

    here = links.where({})

    def g_step(a, half, step):
        o = links.orders[half] + [0]
        bit, done = o[step], o[:step]
        cols = halves(parts[a])[half]
        into = sums[a].at[links.where({}, done) + (slice(None), cols)]
        src = gpiece[a].at[:, cols] if step == 0 else into
        return remote(src, into, ("g", a, half, step), links.flip(bit), me)

    def keep(a, i):
        return pltpu.make_async_copy(gpiece[a], sums[a].at[here], keep_sem.at[a])

    def line(a, way, k):
        q = me - way * k
        at = wholes[a].at[(q,) + here]
        src = mpiece[a] if k == 0 else at
        return remote(src, at, ("l", a, way, k), links.rep, me + way)

    def came(a, way, k):
        at = wholes[a].at[(me - way * (k + 1),) + here]
        return remote(at, at, ("l", a, way, k), links.rep, me)

    def goes(way, k):
        q, there = me - way * k, me + way
        return (q >= 0) & (q < n_shard) & (there >= 0) & (there < n_shard)

    def comes(way, k):
        q = me - way * (k + 1)
        return (q >= 0) & (q < n_shard)

    def plane(a, way, k, half, step):
        o = links.orders[half] + [0]
        bit, done = o[step], o[:step]
        view = wholes[a].at[(me - way * (k + 1),) + links.where({}, done) + (slice(None), halves(parts[a])[half])]
        return remote(view, view, ("p", a, way, k, half, step), links.flip(bit), me)

    ways = (1, -1)

    def finish(a):
        for k in range(n_shard - 1):
            wait_line(a, k).wait_recv()
        acc = bufs[a][nb - 1][me].astype(F32)
        for k in range(n_shard - 1):
            acc = acc + zbuf[a][lax.rem(me + n_shard - 1 - k, n_shard)].astype(F32)
        g = acc.astype(jnp.bfloat16)
        gpiece[a][...] = g
        mpiece[a][...] = (decay * moments[a][...] + g.astype(F32)).astype(jnp.bfloat16)
        for way in ways:
            @pl.when(goes(way, 0))
            def _():
                line(a, way, 0).start()
        for half in range(2):
            g_step(a, half, 0).start()
        keep(a, 0).start()

    def gather_event(a, i, step):
        if i == 0:
            if step == 0:
                keep(a, 0).wait()
            if step < nb:
                for half in range(2):
                    g_step(a, half, step).wait_recv()
                    if step + 1 < nb:
                        g_step(a, half, step + 1).start()
            return
        k = i - 1
        for way in ways:
            @pl.when(comes(way, k))
            def _():
                if step == 0:
                    came(a, way, k).wait_recv()
                    if k + 1 < n_shard - 1:
                        @pl.when(goes(way, k + 1))
                        def _():
                            line(a, way, k + 1).start()
                else:
                    for half in range(2):
                        plane(a, way, k, half, step - 1).wait_recv()
                if step < nb:
                    for half in range(2):
                        plane(a, way, k, half, step).start()

    def reduce_event(a, k, step):
        for half in range(1 if step == 0 else 2):
            send_reduce(a, k, half, step).wait_recv()
            add_reduce(a, k, half, step)
            if step == 0 and nb > 1:
                send_reduce(a, k, 0, 1).start()
                send_reduce(a, k, 1, 1).start()
            elif step + 1 < nb:
                send_reduce(a, k, half, step + 1).start()
        if step == nb - 1 and k < n_shard - 1:
            send_line(a, k).start()

    events = []
    chunks = [(a, k) for a in (1, 0) for k in range(n_shard)]
    for t in range(len(chunks) + nb):
        if t < nb:
            events.append(functools.partial(gain_step, t))
        for step in reversed(range(nb)):
            i = t - step
            if 0 <= i < len(chunks):
                events.append(functools.partial(reduce_event, *chunks[i], step))
        if t == n_shard + nb:
            events.append(functools.partial(finish, 1))
            events.append(gain_end)
        i = t - n_shard - nb - 1
        if i >= 0:
            for j in range(n_shard):
                step = i - j
                if 0 <= step <= nb:
                    events.append(functools.partial(gather_event, 1, j, step))
    done_t = len(chunks) + nb - n_shard - nb - 1
    events.append(functools.partial(finish, 0))
    for t in range(n_shard + nb + 1):
        for a in (1, 0):
            i = t + (done_t if a == 1 else 0)
            for j in range(n_shard):
                step = i - j
                if 0 <= step <= nb:
                    events.append(functools.partial(gather_event, a, j, step))
    for event in events:
        event()

    for a in (1, 0):
        for k in range(n_shard):
            for step in range(nb):
                for half in range(1 if step == 0 else 2):
                    send_reduce(a, k, half, step).wait_send()
            if k < n_shard - 1:
                send_line(a, k).wait_send()
        for half in range(2):
            for step in range(nb):
                g_step(a, half, step).wait_send()
        for way in ways:
            for k in range(n_shard - 1):
                @pl.when(goes(way, k))
                def _():
                    line(a, way, k).wait_send()

                @pl.when(comes(way, k))
                def _():
                    for half in range(2):
                        for step in range(nb):
                            plane(a, way, k, half, step).wait_send()
    assert len(sems.names) <= n_sems, len(sems.names)


def reduce_and_gather(parts, gain_part, moment_pieces, decay, n_rep, n_shard, collective_id):
    nb = n_rep.bit_length() - 1
    bits = (2,) * nb
    b16 = jnp.bfloat16
    shaped = [p.reshape((n_shard,) + bits + (p.shape[0] // n_shard // n_rep, p.shape[1])) for p in parts]
    pieces = [s.shape[-2:] for s in shaped]
    own = gain_part.shape[0] // n_shard
    gain3 = gain_part.reshape(n_shard, 1, own)
    vmem, any_ = pl.BlockSpec(memory_space=pltpu.VMEM), pl.BlockSpec(memory_space=pl.ANY)
    scratch = []
    for p in pieces:
        for j in range(nb):
            scratch.append(pltpu.VMEM((n_shard,) + (2,) * (nb - 1 - j) + p, b16))
    scratch += [pltpu.VMEM((n_shard,) + p, b16) for p in pieces]
    scratch += [pltpu.VMEM(p, b16) for p in pieces] * 2
    scratch += [pltpu.VMEM(gain3.shape, F32), pltpu.VMEM((nb,) + gain3.shape, F32), pltpu.VMEM(gain3.shape, F32)]
    n_sems = 2 * (n_shard * (1 + 2 * (nb - 1)) + (n_shard - 1) + 2 * nb + 2 * (n_shard - 1) * (1 + 2 * nb)) + nb + n_shard
    scratch += [pltpu.SemaphoreType.DMA((2,)), pltpu.SemaphoreType.DMA((n_sems,)), pltpu.SemaphoreType.DMA((n_sems,))]
    out = pl.pallas_call(
        functools.partial(reduce_kernel, n_rep, n_shard, decay, n_sems),
        out_shape=[jax.ShapeDtypeStruct(bits + p, b16) for p in pieces]
        + [jax.ShapeDtypeStruct(s.shape, b16) for s in shaped]
        + [jax.ShapeDtypeStruct((1, own), F32)],
        in_specs=[vmem] * 5,
        out_specs=[any_] * 4 + [vmem],
        scratch_shapes=scratch,
        compiler_params=pltpu.CompilerParams(
            collective_id=collective_id, has_side_effects=True, vmem_limit_bytes=60 << 20
        ),
        name="reduce_and_gather",
    )(*shaped, gain3, *moment_pieces)
    g = [o.reshape(n_rep * p[0], p[1]) for o, p in zip(out[:2], pieces)]
    m = [o.reshape(q.shape) for o, q in zip(out[2:4], parts)]
    return g, m, out[4].reshape(own)


coef_a = 3.4445
coef_b = -4.775
coef_c = 2.0315
SWEEPS = 5


def nt(left, right):
    return lax.dot_general(left, right, (((1,), (1,)), ((), ())), preferred_element_type=jnp.float32)


def tn(left, right):
    return lax.dot_general(left, right, (((0,), (0,)), ((), ())), preferred_element_type=jnp.float32)


def mm(left, right):
    return jnp.dot(left, right, preferred_element_type=jnp.float32)


def eye(n):
    return lax.broadcasted_iota(jnp.int32, (n, n), 0) == lax.broadcasted_iota(jnp.int32, (n, n), 1)


def total(x):
    return jnp.sum(jnp.sum(x, axis=1, keepdims=True), axis=0, keepdims=True)


class Iterate:
    def __init__(self, e, ebf, k, kbf, h, hbf, fbf, tile, rows):
        self.e, self.ebf, self.k, self.kbf, self.h, self.hbf, self.fbf = e, ebf, k, kbf, h, hbf, fbf
        self.n = e.shape[0]
        self.tile = min(tile, self.n)
        self.rows = min(rows, self.n)

    def blocks(self, body):
        nr, nc = self.n // self.rows, self.n // self.tile

        def one(i, carry):
            j, r = lax.div(i, nr), lax.rem(i, nr)
            body(pl.ds(pl.multiple_of(r * self.rows, self.rows), self.rows),
                 pl.ds(pl.multiple_of(j * self.tile, self.tile), self.tile))
            return carry

        if nr * nc == 1:
            one(0, 0)
        else:
            lax.fori_loop(0, nr * nc, one, 0)

    def diagonals(self, body, init):
        def one(i, carry):
            d = pl.ds(pl.multiple_of(i * self.tile, self.tile), self.tile)
            return body(d, carry)

        if self.n == self.tile:
            return one(0, init)
        return lax.fori_loop(0, self.n // self.tile, one, init)

    def trace(self, ref):
        mask = eye(self.tile)
        zero = jnp.zeros((1, 1), jnp.float32)
        return self.diagonals(lambda d, c: c + total(jnp.where(mask, ref[d, d], 0.0)), zero)

    def centre(self, s):
        shift = self.trace(self.e) * (1.0 / self.n)
        mask = eye(self.tile)

        def one(d, c):
            moved = self.e[d, d] - jnp.where(mask, shift, 0.0)
            self.e[d, d] = moved
            self.ebf[d, d] = moved.astype(jnp.bfloat16)
            return c

        self.diagonals(one, 0)
        return s + shift

    def start(self, gram):
        def block(r, c):
            self.e[r, c] = gram(r, c)

        self.blocks(block)
        norm = jnp.sqrt(self.trace(self.e)) + 1e-06
        scale = 1.0 / (norm * norm)

        def scaled(r, c):
            x = self.e[r, c] * scale
            self.e[r, c] = x
            self.ebf[r, c] = x.astype(jnp.bfloat16)

        self.blocks(scaled)
        return self.centre(jnp.zeros((1, 1), jnp.float32)), 1.0 / norm

    def polynomial(self, s):
        p0 = coef_a + s * (coef_b + coef_c * s)
        p1 = coef_b + 2.0 * coef_c * s

        def block(r, c):
            f = p1 * self.e[r, c] + coef_c * mm(self.ebf[r, :], self.ebf[:, c])
            self.fbf[r, c] = f.astype(jnp.bfloat16)

        self.blocks(block)
        return p0

    def first(self):
        def block(r, c):
            f = self.fbf[r, c]
            self.h[r, c] = f.astype(jnp.float32)
            self.hbf[r, c] = f

        self.blocks(block)

    def grow(self, p0, q):
        def block(r, c):
            new = p0 * self.h[r, c] + q * self.fbf[r, c].astype(jnp.float32) + mm(self.fbf[r, :], self.hbf[:, c])
            self.k[r, c] = new

        self.blocks(block)

        def back(r, c):
            new = self.k[r, c]
            self.h[r, c] = new
            self.hbf[r, c] = new.astype(jnp.bfloat16)

        self.blocks(back)

    def advance(self, p0, s):
        def inner(r, c):
            new = p0 * self.e[r, c] + s * self.fbf[r, c].astype(jnp.float32) + mm(self.fbf[r, :], self.ebf[:, c])
            self.k[r, c] = new
            self.kbf[r, c] = new.astype(jnp.bfloat16)

        self.blocks(inner)
        beta = p0 * s

        def outer(r, c):
            new = p0 * self.k[r, c] + beta * self.fbf[r, c].astype(jnp.float32) + mm(self.fbf[r, :], self.kbf[:, c])
            self.e[r, c] = new
            self.ebf[r, c] = new.astype(jnp.bfloat16)

        self.blocks(outer)
        return self.centre(p0 * beta)


def muon_kernel(wide, m_in, m_out, h_out, hs_out, scal, x, *scratch):
    big = Iterate(*scratch[:7], tile=256, rows=512)
    small = Iterate(*scratch[7:], tile=256, rows=256)
    core = lax.rem(lax.axis_index("rep"), 2)
    n, ns = big.n, small.n

    @pl.when(core == 0)
    def _():
        def turn(i, c):
            r = pl.ds(pl.multiple_of(i * 256, 256), 256)
            x[:, r] = m_in[r, pl.ds(0, n)].T
            return c

        lax.fori_loop(0, wide // 256, turn, 0)

    @pl.when(core != 0)
    def _():
        def take(i, c):
            r = pl.ds(pl.multiple_of(i * 128, 128), 128)
            x[r, :] = m_out[r, :]
            return c

        lax.fori_loop(0, n // 128, take, 0)

    s, inv = big.start(lambda r, c: nt(x[r, :], x[c, :]))
    mine = m_in.at[:, pl.ds(pl.multiple_of(n + core * ns, 128), ns)]
    ss, sinv = small.start(lambda r, c: tn(mine[:, r], mine[:, c]))

    def sweep(it, carry):
        s, q, ss, sq = carry
        p0, sp0 = big.polynomial(s), small.polynomial(ss)

        @pl.when(it == 0)
        def _():
            big.first()
            small.first()

        @pl.when(it > 0)
        def _():
            big.grow(p0, q)
            small.grow(sp0, sq)

        q, sq = p0 * q, sp0 * sq
        s, ss = lax.cond(
            it < SWEEPS - 1,
            lambda: (big.advance(p0, s), small.advance(sp0, ss)),
            lambda: (s, ss),
        )
        return s, q, ss, sq

    one = jnp.ones((1, 1), jnp.float32)
    s, q, ss, sq = lax.fori_loop(0, SWEEPS, sweep, (s, one, ss, one))
    h_out[...] = big.hbf[...]
    hs_out[...] = small.hbf[...]
    row = lax.broadcasted_iota(jnp.int32, (8, 128), 0)
    scal[...] = jnp.where(row == 0, q * inv, jnp.where(row == 1, inv, jnp.where(row == 2, sq * sinv, sinv)))


def muon(m_in, m_out, kv):
    wide, n = m_in.shape[0], m_out.shape[0]
    sets = []
    for d in (n, kv):
        f32, b16 = pltpu.VMEM((d, d), jnp.float32), pltpu.VMEM((d, d), jnp.bfloat16)
        sets += [f32, b16, f32, b16, f32, b16, b16]
    vmem = pl.BlockSpec(memory_space=pltpu.VMEM)
    return pl.pallas_call(
        functools.partial(muon_kernel, wide),
        out_shape=[
            jax.ShapeDtypeStruct((n, n), jnp.bfloat16),
            jax.ShapeDtypeStruct((kv, kv), jnp.bfloat16),
            jax.ShapeDtypeStruct((8, 128), jnp.float32),
        ],
        in_specs=[vmem] * 2,
        out_specs=[vmem] * 3,
        scratch_shapes=[pltpu.VMEM((n, wide), jnp.bfloat16)] + sets,
        compiler_params=pltpu.CompilerParams(vmem_limit_bytes=60 << 20),
        name="muon",
    )(m_in, m_out)


HEAD_SIZE = 64

norm_eps = 1e-05
rope_base = 500000.0
decay = 0.95
muon_rate = 0.02
gain_rate = 0.2


def positions_of(seq_segments):
    sequence_length = seq_segments.shape[0]
    token_index = jnp.arange(sequence_length, dtype=jnp.int32)
    before = jnp.concatenate([seq_segments[:1] - 1, seq_segments[:-1]])
    starts = jnp.where(seq_segments != before, token_index, jnp.zeros_like(token_index))
    return token_index - lax.cummax(starts, axis=0)


def rope_tables(seq_segments, head_dim):
    position = positions_of(seq_segments).astype(jnp.float32)
    half_dim = head_dim // 2
    frequency = rope_base ** (-2.0 * jnp.arange(half_dim, dtype=jnp.float32) / head_dim)
    angles = position[:, None] * frequency[None, :]
    return (jnp.cos(angles)[:, None, :], jnp.sin(angles)[:, None, :])


def apply_rotary(values, cosine_table, sine_table):
    half_dim = values.shape[-1] // 2
    front_half = values[..., :half_dim]
    back_half = values[..., half_dim:]
    return jnp.concatenate(
        [
            front_half * cosine_table - back_half * sine_table,
            back_half * cosine_table + front_half * sine_table,
        ],
        -1,
    )


def contract_rows(left, right, dtype=jnp.float32):
    return lax.dot_general(left, right, (((0,), (0,)), ((), ())), preferred_element_type=jnp.float32).astype(dtype)


def contract_cols(left, right):
    return lax.dot_general(left, right, (((1,), (1,)), ((), ())), preferred_element_type=jnp.float32)


def head_forward(q_head, k_head, v_head, allowed, score_scale):
    scores = jnp.einsum("qgd,kd->gqk", q_head, k_head, preferred_element_type=jnp.float32) * score_scale
    exponent = jnp.where(allowed[None], jnp.exp(scores), jnp.zeros_like(scores))
    denom_sum = jnp.sum(exponent, -1, keepdims=True)
    probabilities = (exponent / denom_sum).astype(jnp.bfloat16)
    attended = jnp.einsum("gqk,kd->qgd", probabilities, v_head, preferred_element_type=jnp.float32)
    return (attended, jnp.log(denom_sum))


def head_backward(q_head, k_head, v_head, log_sum, grad_head, allowed, score_scale):
    scores = jnp.einsum("qgd,kd->gqk", q_head, k_head, preferred_element_type=jnp.float32) * score_scale
    recomputed = jnp.where(allowed[None], jnp.exp(scores - log_sum), jnp.zeros_like(scores))
    rounded = recomputed.astype(jnp.bfloat16)
    value_grad = jnp.einsum("gqk,qgd->kd", rounded, grad_head, preferred_element_type=jnp.float32)
    prob_grad = jnp.einsum("qgd,kd->gqk", grad_head, v_head, preferred_element_type=jnp.float32)
    row_inner = jnp.sum(recomputed * prob_grad, -1, keepdims=True)
    score_grad = (recomputed * (prob_grad - row_inner) * score_scale).astype(jnp.bfloat16)
    query_grad = jnp.einsum("gqk,kd->qgd", score_grad, k_head, preferred_element_type=jnp.float32)
    key_grad = jnp.einsum("gqk,qgd->kd", score_grad, q_head, preferred_element_type=jnp.float32)
    return (query_grad, key_grad, value_grad)


def attention(query_rows, rotated_keys, values_bfloat, dattn_of, allowed, score_scale):
    sequence_length, query_heads = query_rows.shape[:2]
    kv_heads = rotated_keys.shape[1]
    group_width = query_heads // kv_heads
    query_width = query_heads * HEAD_SIZE
    query_head_rows = query_rows.reshape(sequence_length, kv_heads, group_width, HEAD_SIZE).transpose(1, 0, 2, 3)
    k_heads = rotated_keys.transpose(1, 0, 2)
    v_heads = values_bfloat.transpose(1, 0, 2)
    attended, log_sum = lax.map(
        lambda blocks: head_forward(blocks[0], blocks[1], blocks[2], allowed, score_scale),
        (query_head_rows, k_heads, v_heads),
    )
    attn_bf = attended.transpose(1, 0, 2, 3).reshape(sequence_length, query_width).astype(jnp.bfloat16)
    head_gradients = dattn_of().reshape(sequence_length, kv_heads, group_width, HEAD_SIZE).transpose(1, 0, 2, 3)
    query_grad, key_grad, value_grad = lax.map(
        lambda blocks: head_backward(blocks[0], blocks[1], blocks[2], blocks[3], blocks[4], allowed, score_scale),
        (query_head_rows, k_heads, v_heads, log_sum, head_gradients),
    )
    return (
        attn_bf,
        query_grad.transpose(1, 0, 2, 3).reshape(sequence_length, query_heads, HEAD_SIZE),
        key_grad.transpose(1, 0, 2),
        value_grad.transpose(1, 0, 2),
    )


def rows_of(matrix, index, count):
    return lax.dynamic_slice_in_dim(matrix, index * count, count, 0)


def cols_of(matrix, index, count):
    return lax.dynamic_slice_in_dim(matrix, index * count, count, 1)


def on_device(
    tokens,
    segments,
    cotangent,
    gain,
    w_query,
    w_key,
    w_value,
    w_outproj,
    moment_gain,
    moment_query,
    moment_key,
    moment_value,
    moment_outproj,
):
    n_rep = lax.axis_size("rep")
    n_shard = lax.axis_size("shard")
    rep_index = lax.axis_index("rep")
    shard_index = lax.axis_index("shard")
    sequence_length = tokens.shape[1]
    query_width = w_query.shape[1]
    kv_width = w_key.shape[1]
    query_heads = query_width // HEAD_SIZE
    kv_heads = kv_width // HEAD_SIZE
    score_scale = 1.0 / math.sqrt(HEAD_SIZE)
    total_tokens = tokens.shape[0] * sequence_length * n_rep * n_shard
    seq_tokens = tokens[0]
    seq_segments = segments[0]
    seq_cotangent = cotangent[0]
    b16, f32 = jnp.bfloat16, jnp.float32
    w_in_bf = jnp.concatenate([w_query, w_key, w_value], 1).astype(b16)
    w_out_bf = w_outproj.astype(b16)
    w_in_all, w_out_all, gain_all = gather_all(
        [w_in_bf, w_out_bf], gain.astype(b16).astype(f32), n_rep, n_shard, 0
    )
    tok_float = seq_tokens.astype(f32)
    inv_rms = lax.rsqrt(jnp.mean(tok_float * tok_float, -1, keepdims=True) + norm_eps)
    normed = tok_float * inv_rms
    norm_bf = (normed * gain_all).astype(b16)
    projected_rows = jnp.dot(norm_bf, w_in_all, preferred_element_type=f32)
    cosine_table, sine_table = rope_tables(seq_segments, HEAD_SIZE)
    query_rows = apply_rotary(
        projected_rows[:, :query_width].reshape(sequence_length, query_heads, HEAD_SIZE), cosine_table, sine_table
    ).astype(b16)
    rotated_keys = apply_rotary(
        projected_rows[:, query_width : query_width + kv_width].reshape(sequence_length, kv_heads, HEAD_SIZE),
        cosine_table,
        sine_table,
    ).astype(b16)
    values_bfloat = projected_rows[:, query_width + kv_width :].reshape(sequence_length, kv_heads, HEAD_SIZE).astype(b16)
    token_index = jnp.arange(sequence_length, dtype=jnp.int32)
    allowed = (token_index[None, :] <= token_index[:, None]) & (seq_segments[None, :] == seq_segments[:, None])
    attn_bf, query_grad, key_grad, value_grad = attention(
        query_rows,
        rotated_keys,
        values_bfloat,
        lambda: contract_cols(seq_cotangent, w_out_all).astype(b16),
        allowed,
        score_scale,
    )
    branch_out = jnp.dot(attn_bf, w_out_all, preferred_element_type=f32)
    result = (tok_float + branch_out).astype(b16)
    part_outproj = contract_rows(attn_bf, seq_cotangent, b16)
    grad_qkv = jnp.concatenate(
        [
            apply_rotary(query_grad, cosine_table, -sine_table).reshape(sequence_length, query_width),
            apply_rotary(key_grad, cosine_table, -sine_table).reshape(sequence_length, kv_width),
            value_grad.reshape(sequence_length, kv_width),
        ],
        1,
    ).astype(b16)
    part_in = contract_rows(norm_bf, grad_qkv, b16)
    grad_normed = contract_cols(grad_qkv, w_in_all)
    part_gain = jnp.sum(grad_normed * normed, 0)
    grad_hat = grad_normed * gain_all
    grad_tokens = (
        seq_cotangent.astype(f32) + inv_rms * (grad_hat - normed * jnp.mean(grad_hat * normed, -1, keepdims=True))
    ).astype(b16)
    return finish(
        result, grad_tokens, part_in, part_outproj, part_gain, total_tokens, gain, (w_query, w_key, w_value, w_outproj),
        moment_gain, (moment_query, moment_key, moment_value, moment_outproj),
    )


def finish(result, grad_tokens, part_in, part_outproj, part_gain, total_tokens, gain, weights, moment_gain, moments):
    n_rep, n_shard = lax.axis_size("rep"), lax.axis_size("shard")
    rep_index, shard_index = lax.axis_index("rep"), lax.axis_index("shard")
    b16, f32 = jnp.bfloat16, jnp.float32
    w_query, w_key, w_value, w_outproj = weights
    query_width, kv_width = w_query.shape[1], w_key.shape[1]
    in_piece = jnp.concatenate([rows_of(m, rep_index, m.shape[0] // n_rep) for m in moments[:3]], 1)
    out_piece = rows_of(moments[3], rep_index, moments[3].shape[0] // n_rep)
    (sum_in, sum_out), (m_in, m_out), grad_gain = reduce_and_gather(
        [part_in, part_outproj], part_gain, [in_piece, out_piece], decay, n_rep, n_shard, 1
    )
    grads = [
        sum_in[:, :query_width].astype(f32),
        sum_in[:, query_width : query_width + kv_width].astype(f32),
        sum_in[:, query_width + kv_width :].astype(f32),
        sum_out.astype(f32),
    ]
    moments_next = [decay * m + g for m, g in zip(moments, grads)]
    moment_gain_next = decay * moment_gain + grad_gain
    gain_next = gain - gain_rate / math.sqrt(total_tokens) * moment_gain_next
    own_in = jnp.concatenate([m.astype(b16) for m in moments_next[:3]], 1)
    own_out = moments_next[3].astype(b16)
    m_in = lax.dynamic_update_slice_in_dim(m_in, own_in, shard_index * own_in.shape[0], 0)
    m_out = lax.dynamic_update_slice_in_dim(m_out, own_out, shard_index * own_out.shape[0], 0)
    mix, mix_kv, scales = muon(m_in, m_out, kv_width)
    core = lax.rem(rep_index, 2)
    other = rep_index + 1 - 2 * core
    widths = [w.shape[1] // n_rep for w in weights]
    pairs = [(i, i ^ 1) for i in range(n_rep)]
    out_rows = w_outproj.shape[0]
    theirs = lax.ppermute(
        (
            rows_of(mix, other, widths[0]),
            rows_of(mix, shard_index, out_rows),
            rows_of(mix_kv, other, widths[1]),
            scales,
        ),
        "rep",
        pairs,
    )
    even = core == 0
    mix_query = jnp.where(even, rows_of(mix, rep_index, widths[0]), theirs[0])
    mix_out = jnp.where(even, theirs[1], rows_of(mix, shard_index, out_rows))
    kv_mine = rows_of(mix_kv, rep_index, widths[1])
    mix_key, mix_value = jnp.where(even, kv_mine, theirs[2]), jnp.where(even, theirs[2], kv_mine)
    first, second = jnp.where(even, scales, theirs[3]), jnp.where(even, theirs[3], scales)
    spans = (
        (0, query_width, mix_query, first[0, 0], first[1, 0]),
        (query_width, kv_width, mix_key, first[2, 0], first[3, 0]),
        (query_width + kv_width, kv_width, mix_value, second[2, 0], second[3, 0]),
    )
    updated = []
    for i, (at, width, mix_rows, straight, mixed) in enumerate(spans):
        whole = (weights[i].shape[0] * n_shard, width)
        ortho = straight * cols_of(moments_next[i], rep_index, widths[i]) + mixed * contract_cols(
            own_in[:, at : at + width], mix_rows
        )
        updated.append(cols_of(weights[i], rep_index, widths[i]) - muon_rate * math.sqrt(max(whole)) * ortho)
    whole = (out_rows * n_shard, w_outproj.shape[1])
    ortho = second[0, 0] * cols_of(moments_next[3], rep_index, widths[3]) + second[1, 0] * jnp.dot(
        mix_out, cols_of(m_out, rep_index, widths[3]), preferred_element_type=f32
    )
    updated.append(cols_of(w_outproj, rep_index, widths[3]) - muon_rate * math.sqrt(max(whole)) * ortho)
    return (
        result[None],
        grad_tokens[None],
        grad_gain,
        *grads,
        gain_next,
        *updated,
        moment_gain_next,
        *moments_next,
    )


def solution(mesh):
    in_specs = (
        P(("rep", "shard"), None, None),
        P(("rep", "shard"), None),
        P(("rep", "shard"), None, None),
        P("shard"),
        P("shard", None),
        P("shard", None),
        P("shard", None),
        P("shard", None),
        P("shard"),
        P("shard", None),
        P("shard", None),
        P("shard", None),
        P("shard", None),
    )
    out_specs = (
        P(("rep", "shard"), None, None),
        P(("rep", "shard"), None, None),
        P("shard"),
        P("shard", None),
        P("shard", None),
        P("shard", None),
        P("shard", None),
        P("shard"),
        P("shard", "rep"),
        P("shard", "rep"),
        P("shard", "rep"),
        P("shard", "rep"),
        P("shard"),
        P("shard", None),
        P("shard", None),
        P("shard", None),
        P("shard", None),
    )
    return jax.shard_map(on_device, mesh=mesh, in_specs=in_specs, out_specs=out_specs, check_vma=False)
```

time: 1460 us -> 511 us (0.35)
  waiting for transfers between devices: 609 us -> 0.01 us
  matrix products: 578 us -> 160 us
  Pallas kernels: 0 us -> 271 us
  blocking collectives: 99.4 us -> 0 us
  other arithmetic: 67.1 us -> 32.9 us
  loops' own time: 30 us -> 0.43 us
  local copies, waits for them, and re-layouts: 50.2 us -> 34.3 us
    dot_general x17 -> x3, matrix products: 414 us -> 15.8 us  [the longest x1 6.45 us: on_device(): branch_out = jnp.dot(attn_bf, w_out_all, preferred_element_type=f32)]
    pallas_call x0 -> x3, Pallas kernels: none -> 271 us  [the longest x1 122 us: reduce_and_gather(): pl.pallas_call(functools.partial(reduce_kernel, n_rep, n_shard, decay, n_...]
    psum x2 -> x0, waiting for transfers between devices: 251 us -> none  [the longest x1 154 us: from_root(): return lax.psum(block, axis)]
    reduce_scatter x2 -> x0, waiting for transfers between devices: 220 us -> none  [the longest x1 215 us: on_device(): lax.psum_scatter(grad_in_local, 'shard', scatter_dimension=0, tiled=True)]
    all_gather x6 -> x0, waiting for transfers between devices: 138 us -> none  [the longest x1 97.6 us: on_device(): w_piece = lax.all_gather(w_in_bf, 'shard', axis=0, tiled=True)]
    all_gather x5 -> x0, blocking collectives: 78.2 us -> none  [the longest x1 16.7 us: on_device(): lax.all_gather(part_query.astype(jnp.bfloat16), 'shard', axis=0, tiled=True)]
    another operation x6 -> x2, loops' own time: 30 us -> 0.43 us  [the longest x1 0.3 us: attention(): lax.map(lambda blocks: head_backward(blocks[0], blocks[1], blocks[2], blo...]
  transfers between devices with their start and end apart: 10 -> 4, of which waited for: 7 -> 0; matrix products, arithmetic and copies ran while one was open for 45% -> 5% of each run, Pallas kernels for 0% -> 0%
where the time goes in v1:
time: 511 us; the launch traced here: 502 us
  Pallas kernels  271 us (53%)
  matrix products  160 us (31%)
  local copies, waits for them, and re-layouts  34.3 us (7%)
  other arithmetic  32.9 us (6%)
    pallas_call x1, Pallas kernels, reduce_and_gather(): pl.pallas_call(functools.partial(reduce_kernel, n_rep, n_shard, decay, n_...  122 us
    pallas_call x1, Pallas kernels, muon(): pl.pallas_call(functools.partial(muon_kernel, wide), out_shape=[jax.Shape...  87.1 us
    pallas_call x1, Pallas kernels, gather_all(): pl.pallas_call(functools.partial(gather_kernel, n_rep, n_shard, n), out_s...  61.8 us
    dot_general x4, matrix products, head_backward(): jnp.einsum('gqk,kd->qgd', score_grad, k_head, preferred_element_type=jnp....  37.9 us
    dot_general x4, matrix products, head_backward(): jnp.einsum('gqk,qgd->kd', score_grad, q_head, preferred_element_type=jnp....  31.9 us
    dot_general x5, matrix products, contract_cols(): lax.dot_general(left, right, (((1,), (1,)), ((), ())), preferred_element_...  21.5 us
    dot_general x4, matrix products, head_backward(): jnp.einsum('qgd,kd->gqk', grad_head, v_head, preferred_element_type=jnp.f...  14.5 us
    while x48, local copies, waits for them, and re-layouts  11.9 us
  transfers between devices with their start and end apart: 4, of which 0 were waited for; matrix products, arithmetic and copies ran while one was open for 5% of the time, Pallas kernels for 0%

profile of v1, /device:TPU:0, one launch (start us, length us, event | category | flops | bytes accessed | tf_op | source)
XLA Modules:
  0.0 502.2 jit_solution(10378758607777022275)
XLA Ops:
  3.2 2.1 fusion.101
  9.0 61.8 %gather_all.1 = (bf16[4,2,2,2,64,1536]{5,4,3,2,1,0:T(8,128)(2,1)}, bf16[4,2,2,2,32,2048]{5,4,3,2,1,0:T(8,128)(2,1)}, f32[4,1,512]{2,1,0:T(1,128)}) custom-call(bf16[2,2,2,64,1536]{4,3,2,1,0:T(8,128)(2,1)} %pad_maximum_fusion.refs_0_, bf16[2,2,2,32,2048]{4,3,2,1,0:T(8,128)(2,1)} %bitcast.374, f32[1,512]{1,0:T(1,128)} %bitcast.397), custom_call_target="tpu_custom_call" | custom-call | tf_op jit(solution)/shard_map/gather_all/pallas_call | solution.py:193
  70.8 5.6 %fusion.107 = f32[512,1536]{1,0:T(8,128)S(1)} fusion(bf16[2048,1536]{1,0:T(8,128)(2,1)} %bitcast.402, bf16[1,512,2048]{2,1,0:T(8,128)(2,1)S(1)} %copy-done.1, f32[2048]{0:T(1024)} %bitcast.398, f32[512]{0:T(512)S(1)} %add_rsqrt_fusion), kind=kOutput, calls=%fused_computation.103 | convolution fusion | flops 3225419776 | bytes 11544576 | tf_op jit(solution)/shard_map/dot_general | solution.py:879
  80.7 2.9 copy.56
  84.1 1.9 subtract_convert_fusion.1
  86.9 22.1 %while.30 = (s32[]{:T(128)}, bf16[4,512,4,64]{1,3,2,0:T(8,128)(2,1)}, f32[4,4,512,1]{2,1,3,0:T(4,128)}, bf16[4,512,64]{1,2,0:T(8,128)(2,1)}, bf16[4,512,64]{1,2,...) while((s32[]{:T(128)}, bf16[4,512,4,64]{1,3,2,0:T(8,128)(2,1)}, ...), condition=%wide.region_5.6_spmd.clone.clone, body=%wide.region_3.5_spmd.clone.sunk.clone | while | flops 276559872 | bytes 18518160 | solution.py:814
  87.1 2.2 fusion.209
  89.3 2.1 fusion.210
  92.6 2.2 fusion.209
  94.8 2.1 fusion.210
  98.1 2.2 fusion.209
  100.3 2.1 fusion.210
  103.6 2.2 fusion.209
  105.8 2.1 fusion.210
  108.9 6.2 %fusion.118 = bf16[1024,512]{1,0:T(8,128)(2,1)} fusion(bf16[1024,2048]{1,0:T(8,128)(2,1)} %bitcast.366, bf16[1,512,2048]{2,1,0:T(8,128)(2,1)} %param.19), kind=kOutput, calls=%fused_computation.117 | convolution fusion | flops 2148007936 | bytes 7340032 | tf_op jit(solution)/shard_map/dot_general | solution.py:781
  115.1 109.6 %while.31 = (s32[]{:T(128)}, f32[4,512,4,64]{1,3,2,0:T(8,128)}, f32[4,512,64]{1,2,0:T(8,128)}, bf16[4,512,64]{1,2,0:T(8,128)(2,1)}, bf16[4,512,64]{1,2,0:T(8,128...) while((s32[]{:T(128)}, f32[4,512,4,64]{1,3,2,0:T(8,128)}, ...), condition=%wide.region_8.9_spmd.clone.clone, body=%wide.region_6.8_spmd.clone.sunk.clone | while | flops 699143168 | bytes 72875232 | solution.py:820
  117.9 1.9 copy-done
  121.6 3.6 fusion.219
  125.2 8.0 %fusion.223 = f32[4,512,64]{1,2,0:T(8,128)} fusion(f32[4,512,64]{1,2,0:T(8,128)} %get-tuple-element.470, s32[]{:T(128)S(6)} %copy.85, f32[512,512,4]{1,0,2:T(8,128)} %fusion.219, f32[512,512,4]{1,0,2:T(8,128)} %copy-done, f32[4,512]{1,0:T(4,128)S(1)} %dynamic-slice_bitcast_fusion.3, pred[512,512]{0,1:T(8,128)(4,1)S(1)} %fusion.221, ...), kind=kOutput, calls=%fused_computation.48.clone.1.clone | convolution fusion | flops 145754624 | bytes 17712128 | tf_op jit(solution)/shard_map/while/body/eval_jaxpr/gqk,qgd->kd/dot_general | solution.py:802
  133.2 9.5 %fusion.222 = f32[4,512,4,64]{1,3,2,0:T(8,128)} fusion(f32[4,512,4,64]{1,3,2,0:T(8,128)} %get-tuple-element.469, s32[]{:T(128)S(6)} %copy.85, f32[512,512,4]{1,0,2:T(8,128)} %fusion.219, f32[512,512,4]{1,0,2:T(8,128)} %copy-done, f32[4,512]{1,0:T(4,128)S(1)} %dynamic-slice_bitcast_fusion.3, pred[512,512]{0,1:T(8,128)(4,1)S(1)} %fusion.221, ...), kind=kOutput, calls=%fused_computation.44.clone.1.clone | convolution fusion | flops 145754624 | bytes 17908736 | tf_op jit(solution)/shard_map/while/body/eval_jaxpr/gqk,kd->qgd/dot_general | solution.py:801
  145.3 1.9 copy-done
  148.9 3.6 fusion.219
  152.6 8.0 %fusion.223 = f32[4,512,64]{1,2,0:T(8,128)} fusion(f32[4,512,64]{1,2,0:T(8,128)} %get-tuple-element.470, s32[]{:T(128)S(6)} %copy.85, f32[512,512,4]{1,0,2:T(8,128)} %fusion.219, f32[512,512,4]{1,0,2:T(8,128)} %copy-done, f32[4,512]{1,0:T(4,128)S(1)} %dynamic-slice_bitcast_fusion.3, pred[512,512]{0,1:T(8,128)(4,1)S(1)} %fusion.221, ...), kind=kOutput, calls=%fused_computation.48.clone.1.clone | convolution fusion | flops 145754624 | bytes 17712128 | tf_op jit(solution)/shard_map/while/body/eval_jaxpr/gqk,qgd->kd/dot_general | solution.py:802
  160.5 9.5 %fusion.222 = f32[4,512,4,64]{1,3,2,0:T(8,128)} fusion(f32[4,512,4,64]{1,3,2,0:T(8,128)} %get-tuple-element.469, s32[]{:T(128)S(6)} %copy.85, f32[512,512,4]{1,0,2:T(8,128)} %fusion.219, f32[512,512,4]{1,0,2:T(8,128)} %copy-done, f32[4,512]{1,0:T(4,128)S(1)} %dynamic-slice_bitcast_fusion.3, pred[512,512]{0,1:T(8,128)(4,1)S(1)} %fusion.221, ...), kind=kOutput, calls=%fused_computation.44.clone.1.clone | convolution fusion | flops 145754624 | bytes 17908736 | tf_op jit(solution)/shard_map/while/body/eval_jaxpr/gqk,kd->qgd/dot_general | solution.py:801
  172.6 1.9 copy-done
  176.3 3.6 fusion.219
  179.9 8.0 %fusion.223 = f32[4,512,64]{1,2,0:T(8,128)} fusion(f32[4,512,64]{1,2,0:T(8,128)} %get-tuple-element.470, s32[]{:T(128)S(6)} %copy.85, f32[512,512,4]{1,0,2:T(8,128)} %fusion.219, f32[512,512,4]{1,0,2:T(8,128)} %copy-done, f32[4,512]{1,0:T(4,128)S(1)} %dynamic-slice_bitcast_fusion.3, pred[512,512]{0,1:T(8,128)(4,1)S(1)} %fusion.221, ...), kind=kOutput, calls=%fused_computation.48.clone.1.clone | convolution fusion | flops 145754624 | bytes 17712128 | tf_op jit(solution)/shard_map/while/body/eval_jaxpr/gqk,qgd->kd/dot_general | solution.py:802
  187.9 9.5 %fusion.222 = f32[4,512,4,64]{1,3,2,0:T(8,128)} fusion(f32[4,512,4,64]{1,3,2,0:T(8,128)} %get-tuple-element.469, s32[]{:T(128)S(6)} %copy.85, f32[512,512,4]{1,0,2:T(8,128)} %fusion.219, f32[512,512,4]{1,0,2:T(8,128)} %copy-done, f32[4,512]{1,0:T(4,128)S(1)} %dynamic-slice_bitcast_fusion.3, pred[512,512]{0,1:T(8,128)(4,1)S(1)} %fusion.221, ...), kind=kOutput, calls=%fused_computation.44.clone.1.clone | convolution fusion | flops 145754624 | bytes 17908736 | tf_op jit(solution)/shard_map/while/body/eval_jaxpr/gqk,kd->qgd/dot_general | solution.py:801
  200.0 1.9 copy-done
  203.6 3.6 fusion.219
  207.3 8.0 %fusion.223 = f32[4,512,64]{1,2,0:T(8,128)} fusion(f32[4,512,64]{1,2,0:T(8,128)} %get-tuple-element.470, s32[]{:T(128)S(6)} %copy.85, f32[512,512,4]{1,0,2:T(8,128)} %fusion.219, f32[512,512,4]{1,0,2:T(8,128)} %copy-done, f32[4,512]{1,0:T(4,128)S(1)} %dynamic-slice_bitcast_fusion.3, pred[512,512]{0,1:T(8,128)(4,1)S(1)} %fusion.221, ...), kind=kOutput, calls=%fused_computation.48.clone.1.clone | convolution fusion | flops 145754624 | bytes 17712128 | tf_op jit(solution)/shard_map/while/body/eval_jaxpr/gqk,qgd->kd/dot_general | solution.py:802
  215.2 9.5 %fusion.222 = f32[4,512,4,64]{1,3,2,0:T(8,128)} fusion(f32[4,512,4,64]{1,3,2,0:T(8,128)} %get-tuple-element.469, s32[]{:T(128)S(6)} %copy.85, f32[512,512,4]{1,0,2:T(8,128)} %fusion.219, f32[512,512,4]{1,0,2:T(8,128)} %copy-done, f32[4,512]{1,0:T(4,128)S(1)} %dynamic-slice_bitcast_fusion.3, pred[512,512]{0,1:T(8,128)(4,1)S(1)} %fusion.221, ...), kind=kOutput, calls=%fused_computation.44.clone.1.clone | convolution fusion | flops 145754624 | bytes 17908736 | tf_op jit(solution)/shard_map/while/body/eval_jaxpr/gqk,kd->qgd/dot_general | solution.py:801
  224.7 2.0 subtract_convert_fusion
  228.5 6.5 %fusion.100 = (f32[2048]{0:T(1024)}, f32[512]{0:T(512)S(1)}, f32[512,2048]{1,0:T(8,128)}) fusion(bf16[1,512,2048]{2,1,0:T(8,128)(2,1)S(1)} %copy-done.1, f32[512]{0:T(512)S(1)} %add_rsqrt_fusion, f32[2048]{0:T(1024)S(1)} %bitcast.399, bf16[2048,1536]{1,0:T(8,128)(2,1)S(1)} %bitcast.403, bf16[512,256]{0,1:T(8,128)(2,1)S(1)} %bitcast.404, ...), kind=kOutput, calls=%fused_computation.95 | convolution fusion | flops 3233281536 | bytes 14176256 | tf_op jit(solution)/shard_map/dot_general | solution.py:781
  235.0 6.8 %convolution_convert_fusion = bf16[2048,1536]{1,0:T(8,128)(2,1)} fusion(bf16[1,512,2048]{2,1,0:T(8,128)(2,1)S(1)} %copy-done.1, f32[2048]{0:T(1024)S(1)} %bitcast.400, f32[512]{0:T(512)S(1)} %add_rsqrt_fusion, bf16[512,256]{0,1:T(8,128)(2,1)S(1)} %bitcast.405, bf16[512,256]{0,1:T(8,128)(2,1)S(1)} %bitcast.393, bf16[512,1024]{0,1:T(8,128)(2,1)S(1)} %bitcast.387), kind=kOutput, calls=%fused_computation.79 | convolution fusion | flops 3233284096 | bytes 9971712 | tf_op jit(solution)/shard_map/dot_general | solution.py:777
  241.8 4.3 convolution_convert_fusion.1
  249.6 122.5 %reduce_and_gather.1 = (bf16[2,2,2,64,1536]{4,3,2,1,0:T(8,128)(2,1)}, bf16[2,2,2,32,2048]{4,3,2,1,0:T(8,128)(2,1)}, bf16[4,2,2,2,64,1536]{5,4,3,2,1,0:T(8,128)(2...) custom-call(bf16[4,2,2,2,64,1536]{5,4,3,2,1,0:T(8,128)(2,1)} %bitcast.369, ...), custom_call_target="tpu_custom_call" | custom-call | tf_op jit(solution)/shard_map/reduce_and_gather/pallas_call | solution.py:499
  372.1 2.7 fusion.159
  374.8 2.6 fusion.157
  377.5 5.0 convert_dynamic-update-slice_fusion
  383.7 87.1 %muon.1 = (bf16[1024,1024]{1,0:T(8,128)(2,1)}, bf16[256,256]{1,0:T(8,128)(2,1)}, f32[8,128]{1,0:T(8,128)}) custom-call(bf16[2048,1536]{1,0:T(8,128)(2,1)} %maximum_dynamic-update-slice_fusion.m_in, bf16[1024,2048]{1,0:T(8,128)(2,1)} %get-tuple-element.246.m_out), custom_call_target="tpu_custom_call" | custom-call | tf_op jit(solution)/shard_map/muon/pallas_call | solution.py:723
  473.7 1.9 constant_dynamic-slice_fusion.1
  476.1 6.4 %fusion.105 = bf16[1,512,2048]{2,1,0:T(8,128)(2,1)} fusion(bf16[512,1024]{0,1:T(8,128)(2,1)} %bitcast.371, bf16[1024,2048]{1,0:T(8,128)(2,1)} %bitcast.367, bf16[1,512,2048]{2,1,0:T(8,128)(2,1)S(1)} %copy-done.1), kind=kOutput, calls=%fused_computation.101 | convolution fusion | flops 2150629376 | bytes 9437184 | tf_op jit(solution)/shard_map/dot_general | solution.py:900
  482.7 2.8 fusion.110
  487.2 2.7 multiply_subtract_fusion.1
  490.7 2.6 multiply_subtract_fusion.2
  494.0 3.5 multiply_subtract_fusion.3
  497.5 3.7 multiply_subtract_fusion
  (165 shorter events, 46.8 us)
Async XLA Ops:
  0.7 5.7 %copy-start.14 = (f32[512,256]{1,0:T(8,128)S(1)}, f32[512,256]{1,0:T(8,128)}, u32[]{:S(2)}) copy-start(f32[512,256]{1,0:T(8,128)} %param.23) | copy-start | bytes 1572868
  0.7 5.8 %copy-start.6 = (f32[512,1024]{1,0:T(8,128)S(1)}, f32[512,1024]{1,0:T(8,128)}, u32[]{:S(2)}) copy-start(f32[512,1024]{1,0:T(8,128)} %param.21) | copy-start | bytes 6291460
  1.8 4.8 copy-start.7
  6.6 64.2 %copy-start.1 = (bf16[1,512,2048]{2,1,0:T(8,128)(2,1)S(1)}, bf16[1,512,2048]{2,1,0:T(8,128)(2,1)}, u32[]{:S(2)}) copy-start(bf16[1,512,2048]{2,1,0:T(8,128)(2,1)} %param.17) | copy-start | bytes 6291460
  76.4 1.6 copy-start.15
  86.9 2.4 copy-start.2
  91.4 1.0 copy-start.3
  92.4 2.4 copy-start.2
  96.9 1.0 copy-start.3
  97.9 2.4 copy-start.2
  102.4 1.0 copy-start.3
  103.4 2.4 copy-start.2
  108.0 1.0 copy-start.3
  115.3 4.6 copy-start.12
  115.3 4.6 copy-start.24
  117.9 1.9 copy-start
  120.9 0.7 copy-start.25
  142.7 4.5 copy-start.12
  142.7 4.5 copy-start.24
  145.3 1.9 copy-start
  148.2 0.7 copy-start.25
  170.0 4.5 copy-start.12
  170.0 4.5 copy-start.24
  172.6 1.9 copy-start
  175.6 0.7 copy-start.25
  197.4 4.5 copy-start.12
  197.4 4.5 copy-start.24
  200.0 1.9 copy-start
  224.7 3.8 copy-start.20
  224.7 3.8 copy-start.23
  224.7 3.8 copy-start.26
  235.0 6.8 %copy-start.4 = (bf16[4,512,4,64]{1,3,2,0:T(8,128)(2,1)S(1)}, bf16[4,512,4,64]{1,3,2,0:T(8,128)(2,1)}, u32[]{:S(2)}) copy-start(bf16[4,512,4,64]{1,3,2,0:T(8,128)(2,1)} %get-tuple-element.122) | copy-start | bytes 3145732
  235.0 6.8 %copy-start.10 = (bf16[1,512,2048]{2,1,0:T(8,128)(2,1)S(1)}, bf16[1,512,2048]{2,1,0:T(8,128)(2,1)}, u32[]{:S(2)}) copy-start(bf16[1,512,2048]{2,1,0:T(8,128)(2,1)} %param.19) | copy-start | bytes 6291460
  241.8 5.3 %copy-start.16 = (f32[512,256]{1,0:T(8,128)S(1)}, f32[512,256]{1,0:T(8,128)}, u32[]{:S(2)}) copy-start(f32[512,256]{1,0:T(8,128)} %param.28) | copy-start | bytes 1572868
  241.8 5.3 %copy-start.17 = (f32[512,256]{1,0:T(8,128)S(1)}, f32[512,256]{1,0:T(8,128)}, u32[]{:S(2)}) copy-start(f32[512,256]{1,0:T(8,128)} %param.27) | copy-start | bytes 1572868
  372.1 2.7 copy-start.8
  372.1 2.7 copy-start.13
  377.5 5.0 copy-start.9
  470.8 15.2 %collective-permute-start = (f32[8,128]{1,0:T(8,128)}, f32[8,128]{1,0:T(8,128)S(1)}, u32[]{:S(2)}, u32[]{:S(2)}) collective-permute-start(f32[8,128]{1,0:T(8,128)} %get-tuple-element.133), channel_id=1, source_target_pairs={{0,4},{4,0},{8,12},{12,8},{16,20},{20,16},{24,28},{28,24},{1,5},{5... | collective-permute-start | bytes 12296 | tf_op jit(solution)/shard_map/ppermute | solution.py:954
  471.5 15.7 %collective-permute-start.2 = (bf16[32,256]{1,0:T(8,128)(2,1)S(1)}, bf16[32,256]{1,0:T(8,128)(2,1)S(1)}, u32[]{:S(2)}, u32[]{:S(2)}) collective-permute-start(bf16[32,256]{1,0:T(8,128)(2,1)S(1)} %constant_dynamic-slice_fusion), channel_id=1, source_target_pairs={{0,4},{4,0},{8,12},{12,8},{16,20},{20,16},{24,28},{28,24},{1,5},{5... | collective-permute-start | bytes 49160 | tf_op jit(solution)/shard_map/ppermute | solution.py:954
  473.7 20.3 %collective-permute-start.1 = (bf16[128,1024]{1,0:T(8,128)(2,1)}, bf16[128,1024]{1,0:T(8,128)(2,1)}, u32[]{:S(2)}, u32[]{:S(2)}) collective-permute-start(bf16[128,1024]{1,0:T(8,128)(2,1)} %constant_dynamic-slice_fusion.2), channel_id=1, source_target_pairs={{0,4},{4,0},{8,12},{12,8},{16,20},{20,16},{24,28},{28,24},{1,5},{5... | collective-permute-start | bytes 786440 | tf_op jit(solution)/shard_map/ppermute | solution.py:954
  475.6 7.0 %copy-start.5 = (f32[512,2048]{1,0:T(8,128)S(1)}, f32[512,2048]{1,0:T(8,128)}, u32[]{:S(2)}) copy-start(f32[512,2048]{1,0:T(8,128)} %get-tuple-element.285) | copy-start | bytes 12582916
  475.6 7.0 %copy-start.11 = (bf16[1,512,2048]{2,1,0:T(8,128)(2,1)S(1)}, bf16[1,512,2048]{2,1,0:T(8,128)(2,1)}, u32[]{:S(2)}) copy-start(bf16[1,512,2048]{2,1,0:T(8,128)(2,1)} %param.19) | copy-start | bytes 6291460
  475.6 21.8 %collective-permute-start.3 = (bf16[256,1024]{1,0:T(8,128)(2,1)}, bf16[256,1024]{1,0:T(8,128)(2,1)}, u32[]{:S(2)}, u32[]{:S(2)}) collective-permute-start(bf16[256,1024]{1,0:T(8,128)(2,1)} %constant_dynamic-slice_fusion.1), channel_id=1, source_target_pairs={{0,4},{4,0},{8,12},{12,8},{16,20},{20,16},{24,28},{28,24},{1,5},{5... | collective-permute-start | bytes 1572872 | tf_op jit(solution)/shard_map/ppermute | solution.py:954
  482.6 2.8 copy-start.18
  482.6 2.8 copy-start.19
  482.6 2.8 copy-start.22
  482.6 3.4 copy-start.21
  (1 other events, 0.7 us)

commit v2 on v1

--- a/solution.py
+++ b/solution.py
@@ -736,97 +736,236 @@
 
 
 HEAD_SIZE = 64
-
+TILE = 256
 norm_eps = 1e-05
 rope_base = 500000.0
+
+
+def tiles(count, body):
+    def one(i, carry):
+        body(i)
+        return carry
+
+    lax.fori_loop(0, count, one, 0)
+
+
+def span(i, size):
+    return pl.ds(pl.multiple_of(i * size, size), size)
+
+
+def swap_halves(x):
+    half, width = HEAD_SIZE // 2, x.shape[1]
+    lane = lax.rem(lax.broadcasted_iota(jnp.int32, x.shape, 1), HEAD_SIZE)
+    return jnp.where(lane < half, pltpu.roll(x, width - half, 1), pltpu.roll(x, half, 1))
+
+
+def block_kernel(
+    tok, cot, w_in, w_out, gain, cosine, sine, bias,
+    out, grad_tok, part_in, part_out, part_gain,
+    xn, xnt, inv_ref, q, dattn, attn_t, attn, dq_t, dqkv, dxn, row_acc, kx, vx, kxt, vxt, dk_acc, dv_acc,
+):
+    f32, b16 = jnp.float32, jnp.bfloat16
+    seq, width = tok.shape
+    q_width = w_out.shape[0]
+    kv_width = (w_in.shape[1] - q_width) // 2
+    kv_heads = kv_width // HEAD_SIZE
+    pair = 2 * HEAD_SIZE
+    pairs = q_width // pair
+    n_q, n_tok = q_width // TILE, seq // TILE
+    scale = 1.0 / math.sqrt(HEAD_SIZE)
+    rows = 64
+
+    def norm(i):
+        r = span(i, rows)
+        x = tok[r, :].astype(f32)
+        inv = lax.rsqrt(jnp.mean(x * x, -1, keepdims=True) + norm_eps)
+        inv_ref[r, :] = jnp.broadcast_to(inv, (rows, 128))
+        xn[r, :] = (x * inv * gain[...]).astype(b16)
+
+    tiles(seq // rows, norm)
+
+    def tables():
+        c, s = cosine[...], sine[...]
+        return jnp.concatenate([c] * (TILE // c.shape[1]), 1), jnp.concatenate([s] * (TILE // s.shape[1]), 1)
+
+    def query(i):
+        x = mm(xn[...], w_in[:, span(i, TILE)])
+        c, s = tables()
+        q[:, span(i, TILE)] = (x * c + swap_halves(x) * s).astype(b16)
+
+    tiles(n_q, query)
+    lane = lax.broadcasted_iota(jnp.int32, (seq, pair), 1)
+    low = lane < HEAD_SIZE
+
+    def split(x, into, into_t):
+        for g in range(kv_heads):
+            two = x[:, (g // 2) * pair : (g // 2 + 1) * pair].astype(f32)
+            other = pltpu.roll(two, HEAD_SIZE, 1)
+            first, second = (two, other) if g % 2 == 0 else (other, two)
+            lo, hi = jnp.where(low, first, 0.0).astype(b16), jnp.where(low, 0.0, second).astype(b16)
+            into[g, 0], into[g, 1] = lo, hi
+            into_t[g, 0], into_t[g, 1] = lo.T, hi.T
+
+    for first, into, into_t, turned in ((q_width, kx, kxt, True), (q_width + kv_width, vx, vxt, False)):
+        x = mm(xn[...], w_in[:, pl.ds(first, kv_width)])
+        if turned:
+            c, s = tables()
+            x = x * c + swap_halves(x) * s
+        split(x.astype(b16), into, into_t)
+
+    def head_grad(i):
+        dattn[:, span(i, TILE)] = nt(cot[...], w_out[span(i, TILE), :]).astype(b16)
+
+    tiles(n_q, head_grad)
+
+    per_group = pairs // kv_heads
+
+    def heads(p):
+        g = lax.div(p, per_group)
+        lanes = span(p, pair)
+
+        @pl.when(lax.rem(p, per_group) == 0)
+        def _():
+            dk_acc[...] = jnp.zeros_like(dk_acc)
+            dv_acc[...] = jnp.zeros_like(dv_acc)
+
+        for b in range(n_tok):
+            qs = slice(b * TILE, (b + 1) * TILE)
+            ks = slice(max(b - 1, 0) * TILE, (b + 1) * TILE)
+            q_b, d_b = q[qs, lanes], dattn[qs, lanes]
+            mask = bias[ks, qs]
+            a_t, dq = None, None
+            for side in range(2):
+                score = nt(kx[g, side, ks, :], q_b) * scale + mask
+                grown = jnp.exp(score)
+                prob = grown * (1.0 / jnp.sum(grown, 0, keepdims=True))
+                prob_b = prob.astype(b16)
+                dp = nt(vx[g, side, ks, :], d_b)
+                inner = jnp.sum(prob * dp, 0, keepdims=True)
+                ds = (prob * (dp - inner) * scale).astype(b16)
+                dv_acc[side, ks, :] += mm(prob_b, d_b)
+                dk_acc[side, ks, :] += mm(ds, q_b)
+                a_part = mm(vxt[g, side, :, ks], prob_b)
+                q_part = mm(kxt[g, side, :, ks], ds)
+                a_t = a_part if a_t is None else a_t + a_part
+                dq = q_part if dq is None else dq + q_part
+            attn_t[lanes, qs] = a_t.astype(b16)
+            attn[qs, lanes] = a_t.T.astype(b16)
+            turned_back = dq.T
+            c, s = cosine[qs, :], sine[qs, :]
+            dqkv[qs, lanes] = (turned_back * c - swap_halves(turned_back) * s).astype(b16)
+
+        @pl.when(lax.rem(p, per_group) == per_group - 1)
+        def _():
+            def joined(acc):
+                return acc[0] + pltpu.roll(acc[1], HEAD_SIZE, 1)
+
+            dk, dv = joined(dk_acc), joined(dv_acc)
+            dk = dk * cosine[...] - swap_halves(dk) * sine[...]
+            for x, first in ((dk, q_width), (dv, q_width + kv_width)):
+                at = span(lax.div(g, 2) + first // pair, pair)
+                odd = lax.rem(g, 2)
+
+                @pl.when(odd == 0)
+                def _():
+                    dqkv[:, at] = x.astype(b16)
+
+                @pl.when(odd == 1)
+                def _():
+                    high = pltpu.roll(x, HEAD_SIZE, 1)
+                    dqkv[:, at] = jnp.where(low, dqkv[:, at].astype(f32), high).astype(b16)
+
+    tiles(pairs, heads)
+
+    def project(i):
+        c = span(i, TILE)
+        out[:, c] = (tok[:, c].astype(f32) + mm(attn[...], w_out[:, c])).astype(b16)
+        part_out[:, c] = mm(attn_t[...], cot[:, c]).astype(b16)
+
+    tiles(width // TILE, project)
+
+    row_acc[...] = jnp.zeros_like(row_acc)
+
+    def input_grad(i):
+        c = span(i, TILE)
+        part_in[c, :] = tn(xn[:, c], dqkv[...]).astype(b16)
+        d = nt(dqkv[...], w_in[c, :])
+        normed = tok[:, c].astype(f32) * inv_ref[:, :1]
+        both = d * normed
+        part_gain[:, c] = jnp.sum(both, 0, keepdims=True)
+        d = d * gain[:, c]
+        dxn[:, c] = d
+        row_acc[...] += jnp.broadcast_to(jnp.sum(d * normed, 1, keepdims=True), row_acc.shape)
+
+    tiles(width // TILE, input_grad)
+
+    def last(i):
+        r = span(i, rows)
+        inv = inv_ref[r, :1]
+        normed = tok[r, :].astype(f32) * inv
+        mean = row_acc[r, :1] * (1.0 / width)
+        grad_tok[r, :] = (cot[r, :].astype(f32) + inv * (dxn[r, :] - normed * mean)).astype(b16)
+
+    tiles(seq // rows, last)
+
+
+def block(tok, cot, seg, w_in, w_out, gain):
+    f32, b16 = jnp.float32, jnp.bfloat16
+    seq, width = tok.shape
+    q_width = w_out.shape[0]
+    kv_width = (w_in.shape[1] - q_width) // 2
+    kv_heads = kv_width // HEAD_SIZE
+    pair = 2 * HEAD_SIZE
+    index = jnp.arange(seq, dtype=jnp.int32)
+    start = jnp.sum((seg[None, :] < seg[:, None]).astype(jnp.int32), 1)
+    position = (index - start).astype(f32)
+    half = HEAD_SIZE // 2
+    frequency = rope_base ** (-2.0 * jnp.arange(half, dtype=f32) / HEAD_SIZE)
+    angles = position[:, None] * frequency[None, :]
+    c, s = jnp.cos(angles), jnp.sin(angles)
+    cosine, sine = jnp.concatenate([c] * 4, 1), jnp.concatenate([-s, s] * 2, 1)
+    allowed = (index[:, None] <= index[None, :]) & (seg[None, :] == seg[:, None])
+    bias = jnp.where(allowed, 0.0, -1e30).astype(f32)
+    vmem = pl.BlockSpec(memory_space=pltpu.VMEM)
+    V = pltpu.VMEM
+    return pl.pallas_call(
+        block_kernel,
+        out_shape=[
+            jax.ShapeDtypeStruct((seq, width), b16),
+            jax.ShapeDtypeStruct((seq, width), b16),
+            jax.ShapeDtypeStruct(w_in.shape, b16),
+            jax.ShapeDtypeStruct(w_out.shape, b16),
+            jax.ShapeDtypeStruct((1, width), f32),
+        ],
+        in_specs=[vmem] * 8,
+        out_specs=[vmem] * 5,
+        scratch_shapes=[
+            V((seq, width), b16),
+            V((8, 128), b16),
+            V((seq, 128), f32),
+            V((seq, q_width), b16),
+            V((seq, q_width), b16),
+            V((q_width, seq), b16),
+            V((seq, q_width), b16),
+            V((8, 128), f32),
+            V((seq, q_width + 2 * kv_width), b16),
+            V((seq, width), f32),
+            V((seq, 128), f32),
+            V((kv_heads, 2, seq, pair), b16),
+            V((kv_heads, 2, seq, pair), b16),
+            V((kv_heads, 2, pair, seq), b16),
+            V((kv_heads, 2, pair, seq), b16),
+            V((2, seq, pair), f32),
+            V((2, seq, pair), f32),
+        ],
+        compiler_params=pltpu.CompilerParams(vmem_limit_bytes=63 << 20),
+        name="block",
+    )(tok, cot, w_in, w_out, gain[None], cosine, sine, bias)
+
+
 decay = 0.95
 muon_rate = 0.02
 gain_rate = 0.2
-
-
-def positions_of(seq_segments):
-    sequence_length = seq_segments.shape[0]
-    token_index = jnp.arange(sequence_length, dtype=jnp.int32)
-    before = jnp.concatenate([seq_segments[:1] - 1, seq_segments[:-1]])
-    starts = jnp.where(seq_segments != before, token_index, jnp.zeros_like(token_index))
-    return token_index - lax.cummax(starts, axis=0)
-
-
-def rope_tables(seq_segments, head_dim):
-    position = positions_of(seq_segments).astype(jnp.float32)
-    half_dim = head_dim // 2
-    frequency = rope_base ** (-2.0 * jnp.arange(half_dim, dtype=jnp.float32) / head_dim)
-    angles = position[:, None] * frequency[None, :]
-    return (jnp.cos(angles)[:, None, :], jnp.sin(angles)[:, None, :])
-
-
-def apply_rotary(values, cosine_table, sine_table):
-    half_dim = values.shape[-1] // 2
-    front_half = values[..., :half_dim]
-    back_half = values[..., half_dim:]
-    return jnp.concatenate(
-        [
-            front_half * cosine_table - back_half * sine_table,
-            back_half * cosine_table + front_half * sine_table,
-        ],
-        -1,
-    )
-
-
-def contract_rows(left, right, dtype=jnp.float32):
-    return lax.dot_general(left, right, (((0,), (0,)), ((), ())), preferred_element_type=jnp.float32).astype(dtype)
-
-
-def contract_cols(left, right):
-    return lax.dot_general(left, right, (((1,), (1,)), ((), ())), preferred_element_type=jnp.float32)
-
-
-def head_forward(q_head, k_head, v_head, allowed, score_scale):
-    scores = jnp.einsum("qgd,kd->gqk", q_head, k_head, preferred_element_type=jnp.float32) * score_scale
-    exponent = jnp.where(allowed[None], jnp.exp(scores), jnp.zeros_like(scores))
-    denom_sum = jnp.sum(exponent, -1, keepdims=True)
-    probabilities = (exponent / denom_sum).astype(jnp.bfloat16)
-    attended = jnp.einsum("gqk,kd->qgd", probabilities, v_head, preferred_element_type=jnp.float32)
-    return (attended, jnp.log(denom_sum))
-
-
-def head_backward(q_head, k_head, v_head, log_sum, grad_head, allowed, score_scale):
-    scores = jnp.einsum("qgd,kd->gqk", q_head, k_head, preferred_element_type=jnp.float32) * score_scale
-    recomputed = jnp.where(allowed[None], jnp.exp(scores - log_sum), jnp.zeros_like(scores))
-    rounded = recomputed.astype(jnp.bfloat16)
-    value_grad = jnp.einsum("gqk,qgd->kd", rounded, grad_head, preferred_element_type=jnp.float32)
-    prob_grad = jnp.einsum("qgd,kd->gqk", grad_head, v_head, preferred_element_type=jnp.float32)
-    row_inner = jnp.sum(recomputed * prob_grad, -1, keepdims=True)
-    score_grad = (recomputed * (prob_grad - row_inner) * score_scale).astype(jnp.bfloat16)
-    query_grad = jnp.einsum("gqk,kd->qgd", score_grad, k_head, preferred_element_type=jnp.float32)
-    key_grad = jnp.einsum("gqk,qgd->kd", score_grad, q_head, preferred_element_type=jnp.float32)
-    return (query_grad, key_grad, value_grad)
-
-
-def attention(query_rows, rotated_keys, values_bfloat, dattn_of, allowed, score_scale):
-    sequence_length, query_heads = query_rows.shape[:2]
-    kv_heads = rotated_keys.shape[1]
-    group_width = query_heads // kv_heads
-    query_width = query_heads * HEAD_SIZE
-    query_head_rows = query_rows.reshape(sequence_length, kv_heads, group_width, HEAD_SIZE).transpose(1, 0, 2, 3)
-    k_heads = rotated_keys.transpose(1, 0, 2)
-    v_heads = values_bfloat.transpose(1, 0, 2)
-    attended, log_sum = lax.map(
-        lambda blocks: head_forward(blocks[0], blocks[1], blocks[2], allowed, score_scale),
-        (query_head_rows, k_heads, v_heads),
-    )
-    attn_bf = attended.transpose(1, 0, 2, 3).reshape(sequence_length, query_width).astype(jnp.bfloat16)
-    head_gradients = dattn_of().reshape(sequence_length, kv_heads, group_width, HEAD_SIZE).transpose(1, 0, 2, 3)
-    query_grad, key_grad, value_grad = lax.map(
-        lambda blocks: head_backward(blocks[0], blocks[1], blocks[2], blocks[3], blocks[4], allowed, score_scale),
-        (query_head_rows, k_heads, v_heads, log_sum, head_gradients),
-    )
-    return (
-        attn_bf,
-        query_grad.transpose(1, 0, 2, 3).reshape(sequence_length, query_heads, HEAD_SIZE),
-        key_grad.transpose(1, 0, 2),
-        value_grad.transpose(1, 0, 2),
-    )
 
 
 def rows_of(matrix, index, count):
@@ -852,71 +991,18 @@
     moment_value,
     moment_outproj,
 ):
-    n_rep = lax.axis_size("rep")
-    n_shard = lax.axis_size("shard")
-    rep_index = lax.axis_index("rep")
-    shard_index = lax.axis_index("shard")
-    sequence_length = tokens.shape[1]
-    query_width = w_query.shape[1]
-    kv_width = w_key.shape[1]
-    query_heads = query_width // HEAD_SIZE
-    kv_heads = kv_width // HEAD_SIZE
-    score_scale = 1.0 / math.sqrt(HEAD_SIZE)
-    total_tokens = tokens.shape[0] * sequence_length * n_rep * n_shard
-    seq_tokens = tokens[0]
-    seq_segments = segments[0]
-    seq_cotangent = cotangent[0]
-    b16, f32 = jnp.bfloat16, jnp.float32
+    n_rep, n_shard = lax.axis_size("rep"), lax.axis_size("shard")
+    total_tokens = tokens.shape[0] * tokens.shape[1] * n_rep * n_shard
+    b16 = jnp.bfloat16
     w_in_bf = jnp.concatenate([w_query, w_key, w_value], 1).astype(b16)
-    w_out_bf = w_outproj.astype(b16)
     w_in_all, w_out_all, gain_all = gather_all(
-        [w_in_bf, w_out_bf], gain.astype(b16).astype(f32), n_rep, n_shard, 0
+        [w_in_bf, w_outproj.astype(b16)], lax.reduce_precision(gain, 8, 7), n_rep, n_shard, 0
     )
-    tok_float = seq_tokens.astype(f32)
-    inv_rms = lax.rsqrt(jnp.mean(tok_float * tok_float, -1, keepdims=True) + norm_eps)
-    normed = tok_float * inv_rms
-    norm_bf = (normed * gain_all).astype(b16)
-    projected_rows = jnp.dot(norm_bf, w_in_all, preferred_element_type=f32)
-    cosine_table, sine_table = rope_tables(seq_segments, HEAD_SIZE)
-    query_rows = apply_rotary(
-        projected_rows[:, :query_width].reshape(sequence_length, query_heads, HEAD_SIZE), cosine_table, sine_table
-    ).astype(b16)
-    rotated_keys = apply_rotary(
-        projected_rows[:, query_width : query_width + kv_width].reshape(sequence_length, kv_heads, HEAD_SIZE),
-        cosine_table,
-        sine_table,
-    ).astype(b16)
-    values_bfloat = projected_rows[:, query_width + kv_width :].reshape(sequence_length, kv_heads, HEAD_SIZE).astype(b16)
-    token_index = jnp.arange(sequence_length, dtype=jnp.int32)
-    allowed = (token_index[None, :] <= token_index[:, None]) & (seq_segments[None, :] == seq_segments[:, None])
-    attn_bf, query_grad, key_grad, value_grad = attention(
-        query_rows,
-        rotated_keys,
-        values_bfloat,
-        lambda: contract_cols(seq_cotangent, w_out_all).astype(b16),
-        allowed,
-        score_scale,
+    result, grad_tokens, part_in, part_outproj, part_gain = block(
+        tokens[0], cotangent[0], segments[0], w_in_all, w_out_all, gain_all
     )
-    branch_out = jnp.dot(attn_bf, w_out_all, preferred_element_type=f32)
-    result = (tok_float + branch_out).astype(b16)
-    part_outproj = contract_rows(attn_bf, seq_cotangent, b16)
-    grad_qkv = jnp.concatenate(
-        [
-            apply_rotary(query_grad, cosine_table, -sine_table).reshape(sequence_length, query_width),
-            apply_rotary(key_grad, cosine_table, -sine_table).reshape(sequence_length, kv_width),
-            value_grad.reshape(sequence_length, kv_width),
-        ],
-        1,
-    ).astype(b16)
-    part_in = contract_rows(norm_bf, grad_qkv, b16)
-    grad_normed = contract_cols(grad_qkv, w_in_all)
-    part_gain = jnp.sum(grad_normed * normed, 0)
-    grad_hat = grad_normed * gain_all
-    grad_tokens = (
-        seq_cotangent.astype(f32) + inv_rms * (grad_hat - normed * jnp.mean(grad_hat * normed, -1, keepdims=True))
-    ).astype(b16)
     return finish(
-        result, grad_tokens, part_in, part_outproj, part_gain, total_tokens, gain, (w_query, w_key, w_value, w_outproj),
+        result, grad_tokens, part_in, part_outproj, part_gain[0], total_tokens, gain, (w_query, w_key, w_value, w_outproj),
         moment_gain, (moment_query, moment_key, moment_value, moment_outproj),
     )
 
@@ -975,7 +1061,7 @@
     updated = []
     for i, (at, width, mix_rows, straight, mixed) in enumerate(spans):
         whole = (weights[i].shape[0] * n_shard, width)
-        ortho = straight * cols_of(moments_next[i], rep_index, widths[i]) + mixed * contract_cols(
+        ortho = straight * cols_of(moments_next[i], rep_index, widths[i]) + mixed * nt(
             own_in[:, at : at + width], mix_rows
         )
         updated.append(cols_of(weights[i], rep_index, widths[i]) - muon_rate * math.sqrt(max(whole)) * ortho)

time: 511 us -> 379 us (0.74); the launches traced: 502 us -> 378 us
  matrix products: 160 us -> 12.2 us
  Pallas kernels: 271 us -> 329 us
  local copies, waits for them, and re-layouts: 34.3 us -> 10.7 us
  other arithmetic: 32.9 us -> 24.3 us
    dot_general x37 -> x3, matrix products: 156 us -> 8.48 us  [nt(): lax.dot_general(left, right, (((1,), (1,)), ((), ())), preferred_element_...]
    pallas_call x0 -> x1, Pallas kernels: none -> 57.1 us  [block(): pl.pallas_call(block_kernel, out_shape=[jax.ShapeDtypeStruct((seq, width)...]
    while x48 -> x0, local copies, waits for them, and re-layouts: 11.9 us -> none
    slice x8 -> x0, local copies, waits for them, and re-layouts: 6.09 us -> none  [the longest x2 4.39 us: on_device(): projected_rows[:, :query_width]]
    another operation x12 -> x3, other arithmetic: 7.19 us -> 1.96 us
  transfers between devices with their start and end apart: 4 -> 4, of which waited for: 0 -> 0; matrix products, arithmetic and copies ran while one was open for 5% -> 4% of each run, Pallas kernels for 0% -> 0%
where the time goes in v2:
time: 379 us; the launch traced here: 378 us
  Pallas kernels  329 us (87%)
  other arithmetic  24.3 us (6%)
  matrix products  12.2 us (3%)
  local copies, waits for them, and re-layouts  10.7 us (3%)
    pallas_call x1, Pallas kernels, reduce_and_gather(): pl.pallas_call(functools.partial(reduce_kernel, n_rep, n_shard, decay, n_...  123 us
    pallas_call x1, Pallas kernels, muon(): pl.pallas_call(functools.partial(muon_kernel, wide), out_shape=[jax.Shape...  86.8 us
    pallas_call x1, Pallas kernels, gather_all(): pl.pallas_call(functools.partial(gather_kernel, n_rep, n_shard, n), out_s...  61.8 us
    pallas_call x1, Pallas kernels, block(): pl.pallas_call(block_kernel, out_shape=[jax.ShapeDtypeStruct((seq, width)...  57.1 us
    dot_general x3, matrix products, nt(): lax.dot_general(left, right, (((1,), (1,)), ((), ())), preferred_element_...  8.48 us
  transfers between devices with their start and end apart: 4, of which 0 were waited for; matrix products, arithmetic and copies ran while one was open for 4% of the time, Pallas kernels for 0%

profile of v2, /device:TPU:0, one launch (start us, length us, event | category | flops | bytes accessed | tf_op | source)
XLA Modules:
  0.0 378.1 jit_solution(3972722230833127703)
XLA Ops:
  0.7 1.0 convert_reduce_fusion
  1.7 0.0 copy-start.7
  1.7 1.9 fusion.1.bias
  3.6 1.9 convert.13
  5.5 0.0 copy-done.7
  5.6 0.0 copy-start.11
  5.6 0.4 copy-done
  6.0 1.1 convert_element_type.42
  7.1 0.6 reduce_precision.3
  7.7 1.0 constant_dynamic-slice_fusion.6
  8.7 0.9 constant_dynamic-slice_fusion.4
  9.6 1.7 constant_dynamic-slice_fusion.3.refs_4_
  11.2 1.0 fusion.10
  12.2 0.8 pad_maximum_fusion.1.refs_3_
  13.0 1.3 pad_maximum_fusion.2
  14.3 1.3 pad_maximum_fusion.refs_0_
  15.5 61.8 %gather_all.1 = (bf16[4,2,2,2,64,1536]{5,4,3,2,1,0:T(8,128)(2,1)}, bf16[4,2,2,2,32,2048]{5,4,3,2,1,0:T(8,128)(2,1)}, f32[4,1,512]{2,1,0:T(1,128)}) custom-call(bf16[2,2,2,64,1536]{4,3,2,1,0:T(8,128)(2,1)} %pad_maximum_fusion.refs_0_, bf16[2,2,2,32,2048]{4,3,2,1,0:T(8,128)(2,1)} %bitcast.40, f32[1,512]{1,0:T(1,128)} %bitcast.54), custom_call_target="tpu_custom_call" | custom-call | tf_op jit(solution)/shard_map/gather_all/pallas_call | solution.py:193
  77.3 57.1 %block.1 = (bf16[512,2048]{1,0:T(8,128)(2,1)}, bf16[512,2048]{1,0:T(8,128)(2,1)}, bf16[2048,1536]{1,0:T(8,128)(2,1)}, bf16[1024,2048]{1,0:T(8,128)(2,1)}, f32[1,2048]{1,0:T(1,128)}) custom-call(bf16[512,2048]{1,0:T(8,128)(2,1)} %bitcast.42, bf16[512,2048]{1,0:T(8,128)(2,1)} %bitcast.43, bf16[2048,1536]{1,0:T(8,128)(2,1)} %bitcast.34, ...), custom_call_target="tpu_custom_call" | custom-call | tf_op jit(solution)/shard_map/block/pallas_call | solution.py:931
  134.4 123.4 %reduce_and_gather.1 = (bf16[2,2,2,64,1536]{4,3,2,1,0:T(8,128)(2,1)}, bf16[2,2,2,32,2048]{4,3,2,1,0:T(8,128)(2,1)}, bf16[4,2,2,2,64,1536]{5,4,3,2,1,0:T(8,128)(2...) custom-call(bf16[4,2,2,2,64,1536]{5,4,3,2,1,0:T(8,128)(2,1)} %bitcast.36, ...), custom_call_target="tpu_custom_call" | custom-call | tf_op jit(solution)/shard_map/reduce_and_gather/pallas_call | solution.py:499
  257.8 0.0 copy-start.9
  257.8 0.0 copy-start.10
  257.8 3.9 %fusion.33 = (bf16[512,1024]{1,0:T(8,128)(2,1)S(1)}, f32[512,1024]{1,0:T(8,128)}, f32[512,1024]{1,0:T(8,128)}) fusion(f32[512,1024]{1,0:T(8,128)S(1)} %copy-done.1, bf16[512,1536]{1,0:T(8,128)(2,1)} %bitcast.44), kind=kLoop, calls=%fused_computation.58 | loop fusion | flops 2097152 | bytes 8388608 | tf_op jit(solution)/shard_map/convert_element_type | solution.py:1030
  261.8 2.7 fusion.35
  264.5 4.3 %convert_dynamic-update-slice_fusion = (bf16[1024,2048]{1,0:T(8,128)(2,1)}, f32[256,2048]{1,0:T(8,128)}, f32[256,2048]{1,0:T(8,128)}) fusion(bf16[1024,2048]{1,0:T(8,128)(2,1)} %bitcast.37, s32[]{:T(128)S(6)} %select_n.87, f32[256,2048]{1,0:T(8,128)S(1)} %copy-done.2, bf16[2,2,2,32,2048]{4,3,2,1,0:T(8,128)(2,1)} %get-tuple-element.43), kind=kLoop, calls=%fused_computation.6 | loop fusion | flops 2097152 | bytes 8388612 | tf_op jit(solution)/shard_map/dynamic_update_slice | solution.py:1033
  268.7 1.3 maximum_dynamic-update-slice_fusion.m_in
  270.0 86.8 %muon.1 = (bf16[1024,1024]{1,0:T(8,128)(2,1)}, bf16[256,256]{1,0:T(8,128)(2,1)}, f32[8,128]{1,0:T(8,128)}) custom-call(bf16[2048,1536]{1,0:T(8,128)(2,1)} %maximum_dynamic-update-slice_fusion.m_in, bf16[1024,2048]{1,0:T(8,128)(2,1)} %get-tuple-element.83.m_out), custom_call_target="tpu_custom_call" | custom-call | tf_op jit(solution)/shard_map/muon/pallas_call | solution.py:723
  356.8 1.1 constant_dynamic-slice_fusion
  358.0 0.1 collective-permute-start.3
  358.1 0.5 collective-permute-start
  358.5 0.7 constant_dynamic-slice_fusion.1
  359.3 0.1 collective-permute-start.2
  359.3 1.7 constant_dynamic-slice_fusion.2
  361.0 0.4 collective-permute-start.1
  361.5 0.6 multiply_subtract_fusion.4
  362.0 0.0 collective-permute-done
  362.0 0.7 broadcast_select_fusion
  362.7 0.6 fusion.36
  363.3 0.5 fusion.37
  363.9 0.0 collective-permute-done.2
  363.9 2.5 multiply_subtract_fusion.1
  366.4 0.7 copy.38
  367.2 2.5 multiply_subtract_fusion.2
  369.7 0.7 copy.37
  370.4 0.0 collective-permute-done.1
  370.4 3.5 multiply_subtract_fusion.3
  373.9 0.0 collective-permute-done.3
  373.9 3.7 multiply_subtract_fusion
  377.5 0.6 copy.44
  (26 shorter events, 0.1 us)
Async XLA Ops:
  1.7 3.8 %copy-start.7 = (f32[512,256]{1,0:T(8,128)S(1)}, f32[512,256]{1,0:T(8,128)}, u32[]{:S(2)}) copy-start(f32[512,256]{1,0:T(8,128)} %param.18) | copy-start | bytes 1572868
  3.6 2.0 copy-start.5
  3.6 2.4 copy-start
  5.6 1.5 copy-start.11
  134.4 123.4 %copy-start.1 = (f32[512,1024]{1,0:T(8,128)S(1)}, f32[512,1024]{1,0:T(8,128)}, u32[]{:S(2)}) copy-start(f32[512,1024]{1,0:T(8,128)} %param.22) | copy-start | bytes 6291460
  257.8 4.0 %copy-start.9 = (f32[512,256]{1,0:T(8,128)S(1)}, f32[512,256]{1,0:T(8,128)}, u32[]{:S(2)}) copy-start(f32[512,256]{1,0:T(8,128)} %param.24) | copy-start | bytes 1572868
  257.8 4.0 %copy-start.10 = (f32[512,256]{1,0:T(8,128)S(1)}, f32[512,256]{1,0:T(8,128)}, u32[]{:S(2)}) copy-start(f32[512,256]{1,0:T(8,128)} %param.23) | copy-start | bytes 1572868
  261.8 2.7 copy-start.2
  264.5 4.3 %copy-start.3 = (bf16[512,256]{1,0:T(8,128)(2,1)S(1)}, bf16[512,256]{1,0:T(8,128)(2,1)}, u32[]{:S(2)}) copy-start(bf16[512,256]{1,0:T(8,128)(2,1)} %get-tuple-element.91) | copy-start | bytes 786436
  270.0 91.4 %copy-start.12 = (f32[1,512]{1,0:T(1,128)S(1)}, f32[1,512]{1,0:T(1,128)}, u32[]{:S(2)}) copy-start(f32[1,512]{1,0:T(1,128)} %get-tuple-element.41) | copy-start | bytes 6148
  270.0 91.4 %copy-start.13 = (f32[512]{0:T(512)S(1)}, f32[512]{0:T(512)}, u32[]{:S(2)}) copy-start(f32[512]{0:T(512)} %param.21) | copy-start | bytes 6148
  270.0 93.9 %copy-start.4 = (bf16[512,256]{1,0:T(8,128)(2,1)S(1)}, bf16[512,256]{1,0:T(8,128)(2,1)}, u32[]{:S(2)}) copy-start(bf16[512,256]{1,0:T(8,128)(2,1)} %get-tuple-element.91) | copy-start | bytes 786436
  270.0 93.9 %copy-start.6 = (f32[512,256]{1,0:T(8,128)S(1)}, f32[512,256]{1,0:T(8,128)}, u32[]{:S(2)}) copy-start(f32[512,256]{1,0:T(8,128)} %param.19) | copy-start | bytes 1572868
  356.8 10.3 %copy-start.8 = (f32[512,256]{1,0:T(8,128)S(1)}, f32[512,256]{1,0:T(8,128)}, u32[]{:S(2)}) copy-start(f32[512,256]{1,0:T(8,128)} %param.18) | copy-start | bytes 1572868
  358.0 15.9 %collective-permute-start.3 = (bf16[256,1024]{1,0:T(8,128)(2,1)S(1)}, bf16[256,1024]{1,0:T(8,128)(2,1)}, u32[]{:S(2)}, u32[]{:S(2)}) collective-permute-start(bf16[256,1024]{1,0:T(8,128)(2,1)S(1)} %constant_dynamic-slice_fusion), channel_id=1, source_target_pairs={{0,4},{4,0},{8,12},{12,8},{16,20},{20,16},{24,28},{28,24},{1,5},{5... | collective-permute-start | bytes 1572872 | tf_op jit(solution)/shard_map/ppermute | solution.py:1040
  358.1 4.0 %collective-permute-start = (f32[8,128]{1,0:T(8,128)}, f32[8,128]{1,0:T(8,128)S(1)}, u32[]{:S(2)}, u32[]{:S(2)}) collective-permute-start(f32[8,128]{1,0:T(8,128)} %get-tuple-element.46), channel_id=1, source_target_pairs={{0,4},{4,0},{8,12},{12,8},{16,20},{20,16},{24,28},{28,24},{1,5},{5... | collective-permute-start | bytes 12296 | tf_op jit(solution)/shard_map/ppermute | solution.py:1040
  359.3 4.6 %collective-permute-start.2 = (bf16[32,256]{1,0:T(8,128)(2,1)S(1)}, bf16[32,256]{1,0:T(8,128)(2,1)S(1)}, u32[]{:S(2)}, u32[]{:S(2)}) collective-permute-start(bf16[32,256]{1,0:T(8,128)(2,1)S(1)} %constant_dynamic-slice_fusion.1), channel_id=1, source_target_pairs={{0,4},{4,0},{8,12},{12,8},{16,20},{20,16},{24,28},{28,24},{1,5},{5... | collective-permute-start | bytes 49160 | tf_op jit(solution)/shard_map/ppermute | solution.py:1040
  361.0 9.4 %collective-permute-start.1 = (bf16[128,1024]{1,0:T(8,128)(2,1)}, bf16[128,1024]{1,0:T(8,128)(2,1)}, u32[]{:S(2)}, u32[]{:S(2)}) collective-permute-start(bf16[128,1024]{1,0:T(8,128)(2,1)} %constant_dynamic-slice_fusion.2), channel_id=1, source_target_pairs={{0,4},{4,0},{8,12},{12,8},{16,20},{20,16},{24,28},{28,24},{1,5},{5... | collective-permute-start | bytes 786440 | tf_op jit(solution)/shard_map/ppermute | solution.py:1040

commit v3 on v2

--- a/solution.py
+++ b/solution.py
@@ -518,6 +518,8 @@
 coef_b = -4.775
 coef_c = 2.0315
 SWEEPS = 5
+decay = 0.95
+muon_rate = 0.02
 
 
 def nt(left, right):
@@ -532,8 +534,16 @@
     return jnp.dot(left, right, preferred_element_type=jnp.float32)
 
 
-def eye(n):
-    return lax.broadcasted_iota(jnp.int32, (n, n), 0) == lax.broadcasted_iota(jnp.int32, (n, n), 1)
+def tiles(count, body):
+    def one(i, carry):
+        body(i)
+        return carry
+
+    lax.fori_loop(0, count, one, 0)
+
+
+def span(i, size):
+    return pl.ds(pl.multiple_of(i * size, size), size)
 
 
 def total(x):
@@ -541,216 +551,348 @@
 
 
 class Iterate:
-    def __init__(self, e, ebf, k, kbf, h, hbf, fbf, tile, rows):
+    def __init__(self, e, ebf, k, kbf, h, hbf, fbf):
         self.e, self.ebf, self.k, self.kbf, self.h, self.hbf, self.fbf = e, ebf, k, kbf, h, hbf, fbf
         self.n = e.shape[0]
-        self.tile = min(tile, self.n)
-        self.rows = min(rows, self.n)
-
-    def blocks(self, body):
-        nr, nc = self.n // self.rows, self.n // self.tile
-
-        def one(i, carry):
-            j, r = lax.div(i, nr), lax.rem(i, nr)
-            body(pl.ds(pl.multiple_of(r * self.rows, self.rows), self.rows),
-                 pl.ds(pl.multiple_of(j * self.tile, self.tile), self.tile))
-            return carry
-
-        if nr * nc == 1:
-            one(0, 0)
-        else:
-            lax.fori_loop(0, nr * nc, one, 0)
-
-    def diagonals(self, body, init):
-        def one(i, carry):
-            d = pl.ds(pl.multiple_of(i * self.tile, self.tile), self.tile)
-            return body(d, carry)
-
-        if self.n == self.tile:
-            return one(0, init)
-        return lax.fori_loop(0, self.n // self.tile, one, init)
+        self.wide = min(512, self.n)
+        self.diag = min(256, self.n)
+        self.columns = [slice(c, c + self.wide) for c in range(0, self.n, self.wide)]
+        self.squares = [slice(d, d + self.diag) for d in range(0, self.n, self.diag)]
+
+    def eye(self):
+        shape = (self.diag, self.diag)
+        return lax.broadcasted_iota(jnp.int32, shape, 0) == lax.broadcasted_iota(jnp.int32, shape, 1)
 
     def trace(self, ref):
-        mask = eye(self.tile)
-        zero = jnp.zeros((1, 1), jnp.float32)
-        return self.diagonals(lambda d, c: c + total(jnp.where(mask, ref[d, d], 0.0)), zero)
+        mask = self.eye()
+        return sum(total(jnp.where(mask, ref[d, d], 0.0)) for d in self.squares)
 
     def centre(self, s):
         shift = self.trace(self.e) * (1.0 / self.n)
-        mask = eye(self.tile)
-
-        def one(d, c):
+        mask = self.eye()
+        for d in self.squares:
             moved = self.e[d, d] - jnp.where(mask, shift, 0.0)
             self.e[d, d] = moved
             self.ebf[d, d] = moved.astype(jnp.bfloat16)
-            return c
-
-        self.diagonals(one, 0)
         return s + shift
 
-    def start(self, gram):
-        def block(r, c):
-            self.e[r, c] = gram(r, c)
-
-        self.blocks(block)
+    def start(self):
         norm = jnp.sqrt(self.trace(self.e)) + 1e-06
         scale = 1.0 / (norm * norm)
-
-        def scaled(r, c):
-            x = self.e[r, c] * scale
-            self.e[r, c] = x
-            self.ebf[r, c] = x.astype(jnp.bfloat16)
-
-        self.blocks(scaled)
+        for c in self.columns:
+            x = self.e[:, c] * scale
+            self.e[:, c] = x
+            self.ebf[:, c] = x.astype(jnp.bfloat16)
         return self.centre(jnp.zeros((1, 1), jnp.float32)), 1.0 / norm
 
-    def polynomial(self, s):
-        p0 = coef_a + s * (coef_b + coef_c * s)
+    def polynomial(self, s, c):
         p1 = coef_b + 2.0 * coef_c * s
-
-        def block(r, c):
-            f = p1 * self.e[r, c] + coef_c * mm(self.ebf[r, :], self.ebf[:, c])
-            self.fbf[r, c] = f.astype(jnp.bfloat16)
-
-        self.blocks(block)
-        return p0
+        f = p1 * self.e[:, c] + coef_c * mm(self.ebf[...], self.ebf[:, c])
+        self.fbf[:, c] = f.astype(jnp.bfloat16)
 
     def first(self):
-        def block(r, c):
-            f = self.fbf[r, c]
-            self.h[r, c] = f.astype(jnp.float32)
-            self.hbf[r, c] = f
-
-        self.blocks(block)
-
-    def grow(self, p0, q):
-        def block(r, c):
-            new = p0 * self.h[r, c] + q * self.fbf[r, c].astype(jnp.float32) + mm(self.fbf[r, :], self.hbf[:, c])
-            self.k[r, c] = new
-
-        self.blocks(block)
-
-        def back(r, c):
-            new = self.k[r, c]
-            self.h[r, c] = new
-            self.hbf[r, c] = new.astype(jnp.bfloat16)
-
-        self.blocks(back)
-
-    def advance(self, p0, s):
-        def inner(r, c):
-            new = p0 * self.e[r, c] + s * self.fbf[r, c].astype(jnp.float32) + mm(self.fbf[r, :], self.ebf[:, c])
-            self.k[r, c] = new
-            self.kbf[r, c] = new.astype(jnp.bfloat16)
-
-        self.blocks(inner)
-        beta = p0 * s
-
-        def outer(r, c):
-            new = p0 * self.k[r, c] + beta * self.fbf[r, c].astype(jnp.float32) + mm(self.fbf[r, :], self.kbf[:, c])
-            self.e[r, c] = new
-            self.ebf[r, c] = new.astype(jnp.bfloat16)
-
-        self.blocks(outer)
-        return self.centre(p0 * beta)
-
-
-def muon_kernel(wide, m_in, m_out, h_out, hs_out, scal, x, *scratch):
-    big = Iterate(*scratch[:7], tile=256, rows=512)
-    small = Iterate(*scratch[7:], tile=256, rows=256)
+        for c in self.columns:
+            f = self.fbf[:, c]
+            self.h[:, c] = f.astype(jnp.float32)
+            self.hbf[0, :, c] = f
+
+    def grow(self, p0, q, c, now, later):
+        new = p0 * self.h[:, c] + q * self.fbf[:, c].astype(jnp.float32) + mm(self.fbf[...], self.hbf[now, :, c])
+        self.h[:, c] = new
+        self.hbf[later, :, c] = new.astype(jnp.bfloat16)
+
+    def inner(self, p0, s, c):
+        new = p0 * self.e[:, c] + s * self.fbf[:, c].astype(jnp.float32) + mm(self.fbf[...], self.ebf[:, c])
+        self.k[:, c] = new
+        self.kbf[:, c] = new.astype(jnp.bfloat16)
+
+    def outer(self, p0, beta, c):
+        new = p0 * self.k[:, c] + beta * self.fbf[:, c].astype(jnp.float32) + mm(self.fbf[...], self.kbf[:, c])
+        self.e[:, c] = new
+        self.ebf[:, c] = new.astype(jnp.bfloat16)
+
+
+def muon_kernel(*refs):
+    m_in, m_out = refs[:2]
+    g_in, g_out, moments = refs[2], refs[3], refs[4:8]
+    grads_out, moments_out = refs[8:12], refs[12:16]
+    h_out, hs_out, scal = refs[16:19]
+    grads, news = refs[19:23], refs[23:27]
+    tall, x, small_m, in_sem, out_sem = refs[27:32]
+    big, small = Iterate(*refs[32:39]), Iterate(*refs[39:46])
+    f32, b16 = jnp.float32, jnp.bfloat16
     core = lax.rem(lax.axis_index("rep"), 2)
+    shard = lax.axis_index("shard")
     n, ns = big.n, small.n
+    own_in, own_out = g_in.shape[0], g_out.shape[0]
+    columns = [(0, n), (n, ns), (n + ns, ns)]
+
+    wide = pltpu.make_async_copy(m_in.at[:, pl.ds(0, n)], tall, in_sem.at[0])
+    flat = pltpu.make_async_copy(m_out, x, in_sem.at[0])
+    kv = pltpu.make_async_copy(m_in.at[:, pl.ds(pl.multiple_of(n + core * ns, 128), ns)], small_m, in_sem.at[1])
 
     @pl.when(core == 0)
     def _():
-        def turn(i, c):
-            r = pl.ds(pl.multiple_of(i * 256, 256), 256)
-            x[:, r] = m_in[r, pl.ds(0, n)].T
-            return c
-
-        lax.fori_loop(0, wide // 256, turn, 0)
+        wide.start()
 
     @pl.when(core != 0)
     def _():
-        def take(i, c):
-            r = pl.ds(pl.multiple_of(i * 128, 128), 128)
-            x[r, :] = m_out[r, :]
-            return c
-
-        lax.fori_loop(0, n // 128, take, 0)
-
-    s, inv = big.start(lambda r, c: nt(x[r, :], x[c, :]))
-    mine = m_in.at[:, pl.ds(pl.multiple_of(n + core * ns, 128), ns)]
-    ss, sinv = small.start(lambda r, c: tn(mine[:, r], mine[:, c]))
+        flat.start()
+
+    kv.start()
+
+    rows = 64
+    copies = []
+    for i in range(4):
+        g, (at, width) = (g_in, columns[i]) if i < 3 else (g_out, (0, g_out.shape[1]))
+
+        def update(j, i=i, g=g, at=at, width=width):
+            r = span(j, rows)
+            grad = g[r, at : at + width].astype(f32)
+            grads[i][r, :] = grad
+            news[i][r, :] = decay * moments[i][r, :] + grad
+
+        tiles(g.shape[0] // rows, update)
+        copies.append(pltpu.make_async_copy(grads[i], grads_out[i], out_sem.at[2 * i]))
+        copies.append(pltpu.make_async_copy(news[i], moments_out[i], out_sem.at[2 * i + 1]))
+        copies[-2].start()
+        copies[-1].start()
+    kv.wait()
+    mine = span(shard, own_in)
+
+    @pl.when(core == 0)
+    def _():
+        wide.wait()
+        tall[mine, :] = news[0][...].astype(b16)
+        small_m[mine, :] = news[1][...].astype(b16)
+        tiles(tall.shape[0] // 256, lambda i: x.__setitem__((slice(None), span(i, 256)), tall[span(i, 256), :].T))
+
+    @pl.when(core != 0)
+    def _():
+        flat.wait()
+        x[span(shard, own_out), :] = news[3][...].astype(b16)
+        small_m[mine, :] = news[2][...].astype(b16)
+
+    tiles(n // big.wide, lambda j: big.e.__setitem__((slice(None), span(j, big.wide)), nt(x[...], x[span(j, big.wide), :])))
+    small.e[...] = tn(small_m[...], small_m[...])
+    s, inv = big.start()
+    ss, sinv = small.start()
 
     def sweep(it, carry):
         s, q, ss, sq = carry
-        p0, sp0 = big.polynomial(s), small.polynomial(ss)
+        now, later = lax.rem(it + 1, 2), lax.rem(it, 2)
+        p0 = coef_a + s * (coef_b + coef_c * s)
+        sp0 = coef_a + ss * (coef_b + coef_c * ss)
+
+        def each(method, *args):
+            for i, c in enumerate(big.columns):
+                getattr(big, method)(*[a[0] for a in args], c, *extra)
+                if i == 0:
+                    for d in small.columns:
+                        getattr(small, method)(*[a[1] for a in args], d, *extra)
+
+        extra = ()
+        each("polynomial", (s, ss))
 
         @pl.when(it == 0)
         def _():
             big.first()
             small.first()
 
+        extra = (now, later)
+
         @pl.when(it > 0)
         def _():
-            big.grow(p0, q)
-            small.grow(sp0, sq)
-
+            each("grow", (p0, sp0), (q, sq))
+
+        extra = ()
         q, sq = p0 * q, sp0 * sq
-        s, ss = lax.cond(
-            it < SWEEPS - 1,
-            lambda: (big.advance(p0, s), small.advance(sp0, ss)),
-            lambda: (s, ss),
-        )
+
+        def advance():
+            each("inner", (p0, sp0), (s, ss))
+            beta, sbeta = p0 * s, sp0 * ss
+            each("outer", (p0, sp0), (beta, sbeta))
+            return big.centre(p0 * beta), small.centre(sp0 * sbeta)
+
+        s, ss = lax.cond(it < SWEEPS - 1, advance, lambda: (s, ss))
         return s, q, ss, sq
 
-    one = jnp.ones((1, 1), jnp.float32)
+    one = jnp.ones((1, 1), f32)
     s, q, ss, sq = lax.fori_loop(0, SWEEPS, sweep, (s, one, ss, one))
-    h_out[...] = big.hbf[...]
-    hs_out[...] = small.hbf[...]
+    last = (SWEEPS - 1) % 2
+    h_out[...] = big.hbf[last]
+    hs_out[...] = small.hbf[last]
     row = lax.broadcasted_iota(jnp.int32, (8, 128), 0)
     scal[...] = jnp.where(row == 0, q * inv, jnp.where(row == 1, inv, jnp.where(row == 2, sq * sinv, sinv)))
-
-
-def muon(m_in, m_out, kv):
-    wide, n = m_in.shape[0], m_out.shape[0]
+    for copy in copies:
+        copy.wait()
+
+
+def muon(m_in, m_out, g_in, g_out, moments):
+    f32, b16 = jnp.float32, jnp.bfloat16
+    tall, n, kv = m_in.shape[0], m_out.shape[0], moments[1].shape[1]
+    V = pltpu.VMEM
     sets = []
     for d in (n, kv):
-        f32, b16 = pltpu.VMEM((d, d), jnp.float32), pltpu.VMEM((d, d), jnp.bfloat16)
-        sets += [f32, b16, f32, b16, f32, b16, b16]
-    vmem = pl.BlockSpec(memory_space=pltpu.VMEM)
+        sets += [V((d, d), f32), V((d, d), b16), V((d, d), f32), V((d, d), b16), V((d, d), f32), V((2, d, d), b16), V((d, d), b16)]
+    vmem, any_ = pl.BlockSpec(memory_space=pltpu.VMEM), pl.BlockSpec(memory_space=pl.ANY)
+    own = [jax.ShapeDtypeStruct(m.shape, f32) for m in moments]
+    out = pl.pallas_call(
+        muon_kernel,
+        out_shape=own
+        + own
+        + [
+            jax.ShapeDtypeStruct((n, n), b16),
+            jax.ShapeDtypeStruct((kv, kv), b16),
+            jax.ShapeDtypeStruct((8, 128), f32),
+        ],
+        in_specs=[any_] * 2 + [vmem] * 6,
+        out_specs=[any_] * 8 + [vmem] * 3,
+        scratch_shapes=[V(m.shape, f32) for m in moments] * 2
+        + [
+            V((tall, n), b16),
+            V(m_out.shape, b16),
+            V((tall, kv), b16),
+            pltpu.SemaphoreType.DMA((2,)),
+            pltpu.SemaphoreType.DMA((8,)),
+        ]
+        + sets,
+        compiler_params=pltpu.CompilerParams(vmem_limit_bytes=63 << 20),
+        name="muon",
+    )(m_in, m_out, g_in, g_out, *moments)
+    return out[:4], out[4:8], out[8:]
+
+
+def swap_kernel(n_rep, h, hs, scal, h_pair, hs_come, scal_come, send, recv):
+    rep, shard = lax.axis_index("rep"), lax.axis_index("shard")
+    core = lax.rem(rep, 2)
+    other = rep + 1 - 2 * core
+    sem = pltpu.get_barrier_semaphore()
+    pl.semaphore_signal(sem, 1, device_id=(other, shard), device_id_type=pl.DeviceIdType.MESH)
+    pl.semaphore_wait(sem, 1)
+
+    def remote(src, dst, i):
+        return pltpu.make_async_remote_copy(
+            src, dst, send.at[i], recv.at[i], device_id=(other, shard), device_id_type=pl.DeviceIdType.MESH
+        )
+
+    count = h_pair.shape[0]
+    at = jnp.where(core == 0, lax.div(rep, 2), shard)
+    copies = [remote(h.at[span(at, count), :], h_pair, 0), remote(hs, hs_come, 1), remote(scal, scal_come, 2)]
+    for c in copies:
+        c.start()
+    for c in copies:
+        c.wait()
+
+
+def swap(h, hs, scal, count, n_rep, collective_id):
+    any_ = pl.BlockSpec(memory_space=pl.ANY)
     return pl.pallas_call(
-        functools.partial(muon_kernel, wide),
+        functools.partial(swap_kernel, n_rep),
         out_shape=[
-            jax.ShapeDtypeStruct((n, n), jnp.bfloat16),
-            jax.ShapeDtypeStruct((kv, kv), jnp.bfloat16),
-            jax.ShapeDtypeStruct((8, 128), jnp.float32),
+            jax.ShapeDtypeStruct((count, h.shape[1]), h.dtype),
+            jax.ShapeDtypeStruct(hs.shape, hs.dtype),
+            jax.ShapeDtypeStruct(scal.shape, scal.dtype),
         ],
-        in_specs=[vmem] * 2,
-        out_specs=[vmem] * 3,
-        scratch_shapes=[pltpu.VMEM((n, wide), jnp.bfloat16)] + sets,
-        compiler_params=pltpu.CompilerParams(vmem_limit_bytes=60 << 20),
-        name="muon",
-    )(m_in, m_out)
+        in_specs=[any_] * 3,
+        out_specs=[any_] * 3,
+        scratch_shapes=[pltpu.SemaphoreType.DMA((3,)), pltpu.SemaphoreType.DMA((3,))],
+        compiler_params=pltpu.CompilerParams(collective_id=collective_id, has_side_effects=True),
+        name="swap",
+    )(h, hs, scal)
+
+
+def window(index, width):
+    size = max(width, 128)
+    start = lax.div(index * width, size) * size
+    return pl.ds(pl.multiple_of(start, 128), size), size, index * width - start
+
+
+def cut(x, size, offset, width):
+    return x if size == width else pltpu.roll(x, lax.rem(size - offset, size), 1)[:, :width]
+
+
+def update_kernel(h, h_pair, hs, hs_come, scal, scal_come, m_out, mq, mk, mv, mo, wq, wk, wv, wo, *refs):
+    nexts, (hq, ho, flat, mo_win), weight_wins, (h_sem, sem) = refs[:4], refs[4:8], refs[8:12], refs[12:]
+    f32, b16 = jnp.float32, jnp.bfloat16
+    rep, shard = lax.axis_index("rep"), lax.axis_index("shard")
+    even = lax.rem(rep, 2) == 0
+    widths = [o.shape[1] for o in nexts]
+    wins = [window(rep, w) for w in widths]
+    own_out = ho.shape[0]
+    copies = [
+        pltpu.make_async_copy(m_out.at[:, wins[3][0]], flat, sem.at[4]),
+        pltpu.make_async_copy(mo.at[:, wins[3][0]], mo_win, sem.at[5]),
+    ] + [pltpu.make_async_copy(w.at[:, wins[i][0]], weight_wins[i], sem.at[i]) for i, w in enumerate((wq, wk, wv, wo))]
+    for copy in copies:
+        copy.start()
+    rows_q = h.at[span(rep, widths[0]), :], h_pair.at[pl.ds(h_pair.shape[0] - widths[0], widths[0]), :]
+    rows_o = h_pair, h.at[span(shard, own_out), :]
+    mixes = [[pltpu.make_async_copy(a, b, h_sem.at[i]) for i, (a, b) in enumerate(((q, hq), (o, ho)))] for q, o in zip(rows_q, rows_o)]
+    for side, here in ((0, even), (1, jnp.logical_not(even))):
+        @pl.when(here)
+        def _():
+            for copy in mixes[side]:
+                copy.start()
+            for copy in mixes[side]:
+                copy.wait()
+    for copy in copies:
+        copy.wait()
+    first = jnp.where(even, scal[...], scal_come[...])
+    second = jnp.where(even, scal_come[...], scal[...])
+    flat[span(shard, own_out), :] = mo_win[...].astype(b16)
+
+    def rows_of(i):
+        at = span(rep, widths[i])
+        mine, theirs = hs[at, :].astype(f32), hs_come[at, :].astype(f32)
+        return jnp.where(even == (i == 1), mine, theirs).astype(b16)
+
+    parts = (
+        (mq, lambda: nt(mq[...].astype(b16), hq[...]), first[0:1, 0:1], first[1:2, 0:1]),
+        (mk, lambda: nt(mk[...].astype(b16), rows_of(1)), first[2:3, 0:1], first[3:4, 0:1]),
+        (mv, lambda: nt(mv[...].astype(b16), rows_of(2)), second[2:3, 0:1], second[3:4, 0:1]),
+        (None, lambda: mm(ho[...], flat[...]), second[0:1, 0:1], second[1:2, 0:1]),
+    )
+    n_shard = lax.axis_size("shard")
+    for i, (moment, product, straight, mixed) in enumerate(parts):
+        at, size, offset = wins[i]
+        here = mo_win[...] if moment is None else cut(moment[:, at], size, offset, widths[i])
+        ortho = straight * here + mixed * product()
+        whole = (weight_wins[i].shape[0] * n_shard, (wq, wk, wv, wo)[i].shape[1])
+        weight = cut(weight_wins[i][...], size, offset, widths[i])
+        nexts[i][...] = weight - muon_rate * math.sqrt(max(whole)) * ortho
+
+
+def update(h, hs, scal, m_out, moments, weights, n_rep, collective_id):
+    f32, b16 = jnp.float32, jnp.bfloat16
+    widths = [w.shape[1] // n_rep for w in weights]
+    own_out = weights[3].shape[0]
+    assert 2 * widths[0] == own_out
+    h_pair, hs_come, scal_come = swap(h, hs, scal, own_out, n_rep, collective_id)
+    vmem, any_ = pl.BlockSpec(memory_space=pltpu.VMEM), pl.BlockSpec(memory_space=pl.ANY)
+    V = pltpu.VMEM
+    sizes = [max(w, 128) for w in widths]
+    return pl.pallas_call(
+        update_kernel,
+        out_shape=[jax.ShapeDtypeStruct((w.shape[0], width), f32) for w, width in zip(weights, widths)],
+        in_specs=[any_] * 2 + [vmem] * 4 + [any_] + [vmem] * 3 + [any_] * 5,
+        out_specs=[vmem] * 4,
+        scratch_shapes=[
+            V((widths[0], h.shape[1]), b16),
+            V((own_out, h.shape[1]), b16),
+            V((m_out.shape[0], sizes[3]), b16),
+            V((own_out, sizes[3]), f32),
+        ]
+        + [V((w.shape[0], size), f32) for w, size in zip(weights, sizes)]
+        + [pltpu.SemaphoreType.DMA((2,)), pltpu.SemaphoreType.DMA((6,))],
+        name="update",
+    )(h, h_pair, hs, hs_come, scal, scal_come, m_out, *moments, *weights)
 
 
 HEAD_SIZE = 64
 TILE = 256
 norm_eps = 1e-05
 rope_base = 500000.0
-
-
-def tiles(count, body):
-    def one(i, carry):
-        body(i)
-        return carry
-
-    lax.fori_loop(0, count, one, 0)
-
-
-def span(i, size):
-    return pl.ds(pl.multiple_of(i * size, size), size)
 
 
 def swap_halves(x):
@@ -963,8 +1105,6 @@
     )(tok, cot, w_in, w_out, gain[None], cosine, sine, bias)
 
 
-decay = 0.95
-muon_rate = 0.02
 gain_rate = 0.2
 
 
@@ -1009,67 +1149,16 @@
 
 def finish(result, grad_tokens, part_in, part_outproj, part_gain, total_tokens, gain, weights, moment_gain, moments):
     n_rep, n_shard = lax.axis_size("rep"), lax.axis_size("shard")
-    rep_index, shard_index = lax.axis_index("rep"), lax.axis_index("shard")
-    b16, f32 = jnp.bfloat16, jnp.float32
-    w_query, w_key, w_value, w_outproj = weights
-    query_width, kv_width = w_query.shape[1], w_key.shape[1]
+    rep_index = lax.axis_index("rep")
     in_piece = jnp.concatenate([rows_of(m, rep_index, m.shape[0] // n_rep) for m in moments[:3]], 1)
     out_piece = rows_of(moments[3], rep_index, moments[3].shape[0] // n_rep)
     (sum_in, sum_out), (m_in, m_out), grad_gain = reduce_and_gather(
         [part_in, part_outproj], part_gain, [in_piece, out_piece], decay, n_rep, n_shard, 1
     )
-    grads = [
-        sum_in[:, :query_width].astype(f32),
-        sum_in[:, query_width : query_width + kv_width].astype(f32),
-        sum_in[:, query_width + kv_width :].astype(f32),
-        sum_out.astype(f32),
-    ]
-    moments_next = [decay * m + g for m, g in zip(moments, grads)]
     moment_gain_next = decay * moment_gain + grad_gain
     gain_next = gain - gain_rate / math.sqrt(total_tokens) * moment_gain_next
-    own_in = jnp.concatenate([m.astype(b16) for m in moments_next[:3]], 1)
-    own_out = moments_next[3].astype(b16)
-    m_in = lax.dynamic_update_slice_in_dim(m_in, own_in, shard_index * own_in.shape[0], 0)
-    m_out = lax.dynamic_update_slice_in_dim(m_out, own_out, shard_index * own_out.shape[0], 0)
-    mix, mix_kv, scales = muon(m_in, m_out, kv_width)
-    core = lax.rem(rep_index, 2)
-    other = rep_index + 1 - 2 * core
-    widths = [w.shape[1] // n_rep for w in weights]
-    pairs = [(i, i ^ 1) for i in range(n_rep)]
-    out_rows = w_outproj.shape[0]
-    theirs = lax.ppermute(
-        (
-            rows_of(mix, other, widths[0]),
-            rows_of(mix, shard_index, out_rows),
-            rows_of(mix_kv, other, widths[1]),
-            scales,
-        ),
-        "rep",
-        pairs,
-    )
-    even = core == 0
-    mix_query = jnp.where(even, rows_of(mix, rep_index, widths[0]), theirs[0])
-    mix_out = jnp.where(even, theirs[1], rows_of(mix, shard_index, out_rows))
-    kv_mine = rows_of(mix_kv, rep_index, widths[1])
-    mix_key, mix_value = jnp.where(even, kv_mine, theirs[2]), jnp.where(even, theirs[2], kv_mine)
-    first, second = jnp.where(even, scales, theirs[3]), jnp.where(even, theirs[3], scales)
-    spans = (
-        (0, query_width, mix_query, first[0, 0], first[1, 0]),
-        (query_width, kv_width, mix_key, first[2, 0], first[3, 0]),
-        (query_width + kv_width, kv_width, mix_value, second[2, 0], second[3, 0]),
-    )
-    updated = []
-    for i, (at, width, mix_rows, straight, mixed) in enumerate(spans):
-        whole = (weights[i].shape[0] * n_shard, width)
-        ortho = straight * cols_of(moments_next[i], rep_index, widths[i]) + mixed * nt(
-            own_in[:, at : at + width], mix_rows
-        )
-        updated.append(cols_of(weights[i], rep_index, widths[i]) - muon_rate * math.sqrt(max(whole)) * ortho)
-    whole = (out_rows * n_shard, w_outproj.shape[1])
-    ortho = second[0, 0] * cols_of(moments_next[3], rep_index, widths[3]) + second[1, 0] * jnp.dot(
-        mix_out, cols_of(m_out, rep_index, widths[3]), preferred_element_type=f32
-    )
-    updated.append(cols_of(w_outproj, rep_index, widths[3]) - muon_rate * math.sqrt(max(whole)) * ortho)
+    grads, moments_next, (mix, mix_kv, scales) = muon(m_in, m_out, sum_in, sum_out, moments)
+    updated = update(mix, mix_kv, scales, m_out, moments_next, weights, n_rep, 2)
     return (
         result[None],
         grad_tokens[None],

time: 379 us -> 330 us (0.87)
  Pallas kernels: 329 us -> 311 us
  other arithmetic: 24.3 us -> 8.96 us
  matrix products: 12.2 us -> 0 us
    pallas_call x1 -> x3, Pallas kernels: 86.8 us -> 70.2 us  [the longest x1 62.4 us: muon(): pl.pallas_call(muon_kernel, out_shape=own + own + [jax.ShapeDtypeStruct((...]
    dot_general x4 -> x0, matrix products: 12.2 us -> none  [the longest x3 8.48 us: nt(): lax.dot_general(left, right, (((1,), (1,)), ((), ())), preferred_element_...]
    convert_element_type x2 -> x0, other arithmetic: 6.63 us -> none  [finish(): own_in = jnp.concatenate([m.astype(b16) for m in moments_next[:3]], 1)]
    dynamic_update_slice x2 -> x0, other arithmetic: 5.53 us -> none  [the longest x1 4.27 us: finish(): lax.dynamic_update_slice_in_dim(m_out, own_out, shard_index * own_out.sha...]
  transfers between devices with their start and end apart: 4 -> 0, of which waited for: 0 -> 0; matrix products, arithmetic and copies ran while one was open for 4% -> 0% of each run, Pallas kernels for 0% -> 0%
where the time goes in v3:
time: 330 us
  Pallas kernels  311 us (94%)
  other arithmetic  8.96 us (3%)
  local copies, waits for them, and re-layouts  8.49 us (3%)
    pallas_call x1, Pallas kernels, reduce_and_gather(): pl.pallas_call(functools.partial(reduce_kernel, n_rep, n_shard, decay, n_...  122 us
    pallas_call x1, Pallas kernels, muon(): pl.pallas_call(muon_kernel, out_shape=own + own + [jax.ShapeDtypeStruct((...  62.4 us
    pallas_call x1, Pallas kernels, gather_all(): pl.pallas_call(functools.partial(gather_kernel, n_rep, n_shard, n), out_s...  61.8 us
    pallas_call x1, Pallas kernels, block(): pl.pallas_call(block_kernel, out_shape=[jax.ShapeDtypeStruct((seq, width)...  57.1 us

profile of v3, /device:TPU:0, one launch (start us, length us, event | category | flops | bytes accessed | tf_op | source)
XLA Modules:
  0.0 329.7 jit_solution(16272744754745189746)
XLA Ops:
  0.7 0.0 copy-start
  0.7 1.0 constant_dynamic-slice_fusion.1
  1.7 1.0 constant_dynamic-slice_fusion.3
  2.7 0.8 pad_maximum_fusion.1.refs_3_
  3.5 1.0 convert_reduce_fusion
  4.5 1.0 fusion.2
  5.5 0.0 copy-start.3
  5.5 1.3 pad_maximum_fusion.2
  6.8 0.0 copy-start.2
  6.8 0.0 copy-done
  6.8 0.2 convert.12
  6.9 0.0 copy-done.3
  7.0 0.0 copy-start.1
  7.0 0.8 copy-done.2
  7.8 1.3 pad_maximum_fusion.refs_0_
  9.1 0.0 copy-done.1
  9.1 0.0 copy-start.5
  9.1 1.1 convert_element_type.15
  10.2 0.0 copy-start.4
  10.2 0.0 copy-done.5
  10.2 0.6 reduce_precision.3
  10.8 61.8 %gather_all.1 = (bf16[4,2,2,2,64,1536]{5,4,3,2,1,0:T(8,128)(2,1)}, bf16[4,2,2,2,32,2048]{5,4,3,2,1,0:T(8,128)(2,1)}, f32[4,1,512]{2,1,0:T(1,128)}) custom-call(bf16[2,2,2,64,1536]{4,3,2,1,0:T(8,128)(2,1)} %pad_maximum_fusion.refs_0_, bf16[2,2,2,32,2048]{4,3,2,1,0:T(8,128)(2,1)} %bitcast.28, f32[1,512]{1,0:T(1,128)} %bitcast.42), custom_call_target="tpu_custom_call" | custom-call | tf_op jit(solution)/shard_map/gather_all/pallas_call | solution.py:193
  72.6 0.0 copy-done.4
  72.6 1.2 fusion.1.bias
  73.8 57.1 %block.1 = (bf16[512,2048]{1,0:T(8,128)(2,1)}, bf16[512,2048]{1,0:T(8,128)(2,1)}, bf16[2048,1536]{1,0:T(8,128)(2,1)}, bf16[1024,2048]{1,0:T(8,128)(2,1)}, f32[1,2048]{1,0:T(1,128)}) custom-call(bf16[512,2048]{1,0:T(8,128)(2,1)} %bitcast.30, bf16[512,2048]{1,0:T(8,128)(2,1)} %bitcast.31, bf16[2048,1536]{1,0:T(8,128)(2,1)} %bitcast.23, ...), custom_call_target="tpu_custom_call" | custom-call | tf_op jit(solution)/shard_map/block/pallas_call | solution.py:1073
  130.8 1.7 constant_dynamic-slice_fusion.refs_4_
  132.5 122.4 %reduce_and_gather.1 = (bf16[2,2,2,64,1536]{4,3,2,1,0:T(8,128)(2,1)}, bf16[2,2,2,32,2048]{4,3,2,1,0:T(8,128)(2,1)}, bf16[4,2,2,2,64,1536]{5,4,3,2,1,0:T(8,128)(2...) custom-call(bf16[4,2,2,2,64,1536]{5,4,3,2,1,0:T(8,128)(2,1)} %bitcast.24, ...), custom_call_target="tpu_custom_call" | custom-call | tf_op jit(solution)/shard_map/reduce_and_gather/pallas_call | solution.py:499
  254.9 62.4 %muon.1 = (f32[512,1024]{1,0:T(8,128)}, f32[512,256]{1,0:T(8,128)}, f32[512,256]{1,0:T(8,128)}, f32[256,2048]{1,0:T(8,128)}, f32[512,1024]{1,0:T(8,128)}, /*inde...) custom-call(bf16[2048,1536]{1,0:T(8,128)(2,1)} %bitcast.25, ...), custom_call_target="tpu_custom_call" | custom-call | tf_op jit(solution)/shard_map/muon/pallas_call | solution.py:740
  317.3 2.5 swap.1
  319.9 0.0 copy-start.6
  319.9 0.0 copy-start.7
  319.9 5.3 %update.1 = (f32[512,128]{1,0:T(8,128)}, f32[512,32]{1,0:T(8,128)}, f32[512,32]{1,0:T(8,128)}, f32[256,256]{1,0:T(8,128)}) custom-call(bf16[1024,1024]{1,0:T(8,128)(2,1)} %get-tuple-element.65.h, bf16[256,1024]{1,0:T(8,128)(2,1)} %get-tuple-element.68.h_pair, bf16[256,256]{1,0:T(8,128)(2,1)} %get-tuple-element.66.hs, ...), custom_call_target="tpu_custom_call" | custom-call | tf_op jit(solution)/shard_map/update/pallas_call | solution.py:875
  325.2 1.7 copy.33
  326.9 1.7 copy.34
  328.6 0.0 copy-done.6
  328.6 0.0 copy-done.7
  328.6 0.6 multiply_subtract_fusion
  329.2 0.6 copy.36
  (4 shorter events, 0.1 us)
Async XLA Ops:
  0.7 6.1 %copy-start = (f32[512,1024]{1,0:T(8,128)S(1)}, f32[512,1024]{1,0:T(8,128)}, u32[]{:S(2)}) copy-start(f32[512,1024]{1,0:T(8,128)} %wq.1) | copy-start | bytes 6291460
  5.5 1.4 copy-start.3
  6.8 1.0 copy-start.2
  7.0 2.1 copy-start.1
  9.1 1.1 copy-start.5
  10.2 62.4 %copy-start.4 = (s32[1,512]{1,0:T(1,128)S(1)}, s32[1,512]{1,0:T(1,128)}, u32[]{:S(2)}) copy-start(s32[1,512]{1,0:T(1,128)} %param.14) | copy-start | bytes 6148
  319.9 8.7 %copy-start.6 = (f32[1,512]{1,0:T(1,128)S(1)}, f32[1,512]{1,0:T(1,128)}, u32[]{:S(2)}) copy-start(f32[1,512]{1,0:T(1,128)} %get-tuple-element.56) | copy-start | bytes 6148
  319.9 8.7 %copy-start.7 = (f32[512]{0:T(512)S(1)}, f32[512]{0:T(512)}, u32[]{:S(2)}) copy-start(f32[512]{0:T(512)} %param.21) | copy-start | bytes 6148

commit v4 on v3

v4 whole, which is shorter than its diff:
```python
import functools
import math

import jax
import jax.numpy as jnp
from jax import lax
from jax.experimental import pallas as pl
from jax.experimental.pallas import tpu as pltpu
from jax.sharding import PartitionSpec as P

coef_a = 3.4445
coef_b = -4.775
coef_c = 2.0315
SWEEPS = 5
decay = 0.95
muon_rate = 0.02


def nt(left, right):
    return lax.dot_general(left, right, (((1,), (1,)), ((), ())), preferred_element_type=jnp.float32)


def tn(left, right):
    return lax.dot_general(left, right, (((0,), (0,)), ((), ())), preferred_element_type=jnp.float32)


def mm(left, right):
    return jnp.dot(left, right, preferred_element_type=jnp.float32)


def tiles(count, body):
    def one(i, carry):
        body(i)
        return carry

    lax.fori_loop(0, count, one, 0)


def span(i, size):
    return pl.ds(pl.multiple_of(i * size, size), size)


def total(x):
    return jnp.sum(jnp.sum(x, axis=1, keepdims=True), axis=0, keepdims=True)


class Iterate:
    def __init__(self, e, ebf, k, kbf, h, hbf, fbf):
        self.e, self.ebf, self.k, self.kbf, self.h, self.hbf, self.fbf = e, ebf, k, kbf, h, hbf, fbf
        self.n = e.shape[0]
        self.wide = min(512, self.n)
        self.diag = min(256, self.n)
        self.columns = [slice(c, c + self.wide) for c in range(0, self.n, self.wide)]
        self.squares = [slice(d, d + self.diag) for d in range(0, self.n, self.diag)]

    def eye(self):
        shape = (self.diag, self.diag)
        return lax.broadcasted_iota(jnp.int32, shape, 0) == lax.broadcasted_iota(jnp.int32, shape, 1)

    def trace(self, ref):
        mask = self.eye()
        return sum(total(jnp.where(mask, ref[d, d], 0.0)) for d in self.squares)

    def centre(self, s):
        shift = self.trace(self.e) * (1.0 / self.n)
        mask = self.eye()
        for d in self.squares:
            moved = self.e[d, d] - jnp.where(mask, shift, 0.0)
            self.e[d, d] = moved
            self.ebf[d, d] = moved.astype(jnp.bfloat16)
        return s + shift

    def start(self):
        norm = jnp.sqrt(self.trace(self.e)) + 1e-06
        scale = 1.0 / (norm * norm)
        for c in self.columns:
            x = self.e[:, c] * scale
            self.e[:, c] = x
            self.ebf[:, c] = x.astype(jnp.bfloat16)
        return self.centre(jnp.zeros((1, 1), jnp.float32)), 1.0 / norm

    def polynomial(self, s, c):
        p1 = coef_b + 2.0 * coef_c * s
        f = p1 * self.e[:, c] + coef_c * mm(self.ebf[...], self.ebf[:, c])
        self.fbf[:, c] = f.astype(jnp.bfloat16)

    def first(self):
        for c in self.columns:
            f = self.fbf[:, c]
            self.h[:, c] = f.astype(jnp.float32)
            self.hbf[0, :, c] = f

    def grow(self, p0, q, c, now, later):
        new = p0 * self.h[:, c] + q * self.fbf[:, c].astype(jnp.float32) + mm(self.fbf[...], self.hbf[now, :, c])
        self.h[:, c] = new
        self.hbf[later, :, c] = new.astype(jnp.bfloat16)

    def inner(self, p0, s, c):
        new = p0 * self.e[:, c] + s * self.fbf[:, c].astype(jnp.float32) + mm(self.fbf[...], self.ebf[:, c])
        self.k[:, c] = new
        self.kbf[:, c] = new.astype(jnp.bfloat16)

    def outer(self, p0, beta, c):
        new = p0 * self.k[:, c] + beta * self.fbf[:, c].astype(jnp.float32) + mm(self.fbf[...], self.kbf[:, c])
        self.e[:, c] = new
        self.ebf[:, c] = new.astype(jnp.bfloat16)


def muon_kernel(*refs):
    m_in, m_out = refs[:2]
    g_in, g_out, moments = refs[2], refs[3], refs[4:8]
    grads_out, moments_out = refs[8:12], refs[12:16]
    h_out, hs_out, scal = refs[16:19]
    grads, news = refs[19:23], refs[23:27]
    tall, lump, x, small_m, in_sem, out_sem = refs[27:33]
    big, small = Iterate(*refs[33:40]), Iterate(*refs[40:47])
    f32, b16 = jnp.float32, jnp.bfloat16
    core = lax.rem(lax.axis_index("rep"), 2)
    shard = lax.axis_index("shard")
    n, ns = big.n, small.n
    own_in = g_in.shape[0]
    n_rep, own_out, cols_out = g_out.shape
    columns = [(0, n), (n, ns), (n + ns, ns)]

    wide = pltpu.make_async_copy(m_in.at[:, pl.ds(0, n)], tall, in_sem.at[0])
    flat = pltpu.make_async_copy(m_out, lump, in_sem.at[0])
    kv = pltpu.make_async_copy(m_in.at[:, pl.ds(pl.multiple_of(n + core * ns, 128), ns)], small_m, in_sem.at[1])

    @pl.when(core == 0)
    def _():
        wide.start()

    @pl.when(core != 0)
    def _():
        flat.start()

    kv.start()

    rows = 64
    copies = []
    for i in range(4):
        if i < 3:
            def update(j, i=i, at=columns[i][0], width=columns[i][1]):
                r = span(j, rows)
                grad = g_in[r, at : at + width].astype(f32)
                grads[i][r, :] = grad
                news[i][r, :] = decay * moments[i][r, :] + grad

            tiles(own_in // rows, update)
        else:
            def update(r, i=i):
                at = span(r, cols_out)
                grad = g_out[r].astype(f32)
                grads[i][:, at] = grad
                news[i][:, at] = decay * moments[i][:, at] + grad

            tiles(n_rep, update)
        copies.append(pltpu.make_async_copy(grads[i], grads_out[i], out_sem.at[2 * i]))
        copies.append(pltpu.make_async_copy(news[i], moments_out[i], out_sem.at[2 * i + 1]))
        copies[-2].start()
        copies[-1].start()
    kv.wait()
    mine = span(shard, own_in)

    @pl.when(core == 0)
    def _():
        wide.wait()
        tall[mine, :] = news[0][...].astype(b16)
        small_m[mine, :] = news[1][...].astype(b16)
        tiles(tall.shape[0] // 256, lambda i: x.__setitem__((slice(None), span(i, 256)), tall[span(i, 256), :].T))

    @pl.when(core != 0)
    def _():
        flat.wait()
        for s in range(lump.shape[0]):
            tiles(n_rep, lambda r, s=s: x.__setitem__((slice(s * own_out, (s + 1) * own_out), span(r, cols_out)), lump[s, r]))
        x[span(shard, own_out), :] = news[3][...].astype(b16)
        small_m[mine, :] = news[2][...].astype(b16)

    tiles(n // big.wide, lambda j: big.e.__setitem__((slice(None), span(j, big.wide)), nt(x[...], x[span(j, big.wide), :])))
    small.e[...] = tn(small_m[...], small_m[...])
    s, inv = big.start()
    ss, sinv = small.start()

    def sweep(it, carry):
        s, q, ss, sq = carry
        now, later = lax.rem(it + 1, 2), lax.rem(it, 2)
        p0 = coef_a + s * (coef_b + coef_c * s)
        sp0 = coef_a + ss * (coef_b + coef_c * ss)

        def each(method, *args):
            for i, c in enumerate(big.columns):
                getattr(big, method)(*[a[0] for a in args], c, *extra)
                if i == 0:
                    for d in small.columns:
                        getattr(small, method)(*[a[1] for a in args], d, *extra)

        extra = ()
        each("polynomial", (s, ss))

        @pl.when(it == 0)
        def _():
            big.first()
            small.first()

        extra = (now, later)

        @pl.when(it > 0)
        def _():
            each("grow", (p0, sp0), (q, sq))

        extra = ()
        q, sq = p0 * q, sp0 * sq

        def advance():
            each("inner", (p0, sp0), (s, ss))
            beta, sbeta = p0 * s, sp0 * ss
            each("outer", (p0, sp0), (beta, sbeta))
            return big.centre(p0 * beta), small.centre(sp0 * sbeta)

        s, ss = lax.cond(it < SWEEPS - 1, advance, lambda: (s, ss))
        return s, q, ss, sq

    one = jnp.ones((1, 1), f32)
    s, q, ss, sq = lax.fori_loop(0, SWEEPS, sweep, (s, one, ss, one))
    last = (SWEEPS - 1) % 2
    h_out[...] = big.hbf[last]
    hs_out[...] = small.hbf[last]
    row = lax.broadcasted_iota(jnp.int32, (8, 128), 0)
    scal[...] = jnp.where(row == 0, q * inv, jnp.where(row == 1, inv, jnp.where(row == 2, sq * sinv, sinv)))
    for copy in copies:
        copy.wait()


def muon(m_in, m_out, g_in, g_out, moments):
    f32, b16 = jnp.float32, jnp.bfloat16
    tall, n, kv = m_in.shape[0], m_out.shape[0] * m_out.shape[2], moments[1].shape[1]
    V = pltpu.VMEM
    sets = []
    for d in (n, kv):
        sets += [V((d, d), f32), V((d, d), b16), V((d, d), f32), V((d, d), b16), V((d, d), f32), V((2, d, d), b16), V((d, d), b16)]
    vmem, any_ = pl.BlockSpec(memory_space=pltpu.VMEM), pl.BlockSpec(memory_space=pl.ANY)
    own = [jax.ShapeDtypeStruct(m.shape, f32) for m in moments]
    out = pl.pallas_call(
        muon_kernel,
        out_shape=own
        + own
        + [
            jax.ShapeDtypeStruct((n, n), b16),
            jax.ShapeDtypeStruct((kv, kv), b16),
            jax.ShapeDtypeStruct((8, 128), f32),
        ],
        in_specs=[any_] * 2 + [vmem] * 6,
        out_specs=[any_] * 8 + [vmem] * 3,
        scratch_shapes=[V(m.shape, f32) for m in moments] * 2
        + [
            V((tall, n), b16),
            V(m_out.shape, b16),
            V((n, m_out.shape[1] * m_out.shape[3]), b16),
            V((tall, kv), b16),
            pltpu.SemaphoreType.DMA((2,)),
            pltpu.SemaphoreType.DMA((8,)),
        ]
        + sets,
        compiler_params=pltpu.CompilerParams(vmem_limit_bytes=63 << 20),
        name="muon",
    )(m_in, m_out, g_in, g_out, *moments)
    return out[:4], out[4:8], out[8:]


def swap_kernel(n_rep, h, hs, scal, h_pair, hs_come, scal_come, send, recv):
    rep, shard = lax.axis_index("rep"), lax.axis_index("shard")
    core = lax.rem(rep, 2)
    other = rep + 1 - 2 * core
    sem = pltpu.get_barrier_semaphore()
    pl.semaphore_signal(sem, 1, device_id=(other, shard), device_id_type=pl.DeviceIdType.MESH)
    pl.semaphore_wait(sem, 1)

    def remote(src, dst, i):
        return pltpu.make_async_remote_copy(
            src, dst, send.at[i], recv.at[i], device_id=(other, shard), device_id_type=pl.DeviceIdType.MESH
        )

    count = h_pair.shape[0]
    at = jnp.where(core == 0, lax.div(rep, 2), shard)
    copies = [remote(h.at[span(at, count), :], h_pair, 0), remote(hs, hs_come, 1), remote(scal, scal_come, 2)]
    for c in copies:
        c.start()
    for c in copies:
        c.wait()


def swap(h, hs, scal, count, n_rep, collective_id):
    any_ = pl.BlockSpec(memory_space=pl.ANY)
    return pl.pallas_call(
        functools.partial(swap_kernel, n_rep),
        out_shape=[
            jax.ShapeDtypeStruct((count, h.shape[1]), h.dtype),
            jax.ShapeDtypeStruct(hs.shape, hs.dtype),
            jax.ShapeDtypeStruct(scal.shape, scal.dtype),
        ],
        in_specs=[any_] * 3,
        out_specs=[any_] * 3,
        scratch_shapes=[pltpu.SemaphoreType.DMA((3,)), pltpu.SemaphoreType.DMA((3,))],
        compiler_params=pltpu.CompilerParams(collective_id=collective_id, has_side_effects=True),
        name="swap",
    )(h, hs, scal)


def window(index, width):
    size = max(width, 128)
    start = lax.div(index * width, size) * size
    return pl.ds(pl.multiple_of(start, 128), size), size, index * width - start


def cut(x, size, offset, width):
    return x if size == width else pltpu.roll(x, lax.rem(size - offset, size), 1)[:, :width]


def update_kernel(h, h_pair, hs, hs_come, scal, scal_come, m_out, mq, mk, mv, mo, wq, wk, wv, wo, *refs):
    nexts, (hq, ho, flat, mo_win), weight_wins, (h_sem, sem) = refs[:4], refs[4:8], refs[8:12], refs[12:]
    f32, b16 = jnp.float32, jnp.bfloat16
    rep, shard = lax.axis_index("rep"), lax.axis_index("shard")
    even = lax.rem(rep, 2) == 0
    widths = [o.shape[1] for o in nexts]
    wins = [window(rep, w) for w in widths]
    own_out = ho.shape[0]
    copies = [
        pltpu.make_async_copy(m_out.at[:, rep], flat, sem.at[4]),
        pltpu.make_async_copy(mo.at[:, wins[3][0]], mo_win, sem.at[5]),
    ] + [pltpu.make_async_copy(w.at[:, wins[i][0]], weight_wins[i], sem.at[i]) for i, w in enumerate((wq, wk, wv, wo))]
    for copy in copies:
        copy.start()
    rows_q = h.at[span(rep, widths[0]), :], h_pair.at[pl.ds(h_pair.shape[0] - widths[0], widths[0]), :]
    rows_o = h_pair, h.at[span(shard, own_out), :]
    mixes = [[pltpu.make_async_copy(a, b, h_sem.at[i]) for i, (a, b) in enumerate(((q, hq), (o, ho)))] for q, o in zip(rows_q, rows_o)]
    for side, here in ((0, even), (1, jnp.logical_not(even))):
        @pl.when(here)
        def _():
            for copy in mixes[side]:
                copy.start()
            for copy in mixes[side]:
                copy.wait()
    for copy in copies:
        copy.wait()
    first = jnp.where(even, scal[...], scal_come[...])
    second = jnp.where(even, scal_come[...], scal[...])
    flat[shard] = mo_win[...].astype(b16)

    def rows_of(i):
        at = span(rep, widths[i])
        mine, theirs = hs[at, :].astype(f32), hs_come[at, :].astype(f32)
        return jnp.where(even == (i == 1), mine, theirs).astype(b16)

    parts = (
        (mq, lambda: nt(mq[...].astype(b16), hq[...]), first[0:1, 0:1], first[1:2, 0:1]),
        (mk, lambda: nt(mk[...].astype(b16), rows_of(1)), first[2:3, 0:1], first[3:4, 0:1]),
        (mv, lambda: nt(mv[...].astype(b16), rows_of(2)), second[2:3, 0:1], second[3:4, 0:1]),
        (None, lambda: mm(ho[...], flat[...].reshape(-1, flat.shape[2])), second[0:1, 0:1], second[1:2, 0:1]),
    )
    n_shard = lax.axis_size("shard")
    for i, (moment, product, straight, mixed) in enumerate(parts):
        at, size, offset = wins[i]
        here = mo_win[...] if moment is None else cut(moment[:, at], size, offset, widths[i])
        ortho = straight * here + mixed * product()
        whole = (weight_wins[i].shape[0] * n_shard, (wq, wk, wv, wo)[i].shape[1])
        weight = cut(weight_wins[i][...], size, offset, widths[i])
        nexts[i][...] = weight - muon_rate * math.sqrt(max(whole)) * ortho


def update(h, hs, scal, m_out, moments, weights, n_rep, collective_id):
    f32, b16 = jnp.float32, jnp.bfloat16
    widths = [w.shape[1] // n_rep for w in weights]
    own_out = weights[3].shape[0]
    assert 2 * widths[0] == own_out and m_out.shape[3] == widths[3]
    h_pair, hs_come, scal_come = swap(h, hs, scal, own_out, n_rep, collective_id)
    vmem, any_ = pl.BlockSpec(memory_space=pltpu.VMEM), pl.BlockSpec(memory_space=pl.ANY)
    V = pltpu.VMEM
    sizes = [max(w, 128) for w in widths]
    return pl.pallas_call(
        update_kernel,
        out_shape=[jax.ShapeDtypeStruct((w.shape[0], width), f32) for w, width in zip(weights, widths)],
        in_specs=[any_] * 2 + [vmem] * 4 + [any_] + [vmem] * 3 + [any_] * 5,
        out_specs=[vmem] * 4,
        scratch_shapes=[
            V((widths[0], h.shape[1]), b16),
            V((own_out, h.shape[1]), b16),
            V((m_out.shape[0],) + m_out.shape[2:], b16),
            V((own_out, sizes[3]), f32),
        ]
        + [V((w.shape[0], size), f32) for w, size in zip(weights, sizes)]
        + [pltpu.SemaphoreType.DMA((2,)), pltpu.SemaphoreType.DMA((6,))],
        name="update",
    )(h, h_pair, hs, hs_come, scal, scal_come, m_out, *moments, *weights)


HEAD_SIZE = 64
TILE = 256
norm_eps = 1e-05
rope_base = 500000.0
F32, B16 = jnp.float32, jnp.bfloat16
MESH = pl.DeviceIdType.MESH
WAYS = (1, -1)


class Links:
    def __init__(self, n_rep, n_shard, send, recv):
        self.n_bits, self.n_shard = n_rep.bit_length() - 1, n_shard
        self.rep, self.shard = lax.axis_index("rep"), lax.axis_index("shard")
        self.bits = [lax.rem(lax.div(self.rep, 1 << b), 2) for b in range(self.n_bits)]
        far = list(range(1, self.n_bits))
        self.orders = (far, far[::-1])
        self.send, self.recv, self.names = send, recv, {}

    def flip(self, bit):
        return self.rep + (1 << bit) * (1 - 2 * self.bits[bit])

    def barrier(self):
        sem = pltpu.get_barrier_semaphore()
        for b in range(self.n_bits):
            pl.semaphore_signal(sem, 1, device_id=(self.flip(b), self.shard), device_id_type=MESH)
        for k in range(1, self.n_shard):
            there = lax.rem(self.shard + k, self.n_shard)
            pl.semaphore_signal(sem, 1, device_id=(self.rep, there), device_id_type=MESH)
        pl.semaphore_wait(sem, self.n_bits + self.n_shard - 1)

    def where(self, free=()):
        return tuple(slice(None) if b in free else self.bits[b] for b in reversed(range(self.n_bits)))

    def remote(self, src, dst, name, rep, shard):
        i = self.names.setdefault(name, len(self.names))
        return pltpu.make_async_remote_copy(
            src, dst, self.send.at[i], self.recv.at[i], device_id=(rep, shard), device_id_type=MESH
        )

    def goes(self, way, k):
        q, there = self.shard - way * k, self.shard + way
        return (q >= 0) & (q < self.n_shard) & (there >= 0) & (there < self.n_shard)

    def comes(self, way, k):
        q = self.shard - way * (k + 1)
        return (q >= 0) & (q < self.n_shard)


class Gather:
    def __init__(self, links, name, full, half, first=None):
        self.links, self.name, self.full, self.half, self.first = links, name, full, half, first

    def line(self, way, k):
        at = self.full.at[(self.links.shard - way * k,) + self.links.where()]
        src = self.first if k == 0 and self.first is not None else at
        return self.links.remote(src, at, (self.name, "l", way, k), self.links.rep, self.links.shard + way)

    def came(self, way, k):
        at = self.full.at[(self.links.shard - way * (k + 1),) + self.links.where()]
        return self.links.remote(at, at, (self.name, "l", way, k), self.links.rep, self.links.shard)

    def plane(self, way, k, h, step):
        links = self.links
        order = links.orders[h] + [0]
        view = self.full.at[(links.shard - way * (k + 1),) + links.where(order[:step]) + self.half[h]]
        return links.remote(view, view, (self.name, "p", way, k, h, step), links.flip(order[step]), links.shard)

    def start(self):
        for way in WAYS:
            @pl.when(self.links.goes(way, 0))
            def _():
                self.line(way, 0).start()

    def event(self, k, step, then=None):
        links = self.links
        for way in WAYS:
            @pl.when(links.comes(way, k))
            def _():
                if step == 0:
                    self.came(way, k).wait_recv()
                    if k + 1 < links.n_shard - 1:
                        @pl.when(links.goes(way, k + 1))
                        def _():
                            self.line(way, k + 1).start()
                else:
                    for h in range(2):
                        self.plane(way, k, h, step - 1).wait_recv()
                if step < links.n_bits:
                    for h in range(2):
                        self.plane(way, k, h, step).start()
                elif then is not None:
                    then(links.shard - way * (k + 1))

    def drain(self):
        links = self.links
        for way in WAYS:
            for k in range(links.n_shard - 1):
                @pl.when(links.goes(way, k))
                def _():
                    self.line(way, k).wait_send()

                @pl.when(links.comes(way, k))
                def _():
                    for h in range(2):
                        for step in range(links.n_bits):
                            self.plane(way, k, h, step).wait_send()


class Reduce:
    def __init__(self, links, name, part, bufs, zbuf, gpiece, mpiece, moment, sums, wholes, half, keep_sem):
        self.links, self.name, self.part, self.bufs, self.zbuf = links, name, part, bufs, zbuf
        self.gpiece, self.mpiece, self.moment, self.sums, self.half = gpiece, mpiece, moment, sums, half
        self.whole = Gather(links, name + "m", wholes, half, mpiece)
        self.keep = lambda: pltpu.make_async_copy(gpiece, sums.at[links.where()], keep_sem)

    def dest(self, k):
        return lax.rem(self.links.shard + 1 + k, self.links.n_shard)

    def origin(self, k):
        return lax.rem(self.links.shard + self.links.n_shard - 1 - k, self.links.n_shard)

    def order(self, h):
        return [0] + self.links.orders[h]

    def cut(self, h, step):
        return (slice(None), slice(None)) if step == 0 else self.half[h]

    def send(self, k, h, step):
        links, o = self.links, self.order(h)
        bit = o[step]
        src = self.part if step == 0 else self.bufs[step - 1]
        left = sorted(o[step:], reverse=True)
        pick = tuple(1 - links.bits[bit] if b == bit else slice(None) for b in left)
        d, cut = self.dest(k), self.cut(h, step)
        into = self.bufs[step].at[(d,) + (slice(None),) * (links.n_bits - 1 - step) + cut]
        return links.remote(src.at[(d,) + pick + cut], into, (self.name, "r", k, h, step), links.flip(bit), links.shard)

    def add(self, k, h, step):
        links, o = self.links, self.order(h)
        src = self.part if step == 0 else self.bufs[step - 1]
        left = sorted(o[step:], reverse=True)
        others = [b for b in left if b != o[step]]
        d, cut = self.dest(k), self.cut(h, step)

        def one(i):
            at = {b: lax.rem(lax.div(i, 1 << (len(others) - 1 - n)), 2) for n, b in enumerate(others)}
            here = (d,) + tuple(at[b] for b in others) + cut
            there = (d,) + tuple(links.bits[b] if b == o[step] else at[b] for b in left) + cut
            both = src[there].astype(F32) + self.bufs[step][here].astype(F32)
            self.bufs[step][here] = both.astype(B16)

        if others:
            tiles(1 << len(others), one)
        else:
            one(0)

    def send_line(self, k):
        links, d = self.links, self.dest(k)
        return links.remote(self.bufs[-1].at[d], self.zbuf.at[links.shard], (self.name, "z", k), links.rep, d)

    def come_line(self, k):
        links, at = self.links, self.zbuf.at[self.origin(k)]
        return links.remote(at, at, (self.name, "z", k), links.rep, links.shard)

    def start(self, k):
        self.send(k, 0, 0).start()

    def event(self, k, step):
        last = self.links.n_bits - 1
        for h in range(1 if step == 0 else 2):
            self.send(k, h, step).wait_recv()
            self.add(k, h, step)
            if step == 0 and last > 0:
                self.send(k, 0, 1).start()
                self.send(k, 1, 1).start()
            elif step < last:
                self.send(k, h, step + 1).start()
        if step == last and k < self.links.n_shard - 1:
            self.send_line(k).start()

    def gather_sum(self, h, step):
        links = self.links
        order = links.orders[h] + [0]
        into = self.sums.at[links.where(order[:step]) + self.half[h]]
        src = self.gpiece.at[self.half[h]] if step == 0 else into
        return links.remote(src, into, (self.name, "g", h, step), links.flip(order[step]), links.shard)

    def finish(self, decay):
        links = self.links
        for k in range(links.n_shard - 1):
            self.come_line(k).wait_recv()
        acc = self.bufs[-1][links.shard].astype(F32)
        for k in range(links.n_shard - 1):
            acc = acc + self.zbuf[self.origin(k)].astype(F32)
        g = acc.astype(B16)
        self.gpiece[...] = g
        self.mpiece[...] = (decay * self.moment[...] + g.astype(F32)).astype(B16)
        self.whole.start()
        for h in range(2):
            self.gather_sum(h, 0).start()
        self.keep().start()

    def gather_event(self, i, step):
        if i > 0:
            self.whole.event(i - 1, step)
            return
        if step == 0:
            self.keep().wait()
        if step < self.links.n_bits:
            for h in range(2):
                self.gather_sum(h, step).wait_recv()
                if step + 1 < self.links.n_bits:
                    self.gather_sum(h, step + 1).start()

    def drain(self):
        links = self.links
        for k in range(links.n_shard):
            for step in range(links.n_bits):
                for h in range(1 if step == 0 else 2):
                    self.send(k, h, step).wait_send()
            if k < links.n_shard - 1:
                self.send_line(k).wait_send()
        for h in range(2):
            for step in range(links.n_bits):
                self.gather_sum(h, step).wait_send()
        self.whole.drain()


class GainSum:
    def __init__(self, links, acc, come, line):
        self.links, self.acc, self.come, self.line = links, acc, come, line

    def send(self, b):
        return self.links.remote(self.acc, self.come.at[b], ("gain", b), self.links.flip(b), self.links.shard)

    def send_line(self, k):
        links = self.links
        d = lax.rem(links.shard + 1 + k, links.n_shard)
        return links.remote(self.acc.at[d], self.line.at[links.shard], ("gainz", k), links.rep, d)

    def event(self, b):
        links = self.links
        self.send(b).wait()
        self.acc[...] = self.acc[...] + self.come[b]
        if b + 1 < links.n_bits:
            self.send(b + 1).start()
        else:
            for k in range(links.n_shard - 1):
                self.send_line(k).start()

    def end(self):
        links = self.links
        for k in range(links.n_shard - 1):
            self.send_line(k).wait_send()
            at = self.line.at[lax.rem(links.shard + links.n_shard - 1 - k, links.n_shard)]
            links.remote(at, at, ("gainz", k), links.rep, links.shard).wait_recv()
        acc = self.acc[links.shard]
        for q in range(links.n_shard):
            acc = jnp.where(links.shard == q, acc, acc + self.line[q])
        return acc


def swap_halves(x):
    half, width = HEAD_SIZE // 2, x.shape[1]
    lane = lax.rem(lax.broadcasted_iota(jnp.int32, x.shape, 1), HEAD_SIZE)
    return jnp.where(lane < half, pltpu.roll(x, width - half, 1), pltpu.roll(x, half, 1))


def flat(x):
    return x.reshape(-1, x.shape[-1])


def bits_of(r, n_bits):
    return tuple((r >> b) & 1 for b in reversed(range(n_bits)))


def layer_kernel(
    n_rep, n_shard, decay,
    tok, cot, seg_col, seg_row, frequency, gain, w_query, w_key, w_value, w_outproj, m_query, m_key, m_value, m_outproj,
    out, grad_tok, sums_in, sums_out, wholes_in, wholes_out, gain_out,
    w_in, w_out, gain_full, xn, inv_ref, q, dattn, attn_t, attn, dqkv, dxn, row_acc, kx, vx, kxt, vxt, dk_acc, dv_acc,
    bias, cosine, sine, inv_l, part_in, part_out, gain_acc, gain_come, gain_line, moment_in, moment_out,
    zbuf_in, gp_in, mp_in, zbuf_out, gp_out, mp_out, load_sem, keep_sem, send, recv, *bufs,
):
    seq, width = tok.shape
    q_width, kv_width = w_query.shape[1], w_key.shape[1]
    kv_heads = kv_width // HEAD_SIZE
    pair = 2 * HEAD_SIZE
    pairs = q_width // pair
    per_group = pairs // kv_heads
    n_tok = seq // TILE
    scale = 1.0 / math.sqrt(HEAD_SIZE)
    rows = 64
    nb = n_rep.bit_length() - 1
    own_in, own_out = width // n_shard, q_width // n_shard
    rows_in, cols_out = own_in // n_rep, width // n_rep
    spans_in = ((0, q_width), (q_width, kv_width), (q_width + kv_width, kv_width))

    links = Links(n_rep, n_shard, send, recv)
    me, rep = links.shard, links.rep
    all_in = w_in.shape[-1]
    half_in = [(slice(None), pl.ds(h * (all_in // 2), all_in // 2)) for h in range(2)]
    half_out = [(pl.ds(h * (own_out // 2), own_out // 2), slice(None)) for h in range(2)]
    get_in, get_out = Gather(links, "wi", w_in, half_in), Gather(links, "wo", w_out, half_out)
    sum_in = Reduce(links, "i", part_in, bufs[:nb], zbuf_in, gp_in, mp_in, moment_in, sums_in, wholes_in, half_in, keep_sem.at[0])
    sum_out = Reduce(links, "o", part_out, bufs[nb:], zbuf_out, gp_out, mp_out, moment_out, sums_out, wholes_out, half_out, keep_sem.at[1])
    sum_gain = GainSum(links, gain_acc, gain_come, gain_line)

    loads = [
        pltpu.make_async_copy(w, dxn.at[pl.ds(0, own_in), pl.ds(at, size)], load_sem.at[i])
        for i, ((at, size), w) in enumerate(zip(spans_in, (w_query, w_key, w_value)))
    ]
    for load in loads:
        load.start()
    links.barrier()
    for load in loads:
        load.wait()
    for r in range(n_rep):
        w_in[(me,) + bits_of(r, nb)] = dxn[r * rows_in : (r + 1) * rows_in, :all_in].astype(B16)
    get_in.start()
    load_out = pltpu.make_async_copy(w_outproj, dxn.at[pl.ds(0, own_out), :], load_sem.at[3])
    load_out.start()

    def gain_line_copy(way, k):
        at = gain_full.at[me - way * k]
        return links.remote(at, at, ("gf", way, k), rep, me + way)

    def gain_came(way, k):
        at = gain_full.at[me - way * (k + 1)]
        return links.remote(at, at, ("gf", way, k), rep, me)

    gain_full[me] = gain[...].astype(B16).astype(F32)
    load_out.wait()
    for r in range(n_rep):
        w_out[(me,) + bits_of(r, nb)] = dxn[:own_out, r * cols_out : (r + 1) * cols_out].astype(B16)
    for way in WAYS:
        @pl.when(links.goes(way, 0))
        def _():
            gain_line_copy(way, 0).start()
    get_out.start()
    loads = [
        pltpu.make_async_copy(m.at[span(rep, rows_in), :], moment_in.at[:, pl.ds(at, size)], load_sem.at[i])
        for i, ((at, size), m) in enumerate(zip(spans_in, (m_query, m_key, m_value)))
    ] + [pltpu.make_async_copy(m_outproj.at[:, span(rep, cols_out)], moment_out, load_sem.at[3])]
    for load in loads:
        load.start()

    def masks(i):
        r = span(i, rows)
        key = lax.broadcasted_iota(jnp.int32, (rows, seq), 0) + i * rows
        query = lax.broadcasted_iota(jnp.int32, (rows, seq), 1)
        seen = (key <= query) & (seg_col[r, :] == seg_row[...])
        bias[r, :] = jnp.where(seen, 0.0, -1e30)
        start = jnp.sum((seg_row[...] < seg_col[r, :]).astype(F32), 1, keepdims=True)
        at = lax.broadcasted_iota(jnp.int32, (rows, 1), 0) + i * rows
        angle = (at.astype(F32) - start) * frequency[...]
        lane = lax.rem(lax.broadcasted_iota(jnp.int32, (rows, pair), 1), HEAD_SIZE)
        cosine[r, :] = jnp.cos(angle)
        s = jnp.sin(angle)
        sine[r, :] = jnp.where(lane < HEAD_SIZE // 2, -s, s)
        x = tok[r, :].astype(F32)
        inv = lax.rsqrt(jnp.mean(x * x, -1, keepdims=True) + norm_eps)
        inv_ref[r, :] = jnp.broadcast_to(inv, (rows, 128))

    tiles(seq // rows, masks)

    for k in range(n_shard - 1):
        for way in WAYS:
            @pl.when(links.comes(way, k))
            def _():
                gain_came(way, k).wait_recv()
                if k + 1 < n_shard - 1:
                    @pl.when(links.goes(way, k + 1))
                    def _():
                        gain_line_copy(way, k + 1).start()

    def gains():
        return jnp.concatenate([gain_full[s] for s in range(n_shard)], 1)

    def norm(i):
        r = span(i, rows)
        xn[r, :] = (tok[r, :].astype(F32) * inv_ref[r, :1] * gains()).astype(B16)

    tiles(seq // rows, norm)

    def project(s, fresh=False):
        x = xn[:, span(s, own_in)]

        def columns(c):
            part = mm(x, flat(w_in[(s,) + (slice(None),) * (nb + 1) + (span(c, TILE),)]))
            at = span(c, TILE)
            dxn[:, at] = part if fresh else dxn[:, at] + part

        tiles(all_in // TILE, columns)

    project(me, True)
    items = [(get_in, k) for k in range(n_shard - 1)] + [(get_out, k) for k in range(n_shard - 1)]

    def gather_time(t):
        for i, (gather, k) in enumerate(items):
            if 0 <= t - i <= nb:
                gather.event(k, t - i, project if gather is get_in else None)

    first_phase = n_shard - 1 + nb
    for t in range(first_phase):
        gather_time(t)
    later = list(range(first_phase, len(items) + nb))

    def tables():
        c, s = cosine[...], sine[...]
        return jnp.concatenate([c] * (TILE // pair), 1), jnp.concatenate([s] * (TILE // pair), 1)

    def query_tile(i):
        at = span(i, TILE)
        x = dxn[:, at]
        c, s = tables()
        q[:, at] = (x * c + swap_halves(x) * s).astype(B16)

    tiles(q_width // TILE, query_tile)
    low = lax.broadcasted_iota(jnp.int32, (seq, pair), 1) < HEAD_SIZE

    def split(x, into, into_t):
        for g in range(kv_heads):
            two = x[:, (g // 2) * pair : (g // 2 + 1) * pair].astype(B16).astype(F32)
            other = pltpu.roll(two, HEAD_SIZE, 1)
            first, second = (two, other) if g % 2 == 0 else (other, two)
            lo, hi = jnp.where(low, first, 0.0).astype(B16), jnp.where(low, 0.0, second).astype(B16)
            into[g, 0], into[g, 1] = lo, hi
            into_t[g, 0], into_t[g, 1] = lo.T, hi.T

    for first, into, into_t, turned in ((q_width, kx, kxt, True), (q_width + kv_width, vx, vxt, False)):
        x = dxn[:, first : first + kv_width]
        if turned:
            c, s = tables()
            x = x * c + swap_halves(x) * s
        split(x, into, into_t)

    def blocks():
        for b in range(n_tok):
            yield slice(b * TILE, (b + 1) * TILE), slice(max(b - 1, 0) * TILE, (b + 1) * TILE)

    def forward(p):
        for i, t in enumerate(later):
            @pl.when(p == min(1 + (i * pairs) // (2 * len(later)) * 2, pairs - 1))
            def _():
                gather_time(t)

        g = lax.div(p, per_group)
        lanes = span(p, pair)
        for qs, ks in blocks():
            q_b, mask, a_t = q[qs, lanes], bias[ks, qs], None
            for side in range(2):
                grown = jnp.exp(nt(kx[g, side, ks, :], q_b) * scale + mask)
                inv = 1.0 / jnp.sum(grown, 0, keepdims=True)
                inv_l[p, side, :, qs] = inv
                part = mm(vxt[g, side, :, ks], (grown * inv).astype(B16))
                a_t = part if a_t is None else a_t + part
            attn_t[lanes, qs] = a_t.astype(B16)
            attn[qs, lanes] = a_t.T.astype(B16)

    tiles(pairs, forward)

    for r in range(n_rep):
        c = slice(r * cols_out, (r + 1) * cols_out)
        x = mm(attn_t[...], cot[:, c]).astype(B16)
        part_out[(slice(None),) + bits_of(r, nb)] = x.reshape(n_shard, own_out, cols_out)
    for k in range(n_shard):
        sum_out.start(k)

    def head_grad(s):
        x = None
        for r in range(n_rep):
            part = nt(cot[:, r * cols_out : (r + 1) * cols_out], w_out[(s,) + bits_of(r, nb)])
            x = part if x is None else x + part
        dattn[:, span(s, own_out)] = x.astype(B16)

    tiles(n_shard, head_grad)

    def reduce_time(who, t):
        for step in reversed(range(nb)):
            if 0 <= t - step < n_shard:
                who.event(t - step, step)

    out_times = list(range(n_shard + nb - 1))

    def backward(p):
        for t in out_times:
            @pl.when(p == min(2 + t, pairs - 1))
            def _():
                reduce_time(sum_out, t)

        g = lax.div(p, per_group)
        lanes = span(p, pair)

        @pl.when(lax.rem(p, per_group) == 0)
        def _():
            dk_acc[...] = jnp.zeros_like(dk_acc)
            dv_acc[...] = jnp.zeros_like(dv_acc)

        for qs, ks in blocks():
            q_b, d_b, mask, dq = q[qs, lanes], dattn[qs, lanes], bias[ks, qs], None
            for side in range(2):
                grown = jnp.exp(nt(kx[g, side, ks, :], q_b) * scale + mask)
                prob = grown * inv_l[p, side, :, qs]
                dp = nt(vx[g, side, ks, :], d_b)
                inner = jnp.sum(prob * dp, 0, keepdims=True)
                ds = (prob * (dp - inner) * scale).astype(B16)
                dv_acc[side, ks, :] += mm(prob.astype(B16), d_b)
                dk_acc[side, ks, :] += mm(ds, q_b)
                part = mm(kxt[g, side, :, ks], ds)
                dq = part if dq is None else dq + part
            x = dq.T
            dqkv[qs, lanes] = (x * cosine[qs, :] - swap_halves(x) * sine[qs, :]).astype(B16)

        @pl.when(lax.rem(p, per_group) == per_group - 1)
        def _():
            def joined(acc):
                return acc[0] + pltpu.roll(acc[1], HEAD_SIZE, 1)

            dk, dv = joined(dk_acc), joined(dv_acc)
            dk = dk * cosine[...] - swap_halves(dk) * sine[...]
            for x, first in ((dk, q_width), (dv, q_width + kv_width)):
                at = span(lax.div(g, 2) + first // pair, pair)
                odd = lax.rem(g, 2)

                @pl.when(odd == 0)
                def _():
                    dqkv[:, at] = x.astype(B16)

                @pl.when(odd == 1)
                def _():
                    high = pltpu.roll(x, HEAD_SIZE, 1)
                    dqkv[:, at] = jnp.where(low, dqkv[:, at].astype(F32), high).astype(B16)

    tiles(pairs, backward)

    def weight_grad(k):
        s = sum_in.dest(k)
        x = tn(xn[:, span(s, own_in)], dqkv[...]).astype(B16)
        part_in[s] = x.reshape((2,) * nb + (rows_in, all_in))
        sum_in.start(k)

    for k in range(n_shard):
        weight_grad(k)

    row_acc[...] = jnp.zeros_like(row_acc)

    def input_grad(s):
        c = slice(s * own_in, (s + 1) * own_in)
        d = nt(dqkv[...], flat(w_in[s]))
        normed = tok[:, c].astype(F32) * inv_ref[:, :1]
        gain_acc[s] = jnp.sum(d * normed, 0, keepdims=True)
        d = d * gain_full[s]
        dxn[:, c] = d
        row_acc[...] += jnp.broadcast_to(jnp.sum(d * normed, 1, keepdims=True), row_acc.shape)

    def token_grad(i):
        r = span(i, rows)
        inv = inv_ref[r, :1]
        normed = tok[r, :].astype(F32) * inv
        mean = row_acc[r, :1] * (1.0 / width)
        grad_tok[r, :] = (cot[r, :].astype(F32) + inv * (dxn[r, :] - normed * mean)).astype(B16)

    def output(r):
        c = slice(r * cols_out, (r + 1) * cols_out)
        x = mm(attn[...], flat(w_out[(slice(None),) + bits_of(r, nb)]))
        out[:, c] = (tok[:, c].astype(F32) + x).astype(B16)

    for load in loads:
        load.wait()
    input_grad(0)
    sum_out.finish(decay)
    for s in range(1, n_shard):
        input_grad(s)
        if s == n_shard // 2:
            reduce_time(sum_in, 0)
    sum_gain.send(0).start()
    reduce_time(sum_in, 1)
    tiles(seq // rows, token_grad)

    def gather_sums_time(who, t):
        for i in range(n_shard):
            if 0 <= t - i <= nb:
                who.gather_event(i, t - i)

    n_times = n_shard + nb
    for r in range(n_rep):
        output(r)
        if r == n_rep // 2:
            reduce_time(sum_in, 2)
            gather_sums_time(sum_out, 0)
    sum_gain.event(0)
    done = 1
    for t in range(3, n_shard + nb - 1):
        reduce_time(sum_in, t)
        if done < n_times:
            gather_sums_time(sum_out, done)
            done += 1
        if t - 2 < nb:
            sum_gain.event(t - 2)
    for b in range(max(n_shard + nb - 3, 1), nb):
        sum_gain.event(b)
    sum_in.finish(decay)
    gain_out[...] = sum_gain.end()
    for t in range(n_times):
        if done < n_times:
            gather_sums_time(sum_out, done)
            done += 1
        gather_sums_time(sum_in, t)

    for who in (get_in, get_out, sum_out, sum_in):
        who.drain()
    for way in WAYS:
        for k in range(n_shard - 1):
            @pl.when(links.goes(way, k))
            def _():
                gain_line_copy(way, k).wait_send()
    assert len(links.names) <= send.shape[0]


def layer(tok, cot, seg, gain, weights, moments, decay, n_rep, n_shard, collective_id):
    seq, width = tok.shape
    w_query, w_key, _, w_outproj = weights
    q_width, kv_width = w_query.shape[1], w_key.shape[1]
    all_in = q_width + 2 * kv_width
    kv_heads, pair = kv_width // HEAD_SIZE, 2 * HEAD_SIZE
    nb = n_rep.bit_length() - 1
    bits = (2,) * nb
    own_in, own_out = width // n_shard, q_width // n_shard
    piece_in, piece_out = (own_in // n_rep, all_in), (own_out, width // n_rep)
    half = HEAD_SIZE // 2
    frequency = rope_base ** (-2.0 * jnp.arange(half, dtype=F32) / HEAD_SIZE)
    frequency = jnp.concatenate([frequency] * (pair // half))[None]
    vmem, any_ = pl.BlockSpec(memory_space=pltpu.VMEM), pl.BlockSpec(memory_space=pl.ANY)
    V, D = pltpu.VMEM, pltpu.SemaphoreType.DMA
    n_sems = (
        2 * 2 * 2 * (n_shard - 1) * (1 + 2 * nb) + 2 * (n_shard * (1 + 2 * (nb - 1)) + n_shard - 1 + 2 * nb) + nb + 3 * n_shard
    )
    bufs = [V((n_shard,) + (2,) * (nb - 1 - j) + piece, B16) for piece in (piece_in, piece_out) for j in range(nb)]
    shape = jax.ShapeDtypeStruct
    return pl.pallas_call(
        functools.partial(layer_kernel, n_rep, n_shard, decay),
        out_shape=[
            shape((seq, width), B16),
            shape((seq, width), B16),
            shape(bits + piece_in, B16),
            shape(bits + piece_out, B16),
            shape((n_shard,) + bits + piece_in, B16),
            shape((n_shard,) + bits + piece_out, B16),
            shape((1, own_in), F32),
        ],
        in_specs=[vmem] * 6 + [any_] * 8,
        out_specs=[vmem] * 2 + [any_] * 4 + [vmem],
        scratch_shapes=[
            V((n_shard,) + bits + piece_in, B16),
            V((n_shard,) + bits + piece_out, B16),
            V((n_shard, 1, own_in), F32),
            V((seq, width), B16),
            V((seq, 128), F32),
            V((seq, q_width), B16),
            V((seq, q_width), B16),
            V((q_width, seq), B16),
            V((seq, q_width), B16),
            V((seq, all_in), B16),
            V((seq, width), F32),
            V((seq, 128), F32),
            V((kv_heads, 2, seq, pair), B16),
            V((kv_heads, 2, seq, pair), B16),
            V((kv_heads, 2, pair, seq), B16),
            V((kv_heads, 2, pair, seq), B16),
            V((2, seq, pair), F32),
            V((2, seq, pair), F32),
            V((seq, seq), F32),
            V((seq, pair), F32),
            V((seq, pair), F32),
            V((q_width // pair, 2, 1, seq), F32),
            V((n_shard,) + bits + piece_in, B16),
            V((n_shard,) + bits + piece_out, B16),
            V((n_shard, 1, own_in), F32),
            V((nb, n_shard, 1, own_in), F32),
            V((n_shard, 1, own_in), F32),
            V(piece_in, F32),
            V(piece_out, F32),
            V((n_shard,) + piece_in, B16),
            V(piece_in, B16),
            V(piece_in, B16),
            V((n_shard,) + piece_out, B16),
            V(piece_out, B16),
            V(piece_out, B16),
            D((4,)),
            D((2,)),
            D((n_sems,)),
            D((n_sems,)),
        ]
        + bufs,
        compiler_params=pltpu.CompilerParams(
            collective_id=collective_id, has_side_effects=True, vmem_limit_bytes=67_043_328
        ),
        name="layer",
    )(tok, cot, seg[:, None], seg[None], frequency, gain[None], *weights, *moments)


gain_rate = 0.2


def on_device(
    tokens,
    segments,
    cotangent,
    gain,
    w_query,
    w_key,
    w_value,
    w_outproj,
    moment_gain,
    moment_query,
    moment_key,
    moment_value,
    moment_outproj,
):
    n_rep, n_shard = lax.axis_size("rep"), lax.axis_size("shard")
    total_tokens = tokens.shape[0] * tokens.shape[1] * n_rep * n_shard
    weights = (w_query, w_key, w_value, w_outproj)
    moments = (moment_query, moment_key, moment_value, moment_outproj)
    result, grad_tokens, sum_in, sum_out, m_in, m_out, grad_gain = layer(
        tokens[0], cotangent[0], segments[0], gain, weights, moments, decay, n_rep, n_shard, 0
    )
    grad_gain = grad_gain[0]
    moment_gain_next = decay * moment_gain + grad_gain
    gain_next = gain - gain_rate / math.sqrt(total_tokens) * moment_gain_next
    own_out, cols_out = sum_out.shape[-2:]
    m_out = m_out.reshape(n_shard, n_rep, own_out, cols_out)
    all_in = sum_in.shape[-1]
    grads, moments_next, (mix, mix_kv, scales) = muon(
        m_in.reshape(-1, all_in), m_out, sum_in.reshape(-1, all_in), sum_out.reshape(n_rep, own_out, cols_out), moments
    )
    updated = update(mix, mix_kv, scales, m_out, moments_next, weights, n_rep, 1)
    return (
        result[None],
        grad_tokens[None],
        grad_gain,
        *grads,
        gain_next,
        *updated,
        moment_gain_next,
        *moments_next,
    )


def solution(mesh):
    in_specs = (
        P(("rep", "shard"), None, None),
        P(("rep", "shard"), None),
        P(("rep", "shard"), None, None),
        P("shard"),
        P("shard", None),
        P("shard", None),
        P("shard", None),
        P("shard", None),
        P("shard"),
        P("shard", None),
        P("shard", None),
        P("shard", None),
        P("shard", None),
    )
    out_specs = (
        P(("rep", "shard"), None, None),
        P(("rep", "shard"), None, None),
        P("shard"),
        P("shard", None),
        P("shard", None),
        P("shard", None),
        P("shard", None),
        P("shard"),
        P("shard", "rep"),
        P("shard", "rep"),
        P("shard", "rep"),
        P("shard", "rep"),
        P("shard"),
        P("shard", None),
        P("shard", None),
        P("shard", None),
        P("shard", None),
    )
    return jax.shard_map(on_device, mesh=mesh, in_specs=in_specs, out_specs=out_specs, check_vma=False)
```

time: 330 us -> 279 us (0.85)
  Pallas kernels: 311 us -> 268 us
  other arithmetic: 8.96 us -> 1.19 us
    pallas_call x3 -> x1, Pallas kernels: 241 us -> 198 us  [layer(): pl.pallas_call(functools.partial(layer_kernel, n_rep, n_shard, decay), ou...]
    dynamic_slice x3 -> x0, local copies, waits for them, and re-layouts: 3.68 us -> none  [rows_of(): return lax.dynamic_slice_in_dim(matrix, index * count, count, 0)]
    unnamed x19 -> x15, local copies, waits for them, and re-layouts: 4.81 us -> 7.64 us
where the time goes in v4:
time: 279 us
  Pallas kernels  268 us (96%)
  local copies, waits for them, and re-layouts  9.18 us (3%)
    pallas_call x1, Pallas kernels, layer(): pl.pallas_call(functools.partial(layer_kernel, n_rep, n_shard, decay), ou...  198 us
    pallas_call x1, Pallas kernels, muon(): pl.pallas_call(muon_kernel, out_shape=own + own + [jax.ShapeDtypeStruct((...  62.3 us
    unnamed x15, local copies, waits for them, and re-layouts  7.64 us

profile of v4, /device:TPU:0, one launch (start us, length us, event | category | flops | bytes accessed | tf_op | source)
XLA Modules:
  0.0 279.1 jit_solution(15839914348630119991)
XLA Ops:
  0.7 1.5 copy.32.seg_col
  2.2 0.6 maximum_bitcast_fusion.frequency
  2.8 197.7 %layer.1 = (bf16[512,2048]{1,0:T(8,128)(2,1)}, bf16[512,2048]{1,0:T(8,128)(2,1)}, bf16[2,2,2,64,1536]{4,3,2,1,0:T(8,128)(2,1)}, bf16[2,2,2,256,256]{4,3,2,1,0:T(...) custom-call(bf16[512,2048]{1,0:T(8,128)(2,1)} %bitcast.16, ...), custom_call_target="tpu_custom_call" | custom-call | tf_op jit(solution)/shard_map/layer/pallas_call | solution.py:1037
  200.5 62.3 %muon.1 = (f32[512,1024]{1,0:T(8,128)}, f32[512,256]{1,0:T(8,128)}, f32[512,256]{1,0:T(8,128)}, f32[256,2048]{1,0:T(8,128)}, f32[512,1024]{1,0:T(8,128)}, /*inde...) custom-call(bf16[2048,1536]{1,0:T(8,128)(2,1)} %bitcast.15, ...), custom_call_target="tpu_custom_call" | custom-call | tf_op jit(solution)/shard_map/muon/pallas_call | solution.py:244
  262.9 2.5 swap.1
  265.4 0.0 copy-start.2
  265.4 0.0 copy-start.3
  265.4 0.0 copy-start.4
  265.4 0.0 copy-start.1
  265.4 5.4 %update.1 = (f32[512,128]{1,0:T(8,128)}, f32[512,32]{1,0:T(8,128)}, f32[512,32]{1,0:T(8,128)}, f32[256,256]{1,0:T(8,128)}) custom-call(bf16[1024,1024]{1,0:T(8,128)(2,1)} %get-tuple-element.53.h, bf16[256,1024]{1,0:T(8,128)(2,1)} %get-tuple-element.56.h_pair, bf16[256,256]{1,0:T(8,128)(2,1)} %get-tuple-element.54.hs, ...), custom_call_target="tpu_custom_call" | custom-call | tf_op jit(solution)/shard_map/update/pallas_call | solution.py:380
  270.8 1.7 copy.33
  272.5 1.7 copy.34
  274.2 0.0 copy-done.2
  274.2 0.0 copy-done.3
  274.2 0.0 copy-done.4
  274.2 0.6 multiply_subtract_fusion
  274.8 0.0 copy-done.1
  274.8 0.0 copy-start
  274.8 1.3 copy.38
  276.1 1.0 copy-done
  277.2 1.3 copy.39
  278.5 0.6 copy.40
  (1 shorter events, 0.0 us)
Async XLA Ops:
  265.4 8.8 %copy-start.2 = (f32[512]{0:T(512)S(1)}, f32[512]{0:T(512)}, u32[]{:S(2)}) copy-start(f32[512]{0:T(512)} %param.16) | copy-start | bytes 6148
  265.4 8.8 %copy-start.3 = (f32[1,512]{1,0:T(1,128)S(1)}, f32[1,512]{1,0:T(1,128)}, u32[]{:S(2)}) copy-start(f32[1,512]{1,0:T(1,128)} %get-tuple-element.44) | copy-start | bytes 6148
  265.4 8.8 %copy-start.4 = (f32[512]{0:T(512)S(1)}, f32[512]{0:T(512)}, u32[]{:S(2)}) copy-start(f32[512]{0:T(512)} %param.21) | copy-start | bytes 6148
  265.4 9.4 %copy-start.1 = (bf16[512,2048]{1,0:T(8,128)(2,1)S(1)}, bf16[512,2048]{1,0:T(8,128)(2,1)}, u32[]{:S(2)}) copy-start(bf16[512,2048]{1,0:T(8,128)(2,1)} %get-tuple-element.42) | copy-start | bytes 6291460
  274.8 2.3 copy-start

commit v5 on v4

--- a/solution.py
+++ b/solution.py
@@ -3,6 +3,7 @@
 
 import jax
 import jax.numpy as jnp
+import numpy as np
 from jax import lax
 from jax.experimental import pallas as pl
 from jax.experimental.pallas import tpu as pltpu
@@ -107,66 +108,65 @@
 
 
 def muon_kernel(*refs):
-    m_in, m_out = refs[:2]
-    g_in, g_out, moments = refs[2], refs[3], refs[4:8]
-    grads_out, moments_out = refs[8:12], refs[12:16]
-    h_out, hs_out, scal = refs[16:19]
-    grads, news = refs[19:23], refs[23:27]
-    tall, lump, x, small_m, in_sem, out_sem = refs[27:33]
-    big, small = Iterate(*refs[33:40]), Iterate(*refs[40:47])
+    refs = list(refs)
+
+    def take(count):
+        return [refs.pop(0) for _ in range(count)]
+
+    m_in, m_out, *passed = take(4)
+    g_in, g_out, *moments = take(6)
+    grads_out, moments_out, passed_out = take(4), take(4), take(2)
+    h_out, hs_out, scal = take(3)
+    grads, news, held = take(4), take(4), take(2)
+    sums_in, sums_out, tall, lump, x, small_m = take(6)
+    in_sem, own_sem, out_sem, pass_sem = take(4)
+    big, small = Iterate(*take(7)), Iterate(*take(7))
     f32, b16 = jnp.float32, jnp.bfloat16
     core = lax.rem(lax.axis_index("rep"), 2)
     shard = lax.axis_index("shard")
     n, ns = big.n, small.n
     own_in = g_in.shape[0]
     n_rep, own_out, cols_out = g_out.shape
-    columns = [(0, n), (n, ns), (n + ns, ns)]
-
-    wide = pltpu.make_async_copy(m_in.at[:, pl.ds(0, n)], tall, in_sem.at[0])
+    chunk, q_part, kv_part = (n + 2 * ns) // 2, n // 2, ns // 2
+    firsts = [(0, q_part), (q_part, kv_part), (q_part + kv_part, kv_part)]
+
+    wide = [
+        pltpu.make_async_copy(m_in.at[:, pl.ds(c * chunk, q_part)], tall.at[:, pl.ds(c * q_part, q_part)], in_sem.at[c])
+        for c in range(2)
+    ]
     flat = pltpu.make_async_copy(m_out, lump, in_sem.at[0])
-    kv = pltpu.make_async_copy(m_in.at[:, pl.ds(pl.multiple_of(n + core * ns, 128), ns)], small_m, in_sem.at[1])
+    kv = [
+        pltpu.make_async_copy(
+            m_in.at[:, pl.ds(pl.multiple_of(c * chunk + q_part + core * kv_part, 128), kv_part)],
+            small_m.at[:, pl.ds(c * kv_part, kv_part)],
+            in_sem.at[2 + c],
+        )
+        for c in range(2)
+    ]
+    own = [pltpu.make_async_copy(a, b, own_sem.at[i]) for i, (a, b) in enumerate(zip(moments, news))]
+    own_sums = [pltpu.make_async_copy(g_in, sums_in, own_sem.at[4]), pltpu.make_async_copy(g_out, sums_out, own_sem.at[5])]
+    passing = [pltpu.make_async_copy(a, b, pass_sem.at[i]) for i, (a, b) in enumerate(zip(passed, held))]
+    leaving = [pltpu.make_async_copy(a, b, pass_sem.at[i]) for i, (a, b) in enumerate(zip(held, passed_out))]
 
     @pl.when(core == 0)
     def _():
-        wide.start()
+        for copy in wide:
+            copy.start()
 
     @pl.when(core != 0)
     def _():
         flat.start()
 
-    kv.start()
-
+    for copy in kv + own_sums + own + passing:
+        copy.start()
+
+    mine = span(shard, own_in)
     rows = 64
-    copies = []
-    for i in range(4):
-        if i < 3:
-            def update(j, i=i, at=columns[i][0], width=columns[i][1]):
-                r = span(j, rows)
-                grad = g_in[r, at : at + width].astype(f32)
-                grads[i][r, :] = grad
-                news[i][r, :] = decay * moments[i][r, :] + grad
-
-            tiles(own_in // rows, update)
-        else:
-            def update(r, i=i):
-                at = span(r, cols_out)
-                grad = g_out[r].astype(f32)
-                grads[i][:, at] = grad
-                news[i][:, at] = decay * moments[i][:, at] + grad
-
-            tiles(n_rep, update)
-        copies.append(pltpu.make_async_copy(grads[i], grads_out[i], out_sem.at[2 * i]))
-        copies.append(pltpu.make_async_copy(news[i], moments_out[i], out_sem.at[2 * i + 1]))
-        copies[-2].start()
-        copies[-1].start()
-    kv.wait()
-    mine = span(shard, own_in)
 
     @pl.when(core == 0)
     def _():
-        wide.wait()
-        tall[mine, :] = news[0][...].astype(b16)
-        small_m[mine, :] = news[1][...].astype(b16)
+        for copy in wide:
+            copy.wait()
         tiles(tall.shape[0] // 256, lambda i: x.__setitem__((slice(None), span(i, 256)), tall[span(i, 256), :].T))
 
     @pl.when(core != 0)
@@ -174,9 +174,48 @@
         flat.wait()
         for s in range(lump.shape[0]):
             tiles(n_rep, lambda r, s=s: x.__setitem__((slice(s * own_out, (s + 1) * own_out), span(r, cols_out)), lump[s, r]))
+
+    for copy in kv + own_sums + own:
+        copy.wait()
+    for i in range(4):
+        if i < 3:
+            def update(j, i=i, first=firsts[i][0], width=firsts[i][1]):
+                r = span(j, rows)
+                for c in range(2):
+                    at, to = c * chunk + first, slice(c * width, (c + 1) * width)
+                    grad = sums_in[r, at : at + width].astype(f32)
+                    grads[i][r, to] = grad
+                    news[i][r, to] = decay * news[i][r, to] + grad
+
+            tiles(own_in // rows, update)
+        else:
+            def update(r, i=i):
+                at = span(r, cols_out)
+                grad = sums_out[r].astype(f32)
+                grads[i][:, at] = grad
+                news[i][:, at] = decay * news[i][:, at] + grad
+
+            tiles(n_rep, update)
+
+    @pl.when(core == 0)
+    def _():
+        x[:, mine] = news[0][...].astype(b16).T
+        small_m[mine, :] = news[1][...].astype(b16)
+
+    @pl.when(core != 0)
+    def _():
         x[span(shard, own_out), :] = news[3][...].astype(b16)
         small_m[mine, :] = news[2][...].astype(b16)
 
+    copies = [
+        pltpu.make_async_copy(a, b, out_sem.at[i])
+        for i, (a, b) in enumerate(zip(grads + news, grads_out + moments_out))
+    ]
+    for copy in copies:
+        copy.start()
+    for a, b in zip(passing, leaving):
+        a.wait()
+        b.start()
     tiles(n // big.wide, lambda j: big.e.__setitem__((slice(None), span(j, big.wide)), nt(x[...], x[span(j, big.wide), :])))
     small.e[...] = tn(small_m[...], small_m[...])
     s, inv = big.start()
@@ -228,11 +267,11 @@
     hs_out[...] = small.hbf[last]
     row = lax.broadcasted_iota(jnp.int32, (8, 128), 0)
     scal[...] = jnp.where(row == 0, q * inv, jnp.where(row == 1, inv, jnp.where(row == 2, sq * sinv, sinv)))
-    for copy in copies:
+    for copy in copies + leaving:
         copy.wait()
 
 
-def muon(m_in, m_out, g_in, g_out, moments):
+def muon(m_in, m_out, g_in, g_out, moments, passed):
     f32, b16 = jnp.float32, jnp.bfloat16
     tall, n, kv = m_in.shape[0], m_out.shape[0] * m_out.shape[2], moments[1].shape[1]
     V = pltpu.VMEM
@@ -245,27 +284,33 @@
         muon_kernel,
         out_shape=own
         + own
+        + [jax.ShapeDtypeStruct(p.shape, p.dtype) for p in passed]
         + [
             jax.ShapeDtypeStruct((n, n), b16),
             jax.ShapeDtypeStruct((kv, kv), b16),
             jax.ShapeDtypeStruct((8, 128), f32),
         ],
-        in_specs=[any_] * 2 + [vmem] * 6,
-        out_specs=[any_] * 8 + [vmem] * 3,
+        in_specs=[any_] * 10,
+        out_specs=[any_] * 10 + [vmem] * 3,
         scratch_shapes=[V(m.shape, f32) for m in moments] * 2
+        + [V(p.shape, p.dtype) for p in passed]
         + [
+            V(g_in.shape, b16),
+            V(g_out.shape, b16),
             V((tall, n), b16),
             V(m_out.shape, b16),
             V((n, m_out.shape[1] * m_out.shape[3]), b16),
             V((tall, kv), b16),
+            pltpu.SemaphoreType.DMA((4,)),
+            pltpu.SemaphoreType.DMA((6,)),
+            pltpu.SemaphoreType.DMA((8,)),
             pltpu.SemaphoreType.DMA((2,)),
-            pltpu.SemaphoreType.DMA((8,)),
         ]
         + sets,
         compiler_params=pltpu.CompilerParams(vmem_limit_bytes=63 << 20),
         name="muon",
-    )(m_in, m_out, g_in, g_out, *moments)
-    return out[:4], out[4:8], out[8:]
+    )(m_in, m_out, *passed, g_in, g_out, *moments)
+    return out[:4], out[4:8], out[8:10], out[10:]
 
 
 def swap_kernel(n_rep, h, hs, scal, h_pair, hs_come, scal_come, send, recv):
@@ -322,7 +367,7 @@
     f32, b16 = jnp.float32, jnp.bfloat16
     rep, shard = lax.axis_index("rep"), lax.axis_index("shard")
     even = lax.rem(rep, 2) == 0
-    widths = [o.shape[1] for o in nexts]
+    widths = [nexts[0].shape[1], nexts[1].shape[0], nexts[2].shape[0], nexts[3].shape[1]]
     wins = [window(rep, w) for w in widths]
     own_out = ho.shape[0]
     copies = [
@@ -354,18 +399,22 @@
 
     parts = (
         (mq, lambda: nt(mq[...].astype(b16), hq[...]), first[0:1, 0:1], first[1:2, 0:1]),
-        (mk, lambda: nt(mk[...].astype(b16), rows_of(1)), first[2:3, 0:1], first[3:4, 0:1]),
-        (mv, lambda: nt(mv[...].astype(b16), rows_of(2)), second[2:3, 0:1], second[3:4, 0:1]),
+        (mk, lambda: nt(rows_of(1), mk[...].astype(b16)), first[2:3, 0:1], first[3:4, 0:1]),
+        (mv, lambda: nt(rows_of(2), mv[...].astype(b16)), second[2:3, 0:1], second[3:4, 0:1]),
         (None, lambda: mm(ho[...], flat[...].reshape(-1, flat.shape[2])), second[0:1, 0:1], second[1:2, 0:1]),
     )
     n_shard = lax.axis_size("shard")
     for i, (moment, product, straight, mixed) in enumerate(parts):
         at, size, offset = wins[i]
-        here = mo_win[...] if moment is None else cut(moment[:, at], size, offset, widths[i])
+
+        def mine(x):
+            x = cut(x, size, offset, widths[i])
+            return x.T if i in (1, 2) else x
+
+        here = mine(mo_win[...] if moment is None else moment[:, at])
         ortho = straight * here + mixed * product()
         whole = (weight_wins[i].shape[0] * n_shard, (wq, wk, wv, wo)[i].shape[1])
-        weight = cut(weight_wins[i][...], size, offset, widths[i])
-        nexts[i][...] = weight - muon_rate * math.sqrt(max(whole)) * ortho
+        nexts[i][...] = mine(weight_wins[i][...]) - muon_rate * math.sqrt(max(whole)) * ortho
 
 
 def update(h, hs, scal, m_out, moments, weights, n_rep, collective_id):
@@ -377,9 +426,10 @@
     vmem, any_ = pl.BlockSpec(memory_space=pltpu.VMEM), pl.BlockSpec(memory_space=pl.ANY)
     V = pltpu.VMEM
     sizes = [max(w, 128) for w in widths]
-    return pl.pallas_call(
+    shapes = [(w.shape[0], width) for w, width in zip(weights, widths)]
+    out = pl.pallas_call(
         update_kernel,
-        out_shape=[jax.ShapeDtypeStruct((w.shape[0], width), f32) for w, width in zip(weights, widths)],
+        out_shape=[jax.ShapeDtypeStruct(s[::-1] if i in (1, 2) else s, f32) for i, s in enumerate(shapes)],
         in_specs=[any_] * 2 + [vmem] * 4 + [any_] + [vmem] * 3 + [any_] * 5,
         out_specs=[vmem] * 4,
         scratch_shapes=[
@@ -392,6 +442,7 @@
         + [pltpu.SemaphoreType.DMA((2,)), pltpu.SemaphoreType.DMA((6,))],
         name="update",
     )(h, h_pair, hs, hs_come, scal, scal_come, m_out, *moments, *weights)
+    return out[0], out[1].T, out[2].T, out[3]
 
 
 HEAD_SIZE = 64
@@ -443,16 +494,16 @@
 
 
 class Gather:
-    def __init__(self, links, name, full, half, first=None):
-        self.links, self.name, self.full, self.half, self.first = links, name, full, half, first
+    def __init__(self, links, name, full, part, half, first=None):
+        self.links, self.name, self.full, self.part, self.half, self.first = links, name, full, part, half, first
 
     def line(self, way, k):
-        at = self.full.at[(self.links.shard - way * k,) + self.links.where()]
+        at = self.full.at[(self.links.shard - way * k,) + self.links.where() + self.part]
         src = self.first if k == 0 and self.first is not None else at
         return self.links.remote(src, at, (self.name, "l", way, k), self.links.rep, self.links.shard + way)
 
     def came(self, way, k):
-        at = self.full.at[(self.links.shard - way * (k + 1),) + self.links.where()]
+        at = self.full.at[(self.links.shard - way * (k + 1),) + self.links.where() + self.part]
         return self.links.remote(at, at, (self.name, "l", way, k), self.links.rep, self.links.shard)
 
     def plane(self, way, k, h, step):
@@ -478,13 +529,12 @@
                         @pl.when(links.goes(way, k + 1))
                         def _():
                             self.line(way, k + 1).start()
-                else:
-                    for h in range(2):
+                for h in range(2):
+                    if step > 0:
                         self.plane(way, k, h, step - 1).wait_recv()
-                if step < links.n_bits:
-                    for h in range(2):
+                    if step < links.n_bits:
                         self.plane(way, k, h, step).start()
-                elif then is not None:
+                if step == links.n_bits and then is not None:
                     then(links.shard - way * (k + 1))
 
     def drain(self):
@@ -503,11 +553,13 @@
 
 
 class Reduce:
-    def __init__(self, links, name, part, bufs, zbuf, gpiece, mpiece, moment, sums, wholes, half, keep_sem):
-        self.links, self.name, self.part, self.bufs, self.zbuf = links, name, part, bufs, zbuf
-        self.gpiece, self.mpiece, self.moment, self.sums, self.half = gpiece, mpiece, moment, sums, half
-        self.whole = Gather(links, name + "m", wholes, half, mpiece)
-        self.keep = lambda: pltpu.make_async_copy(gpiece, sums.at[links.where()], keep_sem)
+    def __init__(self, links, name, refs, region, half, keep_sem):
+        self.links, self.name, self.region, self.half = links, name, region, half
+        self.part, self.bufs, self.zbuf, self.gpiece, self.mpiece, self.moment, self.sums, wholes = refs
+        self.whole = Gather(links, name + "m", wholes, region, half, self.mpiece.at[region])
+        self.keep = lambda: pltpu.make_async_copy(
+            self.gpiece.at[region], self.sums.at[links.where() + region], keep_sem
+        )
 
     def dest(self, k):
         return lax.rem(self.links.shard + 1 + k, self.links.n_shard)
@@ -519,7 +571,7 @@
         return [0] + self.links.orders[h]
 
     def cut(self, h, step):
-        return (slice(None), slice(None)) if step == 0 else self.half[h]
+        return self.region if step == 0 else self.half[h]
 
     def send(self, k, h, step):
         links, o = self.links, self.order(h)
@@ -552,10 +604,11 @@
 
     def send_line(self, k):
         links, d = self.links, self.dest(k)
-        return links.remote(self.bufs[-1].at[d], self.zbuf.at[links.shard], (self.name, "z", k), links.rep, d)
+        src, into = self.bufs[-1].at[(d,) + self.region], self.zbuf.at[(links.shard,) + self.region]
+        return links.remote(src, into, (self.name, "z", k), links.rep, d)
 
     def come_line(self, k):
-        links, at = self.links, self.zbuf.at[self.origin(k)]
+        links, at = self.links, self.zbuf.at[(self.origin(k),) + self.region]
         return links.remote(at, at, (self.name, "z", k), links.rep, links.shard)
 
     def start(self, k):
@@ -585,12 +638,12 @@
         links = self.links
         for k in range(links.n_shard - 1):
             self.come_line(k).wait_recv()
-        acc = self.bufs[-1][links.shard].astype(F32)
+        acc = self.bufs[-1][(links.shard,) + self.region].astype(F32)
         for k in range(links.n_shard - 1):
-            acc = acc + self.zbuf[self.origin(k)].astype(F32)
+            acc = acc + self.zbuf[(self.origin(k),) + self.region].astype(F32)
         g = acc.astype(B16)
-        self.gpiece[...] = g
-        self.mpiece[...] = (decay * self.moment[...] + g.astype(F32)).astype(B16)
+        self.gpiece[self.region] = g
+        self.mpiece[self.region] = (decay * self.moment[self.region] + g.astype(F32)).astype(B16)
         self.whole.start()
         for h in range(2):
             self.gather_sum(h, 0).start()
@@ -667,14 +720,14 @@
 
 
 def bits_of(r, n_bits):
-    return tuple((r >> b) & 1 for b in reversed(range(n_bits)))
+    return tuple(lax.rem(lax.div(r, 1 << b), 2) if isinstance(r, jax.Array) else (r >> b) & 1 for b in reversed(range(n_bits)))
 
 
 def layer_kernel(
     n_rep, n_shard, decay,
-    tok, cot, seg_col, seg_row, frequency, gain, w_query, w_key, w_value, w_outproj, m_query, m_key, m_value, m_outproj,
+    tok_hbm, cot_hbm, seg_row, frequency, gain, w_query, w_key, w_value, w_outproj, m_query, m_key, m_value, m_outproj,
     out, grad_tok, sums_in, sums_out, wholes_in, wholes_out, gain_out,
-    w_in, w_out, gain_full, xn, inv_ref, q, dattn, attn_t, attn, dqkv, dxn, row_acc, kx, vx, kxt, vxt, dk_acc, dv_acc,
+    tok, cot, w_in, w_out, gain_full, xn, inv_ref, q, dattn, attn_t, attn, dqkv, dxn, row_acc, kx, vx, kxt, vxt, dk_acc, dv_acc,
     bias, cosine, sine, inv_l, part_in, part_out, gain_acc, gain_come, gain_line, moment_in, moment_out,
     zbuf_in, gp_in, mp_in, zbuf_out, gp_out, mp_out, load_sem, keep_sem, send, recv, *bufs,
 ):
@@ -690,64 +743,79 @@
     nb = n_rep.bit_length() - 1
     own_in, own_out = width // n_shard, q_width // n_shard
     rows_in, cols_out = own_in // n_rep, width // n_rep
-    spans_in = ((0, q_width), (q_width, kv_width), (q_width + kv_width, kv_width))
+    all_in = w_in.shape[-1]
+    chunk, q_part, kv_part = all_in // 2, q_width // 2, kv_width // 2
+    places = [
+        (i, c * size, c * chunk + first, size)
+        for c in range(2)
+        for i, (first, size) in enumerate(((0, q_part), (q_part, kv_part), (q_part + kv_part, kv_part)))
+    ]
 
     links = Links(n_rep, n_shard, send, recv)
     me, rep = links.shard, links.rep
-    all_in = w_in.shape[-1]
-    half_in = [(slice(None), pl.ds(h * (all_in // 2), all_in // 2)) for h in range(2)]
-    half_out = [(pl.ds(h * (own_out // 2), own_out // 2), slice(None)) for h in range(2)]
-    get_in, get_out = Gather(links, "wi", w_in, half_in), Gather(links, "wo", w_out, half_out)
-    sum_in = Reduce(links, "i", part_in, bufs[:nb], zbuf_in, gp_in, mp_in, moment_in, sums_in, wholes_in, half_in, keep_sem.at[0])
-    sum_out = Reduce(links, "o", part_out, bufs[nb:], zbuf_out, gp_out, mp_out, moment_out, sums_out, wholes_out, half_out, keep_sem.at[1])
+    both = slice(None)
+    part_cols = [(both, pl.ds(c * chunk, chunk)) for c in range(2)]
+    half_cols = [[(both, pl.ds(c * chunk + h * (chunk // 2), chunk // 2)) for h in range(2)] for c in range(2)]
+    half_in = [(both, pl.ds(h * chunk, chunk)) for h in range(2)]
+    half_out = [(pl.ds(h * (own_out // 2), own_out // 2), both) for h in range(2)]
+    get_in, get_out = Gather(links, "wi", w_in, (both, both), half_in), Gather(links, "wo", w_out, (both, both), half_out)
+    refs_in = (part_in, bufs[:nb], zbuf_in, gp_in, mp_in, moment_in, sums_in, wholes_in)
+    refs_out = (part_out, bufs[nb:], zbuf_out, gp_out, mp_out, moment_out, sums_out, wholes_out)
+    sum_in = [Reduce(links, f"i{c}", refs_in, part_cols[c], half_cols[c], keep_sem.at[c]) for c in range(2)]
+    sum_out = Reduce(links, "o", refs_out, (both, both), half_out, keep_sem.at[2])
     sum_gain = GainSum(links, gain_acc, gain_come, gain_line)
 
+    ws, ms = (w_query, w_key, w_value), (m_query, m_key, m_value)
     loads = [
-        pltpu.make_async_copy(w, dxn.at[pl.ds(0, own_in), pl.ds(at, size)], load_sem.at[i])
-        for i, ((at, size), w) in enumerate(zip(spans_in, (w_query, w_key, w_value)))
+        pltpu.make_async_copy(ws[i].at[:, pl.ds(at, size)], dxn.at[pl.ds(0, own_in), pl.ds(to, size)], load_sem.at[n])
+        for n, (i, at, to, size) in enumerate(places)
     ]
-    for load in loads:
+    early = [pltpu.make_async_copy(a, b, load_sem.at[7 + i]) for i, (a, b) in enumerate(((tok_hbm, tok), (cot_hbm, cot)))]
+    for load in loads + early:
         load.start()
     links.barrier()
+
+    def gain_line_copy(way, k):
+        at = gain_full.at[me - way * k]
+        return links.remote(gain if k == 0 else at, at, ("gf", way, k), rep, me + way)
+
+    def gain_came(way, k):
+        at = gain_full.at[me - way * (k + 1)]
+        return links.remote(at, at, ("gf", way, k), rep, me)
+
+    gain_full[me] = gain[...]
+    for way in WAYS:
+        @pl.when(links.goes(way, 0))
+        def _():
+            gain_line_copy(way, 0).start()
     for load in loads:
         load.wait()
     for r in range(n_rep):
         w_in[(me,) + bits_of(r, nb)] = dxn[r * rows_in : (r + 1) * rows_in, :all_in].astype(B16)
     get_in.start()
-    load_out = pltpu.make_async_copy(w_outproj, dxn.at[pl.ds(0, own_out), :], load_sem.at[3])
+    load_out = pltpu.make_async_copy(w_outproj, dxn.at[pl.ds(0, own_out), :], load_sem.at[6])
     load_out.start()
-
-    def gain_line_copy(way, k):
-        at = gain_full.at[me - way * k]
-        return links.remote(at, at, ("gf", way, k), rep, me + way)
-
-    def gain_came(way, k):
-        at = gain_full.at[me - way * (k + 1)]
-        return links.remote(at, at, ("gf", way, k), rep, me)
-
-    gain_full[me] = gain[...].astype(B16).astype(F32)
     load_out.wait()
     for r in range(n_rep):
         w_out[(me,) + bits_of(r, nb)] = dxn[:own_out, r * cols_out : (r + 1) * cols_out].astype(B16)
-    for way in WAYS:
-        @pl.when(links.goes(way, 0))
-        def _():
-            gain_line_copy(way, 0).start()
-    get_out.start()
     loads = [
-        pltpu.make_async_copy(m.at[span(rep, rows_in), :], moment_in.at[:, pl.ds(at, size)], load_sem.at[i])
-        for i, ((at, size), m) in enumerate(zip(spans_in, (m_query, m_key, m_value)))
-    ] + [pltpu.make_async_copy(m_outproj.at[:, span(rep, cols_out)], moment_out, load_sem.at[3])]
+        pltpu.make_async_copy(ms[i].at[span(rep, rows_in), pl.ds(at, size)], moment_in.at[:, pl.ds(to, size)], load_sem.at[n])
+        for n, (i, at, to, size) in enumerate(places)
+    ] + [pltpu.make_async_copy(m_outproj.at[:, span(rep, cols_out)], moment_out, load_sem.at[6])]
     for load in loads:
         load.start()
 
+    row_acc[...] = jnp.broadcast_to(seg_row[...].astype(F32), (row_acc.shape[1], seq)).T
+    own_seg = seg_row[...].astype(F32)
+
     def masks(i):
         r = span(i, rows)
+        seg_col = row_acc[r, :1]
         key = lax.broadcasted_iota(jnp.int32, (rows, seq), 0) + i * rows
         query = lax.broadcasted_iota(jnp.int32, (rows, seq), 1)
-        seen = (key <= query) & (seg_col[r, :] == seg_row[...])
+        seen = (key <= query) & (seg_col == own_seg)
         bias[r, :] = jnp.where(seen, 0.0, -1e30)
-        start = jnp.sum((seg_row[...] < seg_col[r, :]).astype(F32), 1, keepdims=True)
+        start = jnp.sum(jnp.where(own_seg < seg_col, 1.0, 0.0), 1, keepdims=True)
         at = lax.broadcasted_iota(jnp.int32, (rows, 1), 0) + i * rows
         angle = (at.astype(F32) - start) * frequency[...]
         lane = lax.rem(lax.broadcasted_iota(jnp.int32, (rows, pair), 1), HEAD_SIZE)
@@ -758,7 +826,9 @@
         inv = lax.rsqrt(jnp.mean(x * x, -1, keepdims=True) + norm_eps)
         inv_ref[r, :] = jnp.broadcast_to(inv, (rows, 128))
 
+    early[0].wait()
     tiles(seq // rows, masks)
+    early[1].wait()
 
     for k in range(n_shard - 1):
         for way in WAYS:
@@ -790,78 +860,99 @@
         tiles(all_in // TILE, columns)
 
     project(me, True)
-    items = [(get_in, k) for k in range(n_shard - 1)] + [(get_out, k) for k in range(n_shard - 1)]
+    items = [(get_in, k, k) for k in range(n_shard - 1)] + [(get_out, k, n_shard + k) for k in range(n_shard - 1)]
 
     def gather_time(t):
-        for i, (gather, k) in enumerate(items):
-            if 0 <= t - i <= nb:
-                gather.event(k, t - i, project if gather is get_in else None)
+        for gather, k, at in items:
+            if 0 <= t - at <= nb:
+                gather.event(k, t - at, project if gather is get_in else None)
 
     first_phase = n_shard - 1 + nb
     for t in range(first_phase):
         gather_time(t)
-    later = list(range(first_phase, len(items) + nb))
+        if t == 1:
+            get_out.start()
+    later = list(range(first_phase, items[-1][2] + nb + 1))
 
     def tables():
         c, s = cosine[...], sine[...]
         return jnp.concatenate([c] * (TILE // pair), 1), jnp.concatenate([s] * (TILE // pair), 1)
 
     def query_tile(i):
-        at = span(i, TILE)
-        x = dxn[:, at]
+        per = q_part // TILE
+        x = dxn[:, pl.ds(pl.multiple_of(lax.div(i, per) * chunk + lax.rem(i, per) * TILE, TILE), TILE)]
         c, s = tables()
-        q[:, at] = (x * c + swap_halves(x) * s).astype(B16)
+        q[:, span(i, TILE)] = (x * c + swap_halves(x) * s).astype(B16) * B16(scale)
 
     tiles(q_width // TILE, query_tile)
     low = lax.broadcasted_iota(jnp.int32, (seq, pair), 1) < HEAD_SIZE
 
-    def split(x, into, into_t):
+    def split(x, into, into_t, shrink):
         for g in range(kv_heads):
             two = x[:, (g // 2) * pair : (g // 2 + 1) * pair].astype(B16).astype(F32)
             other = pltpu.roll(two, HEAD_SIZE, 1)
             first, second = (two, other) if g % 2 == 0 else (other, two)
-            lo, hi = jnp.where(low, first, 0.0).astype(B16), jnp.where(low, 0.0, second).astype(B16)
-            into[g, 0], into[g, 1] = lo, hi
-            into_t[g, 0], into_t[g, 1] = lo.T, hi.T
-
-    for first, into, into_t, turned in ((q_width, kx, kxt, True), (q_width + kv_width, vx, vxt, False)):
-        x = dxn[:, first : first + kv_width]
+            sides = jnp.where(low, first, 0.0).astype(B16), jnp.where(low, 0.0, second).astype(B16)
+            for b in range(n_tok):
+                for side in range(2):
+                    at = slice((2 * b + side) * TILE, (2 * b + side + 1) * TILE)
+                    part = sides[side][b * TILE : (b + 1) * TILE]
+                    into[g, at, :] = part
+                    into_t[g, :, at] = part.T * B16(shrink)
+
+    for first, into, into_t, turned in ((q_part, kx, kxt, True), (q_part + kv_part, vx, vxt, False)):
+        x = jnp.concatenate([dxn[:, c * chunk + first : c * chunk + first + kv_part] for c in range(2)], 1)
         if turned:
             c, s = tables()
             x = x * c + swap_halves(x) * s
-        split(x, into, into_t)
+        split(x, into, into_t, scale if turned else 1.0)
 
     def blocks():
         for b in range(n_tok):
-            yield slice(b * TILE, (b + 1) * TILE), slice(max(b - 1, 0) * TILE, (b + 1) * TILE)
-
-    def forward(p):
-        for i, t in enumerate(later):
-            @pl.when(p == min(1 + (i * pairs) // (2 * len(later)) * 2, pairs - 1))
+            first = max(b - 1, 0)
+            yield b, slice(b * TILE, (b + 1) * TILE), slice(2 * first * TILE, 2 * (b + 1) * TILE), range(first, b + 1)
+
+    def tile_of(x, j):
+        return x[j * TILE : (j + 1) * TILE]
+
+    together = 2
+
+    def forward(i):
+        for n, t in enumerate(later):
+            @pl.when(i == min(1 + n, pairs // together))
             def _():
                 gather_time(t)
 
-        g = lax.div(p, per_group)
-        lanes = span(p, pair)
-        for qs, ks in blocks():
-            q_b, mask, a_t = q[qs, lanes], bias[ks, qs], None
+        here = [(i * together + u, *block) for u in range(together) for block in blocks()]
+        scores = [nt(kx[lax.div(p, per_group), rs, :], q[qs, span(p, pair)]) for p, b, qs, rs, keys in here]
+        probs = []
+        for (p, b, qs, rs, keys), score in zip(here, scores):
+            grown = [
+                jnp.exp(tile_of(score, 2 * j + side) + bias[key * TILE : (key + 1) * TILE, qs])
+                for j, key in enumerate(keys)
+                for side in range(2)
+            ]
+            inv = []
             for side in range(2):
-                grown = jnp.exp(nt(kx[g, side, ks, :], q_b) * scale + mask)
-                inv = 1.0 / jnp.sum(grown, 0, keepdims=True)
-                inv_l[p, side, :, qs] = inv
-                part = mm(vxt[g, side, :, ks], (grown * inv).astype(B16))
-                a_t = part if a_t is None else a_t + part
-            attn_t[lanes, qs] = a_t.astype(B16)
-            attn[qs, lanes] = a_t.T.astype(B16)
-
-    tiles(pairs, forward)
-
-    for r in range(n_rep):
-        c = slice(r * cols_out, (r + 1) * cols_out)
-        x = mm(attn_t[...], cot[:, c]).astype(B16)
+                inv.append(1.0 / sum(jnp.sum(x, 0, keepdims=True) for x in grown[side::2]))
+                inv_l[p, side, :, qs] = inv[side]
+            probs.append(jnp.concatenate([(x * inv[j % 2]).astype(B16) for j, x in enumerate(grown)], 0))
+        for (p, b, qs, rs, keys), prob in zip(here, probs):
+            a_t = mm(vxt[lax.div(p, per_group), :, rs], prob)
+            attn_t[span(p, pair), qs] = a_t.astype(B16)
+            attn[qs, span(p, pair)] = a_t.T.astype(B16)
+
+    tiles(pairs // together, forward)
+
+    def out_grad(r):
+        x = mm(attn_t[...], cot[:, span(r, cols_out)]).astype(B16)
         part_out[(slice(None),) + bits_of(r, nb)] = x.reshape(n_shard, own_out, cols_out)
+
+    tiles(n_rep, out_grad)
     for k in range(n_shard):
         sum_out.start(k)
+    for t in later[max(pairs // together - 1, 0) :]:
+        gather_time(t)
 
     def head_grad(s):
         x = None
@@ -877,13 +968,31 @@
             if 0 <= t - step < n_shard:
                 who.event(t - step, step)
 
-    out_times = list(range(n_shard + nb - 1))
+    def weight_grad(c):
+        cols = dqkv[:, c * chunk : (c + 1) * chunk]
+
+        def one(k):
+            s = sum_in[c].dest(k)
+            x = tn(xn[:, span(s, own_in)], cols).astype(B16)
+            part_in[(s,) + (both,) * nb + part_cols[c]] = x.reshape((2,) * nb + (rows_in, chunk))
+
+        tiles(n_shard, one)
+        for k in range(n_shard):
+            sum_in[c].start(k)
+
+    n_reduce, n_gather = n_shard + nb - 1, n_shard + nb
+
+    in_loop = (2 * n_reduce) // 3
 
     def backward(p):
-        for t in out_times:
-            @pl.when(p == min(2 + t, pairs - 1))
+        for t in range(in_loop):
+            @pl.when(p == 1 + (t * (pairs - 1)) // in_loop)
             def _():
                 reduce_time(sum_out, t)
+
+        @pl.when(p == pairs // 2)
+        def _():
+            weight_grad(0)
 
         g = lax.div(p, per_group)
         lanes = span(p, pair)
@@ -893,30 +1002,40 @@
             dk_acc[...] = jnp.zeros_like(dk_acc)
             dv_acc[...] = jnp.zeros_like(dv_acc)
 
-        for qs, ks in blocks():
-            q_b, d_b, mask, dq = q[qs, lanes], dattn[qs, lanes], bias[ks, qs], None
-            for side in range(2):
-                grown = jnp.exp(nt(kx[g, side, ks, :], q_b) * scale + mask)
-                prob = grown * inv_l[p, side, :, qs]
-                dp = nt(vx[g, side, ks, :], d_b)
-                inner = jnp.sum(prob * dp, 0, keepdims=True)
-                ds = (prob * (dp - inner) * scale).astype(B16)
-                dv_acc[side, ks, :] += mm(prob.astype(B16), d_b)
-                dk_acc[side, ks, :] += mm(ds, q_b)
-                part = mm(kxt[g, side, :, ks], ds)
-                dq = part if dq is None else dq + part
-            x = dq.T
-            dqkv[qs, lanes] = (x * cosine[qs, :] - swap_halves(x) * sine[qs, :]).astype(B16)
+        scores = [(nt(kx[g, rs, :], q[qs, lanes]), nt(vx[g, rs, :], dattn[qs, lanes])) for b, qs, rs, keys in blocks()]
+        grads = []
+        for (b, qs, rs, keys), (score, dp) in zip(blocks(), scores):
+            prob = [
+                jnp.exp(tile_of(score, 2 * j + side) + bias[key * TILE : (key + 1) * TILE, qs]) * inv_l[p, side, :, qs]
+                for j, key in enumerate(keys)
+                for side in range(2)
+            ]
+            inner = [
+                sum(jnp.sum(x * tile_of(dp, 2 * j + side), 0, keepdims=True) for j, x in enumerate(prob[side::2]))
+                for side in range(2)
+            ]
+            ds = [(x * (tile_of(dp, j) - inner[j % 2])).astype(B16) for j, x in enumerate(prob)]
+            grads.append((jnp.concatenate([x.astype(B16) for x in prob], 0), jnp.concatenate(ds, 0)))
+        for (b, qs, rs, keys), (prob, ds) in zip(blocks(), grads):
+            dv_acc[rs, :] += mm(prob, dattn[qs, lanes])
+            dk_acc[rs, :] += mm(ds, q[qs, lanes])
+            x = mm(kxt[g, :, rs], ds).T
+            half_pairs = pairs // 2
+            to = lax.div(p, half_pairs) * chunk + lax.rem(p, half_pairs) * pair
+            dqkv[qs, pl.ds(pl.multiple_of(to, pair), pair)] = (x * cosine[qs, :] - swap_halves(x) * sine[qs, :]).astype(B16)
 
         @pl.when(lax.rem(p, per_group) == per_group - 1)
         def _():
             def joined(acc):
-                return acc[0] + pltpu.roll(acc[1], HEAD_SIZE, 1)
+                both = [acc[j * TILE : (j + 1) * TILE, :] for j in range(2 * n_tok)]
+                return jnp.concatenate([both[2 * b] + pltpu.roll(both[2 * b + 1], HEAD_SIZE, 1) for b in range(n_tok)], 0)
 
             dk, dv = joined(dk_acc), joined(dv_acc)
             dk = dk * cosine[...] - swap_halves(dk) * sine[...]
-            for x, first in ((dk, q_width), (dv, q_width + kv_width)):
-                at = span(lax.div(g, 2) + first // pair, pair)
+            for x, first in ((dk, q_part), (dv, q_part + kv_part)):
+                half_groups = kv_heads // 2
+                to = lax.div(g, half_groups) * chunk + first + lax.div(lax.rem(g, half_groups), 2) * pair
+                at = pl.ds(pl.multiple_of(to, pair), pair)
                 odd = lax.rem(g, 2)
 
                 @pl.when(odd == 0)
@@ -930,14 +1049,9 @@
 
     tiles(pairs, backward)
 
-    def weight_grad(k):
-        s = sum_in.dest(k)
-        x = tn(xn[:, span(s, own_in)], dqkv[...]).astype(B16)
-        part_in[s] = x.reshape((2,) * nb + (rows_in, all_in))
-        sum_in.start(k)
-
-    for k in range(n_shard):
-        weight_grad(k)
+    weight_grad(1)
+    for load in loads:
+        load.wait()
 
     row_acc[...] = jnp.zeros_like(row_acc)
 
@@ -958,53 +1072,62 @@
         grad_tok[r, :] = (cot[r, :].astype(F32) + inv * (dxn[r, :] - normed * mean)).astype(B16)
 
     def output(r):
-        c = slice(r * cols_out, (r + 1) * cols_out)
+        c = span(r, cols_out)
         x = mm(attn[...], flat(w_out[(slice(None),) + bits_of(r, nb)]))
         out[:, c] = (tok[:, c].astype(F32) + x).astype(B16)
-
-    for load in loads:
-        load.wait()
-    input_grad(0)
-    sum_out.finish(decay)
-    for s in range(1, n_shard):
-        input_grad(s)
-        if s == n_shard // 2:
-            reduce_time(sum_in, 0)
-    sum_gain.send(0).start()
-    reduce_time(sum_in, 1)
-    tiles(seq // rows, token_grad)
 
     def gather_sums_time(who, t):
         for i in range(n_shard):
             if 0 <= t - i <= nb:
                 who.gather_event(i, t - i)
 
-    n_times = n_shard + nb
-    for r in range(n_rep):
-        output(r)
-        if r == n_rep // 2:
-            reduce_time(sum_in, 2)
-            gather_sums_time(sum_out, 0)
-    sum_gain.event(0)
-    done = 1
-    for t in range(3, n_shard + nb - 1):
-        reduce_time(sum_in, t)
-        if done < n_times:
-            gather_sums_time(sum_out, done)
-            done += 1
-        if t - 2 < nb:
-            sum_gain.event(t - 2)
-    for b in range(max(n_shard + nb - 3, 1), nb):
-        sum_gain.event(b)
-    sum_in.finish(decay)
-    gain_out[...] = sum_gain.end()
-    for t in range(n_times):
-        if done < n_times:
-            gather_sums_time(sum_out, done)
-            done += 1
-        gather_sums_time(sum_in, t)
-
-    for who in (get_in, get_out, sum_out, sum_in):
+    todo = []
+
+    def then(method, *args):
+        todo.append(functools.partial(method, *args))
+
+    def gain_end():
+        gain_out[...] = sum_gain.end()
+
+    out_end = n_reduce - in_loop
+    for u in range(3 * n_gather + n_reduce):
+        if u < out_end:
+            then(reduce_time, sum_out, in_loop + u)
+        if u < n_reduce:
+            then(reduce_time, sum_in[0], u)
+        if 0 <= u - 2 < n_reduce:
+            then(reduce_time, sum_in[1], u - 2)
+        if u == out_end + 1:
+            then(sum_out.finish, decay)
+        if u == n_reduce + 1:
+            then(sum_in[0].finish, decay)
+        if u == n_reduce + 3:
+            then(sum_in[1].finish, decay)
+        for who, lag in ((sum_in[0], n_reduce + 2), (sum_in[1], n_reduce + 4), (sum_out, out_end + 2)):
+            if 0 <= u - lag < n_gather:
+                then(gather_sums_time, who, u - lag)
+        if 0 <= u - n_reduce - 3 < nb:
+            then(sum_gain.event, u - n_reduce - 3)
+        if u == n_reduce + nb + 4:
+            then(gain_end)
+
+    def advance():
+        todo.pop(0)()
+
+    for s in range(n_shard):
+        advance()
+        input_grad(s)
+    sum_gain.send(0).start()
+    advance()
+    tiles(seq // rows, token_grad)
+    advance()
+    tiles(n_rep // 2, output)
+    advance()
+    tiles(n_rep // 2, lambda r: output(r + n_rep // 2))
+    while todo:
+        advance()
+
+    for who in (get_in, get_out, sum_out, *sum_in):
         who.drain()
     for way in WAYS:
         for k in range(n_shard - 1):
@@ -1025,12 +1148,11 @@
     own_in, own_out = width // n_shard, q_width // n_shard
     piece_in, piece_out = (own_in // n_rep, all_in), (own_out, width // n_rep)
     half = HEAD_SIZE // 2
-    frequency = rope_base ** (-2.0 * jnp.arange(half, dtype=F32) / HEAD_SIZE)
-    frequency = jnp.concatenate([frequency] * (pair // half))[None]
+    frequency = np.tile((rope_base ** (-2.0 * np.arange(half) / HEAD_SIZE)).astype(np.float32), pair // half)[None]
     vmem, any_ = pl.BlockSpec(memory_space=pltpu.VMEM), pl.BlockSpec(memory_space=pl.ANY)
     V, D = pltpu.VMEM, pltpu.SemaphoreType.DMA
     n_sems = (
-        2 * 2 * 2 * (n_shard - 1) * (1 + 2 * nb) + 2 * (n_shard * (1 + 2 * (nb - 1)) + n_shard - 1 + 2 * nb) + nb + 3 * n_shard
+        5 * 2 * (n_shard - 1) * (1 + 2 * nb) + 3 * (n_shard * (1 + 2 * (nb - 1)) + n_shard - 1 + 2 * nb) + nb + 3 * n_shard
     )
     bufs = [V((n_shard,) + (2,) * (nb - 1 - j) + piece, B16) for piece in (piece_in, piece_out) for j in range(nb)]
     shape = jax.ShapeDtypeStruct
@@ -1045,9 +1167,11 @@
             shape((n_shard,) + bits + piece_out, B16),
             shape((1, own_in), F32),
         ],
-        in_specs=[vmem] * 6 + [any_] * 8,
+        in_specs=[any_] * 2 + [vmem] * 3 + [any_] * 8,
         out_specs=[vmem] * 2 + [any_] * 4 + [vmem],
         scratch_shapes=[
+            V((seq, width), B16),
+            V((seq, width), B16),
             V((n_shard,) + bits + piece_in, B16),
             V((n_shard,) + bits + piece_out, B16),
             V((n_shard, 1, own_in), F32),
@@ -1060,12 +1184,12 @@
             V((seq, all_in), B16),
             V((seq, width), F32),
             V((seq, 128), F32),
-            V((kv_heads, 2, seq, pair), B16),
-            V((kv_heads, 2, seq, pair), B16),
-            V((kv_heads, 2, pair, seq), B16),
-            V((kv_heads, 2, pair, seq), B16),
-            V((2, seq, pair), F32),
-            V((2, seq, pair), F32),
+            V((kv_heads, 2 * seq, pair), B16),
+            V((kv_heads, 2 * seq, pair), B16),
+            V((kv_heads, pair, 2 * seq), B16),
+            V((kv_heads, pair, 2 * seq), B16),
+            V((2 * seq, pair), F32),
+            V((2 * seq, pair), F32),
             V((seq, seq), F32),
             V((seq, pair), F32),
             V((seq, pair), F32),
@@ -1083,8 +1207,8 @@
             V((n_shard,) + piece_out, B16),
             V(piece_out, B16),
             V(piece_out, B16),
-            D((4,)),
-            D((2,)),
+            D((9,)),
+            D((3,)),
             D((n_sems,)),
             D((n_sems,)),
         ]
@@ -1093,7 +1217,7 @@
             collective_id=collective_id, has_side_effects=True, vmem_limit_bytes=67_043_328
         ),
         name="layer",
-    )(tok, cot, seg[:, None], seg[None], frequency, gain[None], *weights, *moments)
+    )(tok, cot, seg[None], frequency, lax.reduce_precision(gain, 8, 7)[None], *weights, *moments)
 
 
 gain_rate = 0.2
@@ -1127,8 +1251,13 @@
     own_out, cols_out = sum_out.shape[-2:]
     m_out = m_out.reshape(n_shard, n_rep, own_out, cols_out)
     all_in = sum_in.shape[-1]
-    grads, moments_next, (mix, mix_kv, scales) = muon(
-        m_in.reshape(-1, all_in), m_out, sum_in.reshape(-1, all_in), sum_out.reshape(n_rep, own_out, cols_out), moments
+    grads, moments_next, (result, grad_tokens), (mix, mix_kv, scales) = muon(
+        m_in.reshape(-1, all_in),
+        m_out,
+        sum_in.reshape(-1, all_in),
+        sum_out.reshape(n_rep, own_out, cols_out),
+        moments,
+        (result, grad_tokens),
     )
     updated = update(mix, mix_kv, scales, m_out, moments_next, weights, n_rep, 1)
     return (

time: 279 us -> 256 us (0.918)
  Pallas kernels: 268 us -> 253 us
  local copies, waits for them, and re-layouts: 9.18 us -> 0.6 us
    pallas_call x1, Pallas kernels: 198 us -> 186 us  [layer(): pl.pallas_call(functools.partial(layer_kernel, n_rep, n_shard, decay), ou...]
    unnamed x15 -> x7, local copies, waits for them, and re-layouts: 7.64 us -> 0.6 us
    pallas_call x2, Pallas kernels: 67.7 us -> 63.9 us  [the longest x1 58.6 us: muon(): pl.pallas_call(muon_kernel, out_shape=own + own + [jax.ShapeDtypeStruct(p...]
where the time goes in v5:
time: 256 us
  Pallas kernels  253 us (99%)
    pallas_call x1, Pallas kernels, layer(): pl.pallas_call(functools.partial(layer_kernel, n_rep, n_shard, decay), ou...  186 us
    pallas_call x1, Pallas kernels, muon(): pl.pallas_call(muon_kernel, out_shape=own + own + [jax.ShapeDtypeStruct(p...  58.6 us
    pallas_call x1, Pallas kernels, update(): pl.pallas_call(update_kernel, out_shape=[jax.ShapeDtypeStruct(s[::-1] if...  5.26 us

profile of v5, /device:TPU:0, one launch (start us, length us, event | category | flops | bytes accessed | tf_op | source)
XLA Modules:
  0.0 256.1 jit_solution(4679226197902794175)
XLA Ops:
  0.7 1.3 reduce_precision.3
  1.9 186.4 %layer.1 = (bf16[512,2048]{1,0:T(8,128)(2,1)}, bf16[512,2048]{1,0:T(8,128)(2,1)}, bf16[2,2,2,64,1536]{4,3,2,1,0:T(8,128)(2,1)}, bf16[2,2,2,256,256]{4,3,2,1,0:T(...) custom-call(bf16[512,2048]{1,0:T(8,128)(2,1)} %bitcast.15, ...), custom_call_target="tpu_custom_call" | custom-call | tf_op jit(solution)/shard_map/layer/pallas_call | solution.py:1159
  188.4 58.6 %muon.1 = (f32[512,1024]{1,0:T(8,128)}, f32[512,256]{1,0:T(8,128)}, f32[512,256]{1,0:T(8,128)}, f32[256,2048]{1,0:T(8,128)}, f32[512,1024]{1,0:T(8,128)}, /*inde...) custom-call(bf16[2048,1536]{1,0:T(8,128)(2,1)} %bitcast.14, ...), custom_call_target="tpu_custom_call" | custom-call | tf_op jit(solution)/shard_map/muon/pallas_call | solution.py:283
  247.0 2.7 %swap.1 = (bf16[256,1024]{1,0:T(8,128)(2,1)}, bf16[256,256]{1,0:T(8,128)(2,1)}, f32[8,128]{1,0:T(8,128)}) custom-call(bf16[1024,1024]{1,0:T(8,128)(2,1)} %get-tuple-element.57.h, bf16[256,256]{1,0:T(8,128)(2,1)} %get-tuple-element.58.hs, f32[8,128]{1,0:T(8,128)} %get-tuple-element.59.scal), custom_call_target="tpu_custom_call" | custom-call | tf_op jit(solution)/shard_map/swap/pallas_call | solution.py:340
  249.6 0.0 copy-start
  249.7 0.0 copy-start.1
  249.7 0.0 copy-start.2
  249.7 5.3 %update.1 = (f32[512,128]{1,0:T(8,128)}, f32[32,512]{1,0:T(8,128)}, f32[32,512]{1,0:T(8,128)}, f32[256,256]{1,0:T(8,128)}) custom-call(bf16[1024,1024]{1,0:T(8,128)(2,1)} %get-tuple-element.57.h, bf16[256,1024]{1,0:T(8,128)(2,1)} %get-tuple-element.60.h_pair, bf16[256,256]{1,0:T(8,128)(2,1)} %get-tuple-element.58.hs, ...), custom_call_target="tpu_custom_call" | custom-call | tf_op jit(solution)/shard_map/update/pallas_call | solution.py:430
  254.9 0.0 copy-done
  255.0 0.0 copy-done.1
  255.0 0.0 copy-done.2
  255.0 0.6 multiply_subtract_fusion
  255.6 0.6 copy.32
Async XLA Ops:
  249.6 5.3 %copy-start = (f32[512]{0:T(512)S(1)}, f32[512]{0:T(512)}, u32[]{:S(2)}) copy-start(f32[512]{0:T(512)} %param.17) | copy-start | bytes 6148
  249.7 5.3 %copy-start.1 = (f32[1,512]{1,0:T(1,128)S(1)}, f32[1,512]{1,0:T(1,128)}, u32[]{:S(2)}) copy-start(f32[1,512]{1,0:T(1,128)} %get-tuple-element.52) | copy-start | bytes 6148
  249.7 5.3 %copy-start.2 = (f32[512]{0:T(512)S(1)}, f32[512]{0:T(512)}, u32[]{:S(2)}) copy-start(f32[512]{0:T(512)} %param.22) | copy-start | bytes 6148

commit v6 on v5

--- a/solution.py
+++ b/solution.py
@@ -48,11 +48,20 @@
 class Iterate:
     def __init__(self, e, ebf, k, kbf, h, hbf, fbf):
         self.e, self.ebf, self.k, self.kbf, self.h, self.hbf, self.fbf = e, ebf, k, kbf, h, hbf, fbf
-        self.n = e.shape[0]
-        self.wide = min(512, self.n)
-        self.diag = min(256, self.n)
-        self.columns = [slice(c, c + self.wide) for c in range(0, self.n, self.wide)]
-        self.squares = [slice(d, d + self.diag) for d in range(0, self.n, self.diag)]
+        self.n = n = e.shape[0]
+        self.diag = min(256, n)
+        self.squares = [slice(d, d + self.diag) for d in range(0, n, self.diag)]
+        half = n // 2
+        if n <= 256:
+            self.blocks = [(slice(0, n), slice(0, n))]
+        else:
+            self.blocks = [(slice(0, n), slice(0, half)), (slice(half, n), slice(half, n))]
+
+    def put(self, ref, at, value):
+        r, c = at
+        ref[r, c] = value.astype(jnp.bfloat16)
+        if r != c:
+            ref[c, c.stop : r.stop] = ref[c.stop : r.stop, c].T
 
     def eye(self):
         shape = (self.diag, self.diag)
@@ -74,37 +83,36 @@
     def start(self):
         norm = jnp.sqrt(self.trace(self.e)) + 1e-06
         scale = 1.0 / (norm * norm)
-        for c in self.columns:
-            x = self.e[:, c] * scale
-            self.e[:, c] = x
-            self.ebf[:, c] = x.astype(jnp.bfloat16)
+        for at in self.blocks:
+            x = self.e[at] * scale
+            self.e[at] = x
+            self.put(self.ebf, at, x)
         return self.centre(jnp.zeros((1, 1), jnp.float32)), 1.0 / norm
 
-    def polynomial(self, s, c):
+    def polynomial(self, s, at):
         p1 = coef_b + 2.0 * coef_c * s
-        f = p1 * self.e[:, c] + coef_c * mm(self.ebf[...], self.ebf[:, c])
-        self.fbf[:, c] = f.astype(jnp.bfloat16)
+        self.put(self.fbf, at, p1 * self.e[at] + coef_c * mm(self.ebf[at[0], :], self.ebf[:, at[1]]))
 
     def first(self):
-        for c in self.columns:
-            f = self.fbf[:, c]
-            self.h[:, c] = f.astype(jnp.float32)
-            self.hbf[0, :, c] = f
-
-    def grow(self, p0, q, c, now, later):
-        new = p0 * self.h[:, c] + q * self.fbf[:, c].astype(jnp.float32) + mm(self.fbf[...], self.hbf[now, :, c])
-        self.h[:, c] = new
-        self.hbf[later, :, c] = new.astype(jnp.bfloat16)
-
-    def inner(self, p0, s, c):
-        new = p0 * self.e[:, c] + s * self.fbf[:, c].astype(jnp.float32) + mm(self.fbf[...], self.ebf[:, c])
-        self.k[:, c] = new
-        self.kbf[:, c] = new.astype(jnp.bfloat16)
-
-    def outer(self, p0, beta, c):
-        new = p0 * self.k[:, c] + beta * self.fbf[:, c].astype(jnp.float32) + mm(self.fbf[...], self.kbf[:, c])
-        self.e[:, c] = new
-        self.ebf[:, c] = new.astype(jnp.bfloat16)
+        for at in self.blocks:
+            f = self.fbf[at].astype(jnp.float32)
+            self.h[at] = f
+            self.put(self.hbf.at[0], at, f)
+
+    def grow(self, p0, q, at, now, later):
+        new = p0 * self.h[at] + q * self.fbf[at].astype(jnp.float32) + mm(self.fbf[at[0], :], self.hbf[now, :, at[1]])
+        self.h[at] = new
+        self.put(self.hbf.at[later], at, new)
+
+    def inner(self, p0, s, at):
+        new = p0 * self.e[at] + s * self.fbf[at].astype(jnp.float32) + mm(self.fbf[at[0], :], self.ebf[:, at[1]])
+        self.k[at] = new
+        self.put(self.kbf, at, new)
+
+    def outer(self, p0, beta, at):
+        new = p0 * self.k[at] + beta * self.fbf[at].astype(jnp.float32) + mm(self.fbf[at[0], :], self.kbf[:, at[1]])
+        self.e[at] = new
+        self.put(self.ebf, at, new)
 
 
 def muon_kernel(*refs):
@@ -157,7 +165,7 @@
     def _():
         flat.start()
 
-    for copy in kv + own_sums + own + passing:
+    for copy in kv + own_sums + own:
         copy.start()
 
     mine = span(shard, own_in)
@@ -177,6 +185,8 @@
 
     for copy in kv + own_sums + own:
         copy.wait()
+    for copy in passing:
+        copy.start()
     for i in range(4):
         if i < 3:
             def update(j, i=i, first=firsts[i][0], width=firsts[i][1]):
@@ -216,7 +226,8 @@
     for a, b in zip(passing, leaving):
         a.wait()
         b.start()
-    tiles(n // big.wide, lambda j: big.e.__setitem__((slice(None), span(j, big.wide)), nt(x[...], x[span(j, big.wide), :])))
+    for r, c in big.blocks:
+        big.e[r, c] = nt(x[r, :], x[c, :])
     small.e[...] = tn(small_m[...], small_m[...])
     s, inv = big.start()
     ss, sinv = small.start()
@@ -228,10 +239,10 @@
         sp0 = coef_a + ss * (coef_b + coef_c * ss)
 
         def each(method, *args):
-            for i, c in enumerate(big.columns):
+            for i, c in enumerate(big.blocks):
                 getattr(big, method)(*[a[0] for a in args], c, *extra)
                 if i == 0:
-                    for d in small.columns:
+                    for d in small.blocks:
                         getattr(small, method)(*[a[1] for a in args], d, *extra)
 
         extra = ()
@@ -362,8 +373,10 @@
     return x if size == width else pltpu.roll(x, lax.rem(size - offset, size), 1)[:, :width]
 
 
-def update_kernel(h, h_pair, hs, hs_come, scal, scal_come, m_out, mq, mk, mv, mo, wq, wk, wv, wo, *refs):
-    nexts, (hq, ho, flat, mo_win), weight_wins, (h_sem, sem) = refs[:4], refs[4:8], refs[8:12], refs[12:]
+def update_kernel(h, h_pair, hs, hs_come, scal, scal_come, m_out, mq_hbm, mk_hbm, mv_hbm, mo, wq, wk, wv, wo, *refs):
+    nexts, (hq, ho, flat, mo_win), weight_wins, (mq, mk, mv), (h_sem, sem) = (
+        refs[:4], refs[4:8], refs[8:12], refs[12:15], refs[15:]
+    )
     f32, b16 = jnp.float32, jnp.bfloat16
     rep, shard = lax.axis_index("rep"), lax.axis_index("shard")
     even = lax.rem(rep, 2) == 0
@@ -373,6 +386,9 @@
     copies = [
         pltpu.make_async_copy(m_out.at[:, rep], flat, sem.at[4]),
         pltpu.make_async_copy(mo.at[:, wins[3][0]], mo_win, sem.at[5]),
+        pltpu.make_async_copy(mq_hbm, mq, sem.at[6]),
+        pltpu.make_async_copy(mk_hbm, mk, sem.at[7]),
+        pltpu.make_async_copy(mv_hbm, mv, sem.at[8]),
     ] + [pltpu.make_async_copy(w.at[:, wins[i][0]], weight_wins[i], sem.at[i]) for i, w in enumerate((wq, wk, wv, wo))]
     for copy in copies:
         copy.start()
@@ -430,7 +446,7 @@
     out = pl.pallas_call(
         update_kernel,
         out_shape=[jax.ShapeDtypeStruct(s[::-1] if i in (1, 2) else s, f32) for i, s in enumerate(shapes)],
-        in_specs=[any_] * 2 + [vmem] * 4 + [any_] + [vmem] * 3 + [any_] * 5,
+        in_specs=[any_] * 2 + [vmem] * 4 + [any_] * 9,
         out_specs=[vmem] * 4,
         scratch_shapes=[
             V((widths[0], h.shape[1]), b16),
@@ -439,7 +455,8 @@
             V((own_out, sizes[3]), f32),
         ]
         + [V((w.shape[0], size), f32) for w, size in zip(weights, sizes)]
-        + [pltpu.SemaphoreType.DMA((2,)), pltpu.SemaphoreType.DMA((6,))],
+        + [V(m.shape, f32) for m in moments[:3]]
+        + [pltpu.SemaphoreType.DMA((2,)), pltpu.SemaphoreType.DMA((9,))],
         name="update",
     )(h, h_pair, hs, hs_come, scal, scal_come, m_out, *moments, *weights)
     return out[0], out[1].T, out[2].T, out[3]
@@ -494,17 +511,17 @@
 
 
 class Gather:
-    def __init__(self, links, name, full, part, half, first=None):
-        self.links, self.name, self.full, self.part, self.half, self.first = links, name, full, part, half, first
-
-    def line(self, way, k):
-        at = self.full.at[(self.links.shard - way * k,) + self.links.where() + self.part]
-        src = self.first if k == 0 and self.first is not None else at
-        return self.links.remote(src, at, (self.name, "l", way, k), self.links.rep, self.links.shard + way)
-
-    def came(self, way, k):
-        at = self.full.at[(self.links.shard - way * (k + 1),) + self.links.where() + self.part]
-        return self.links.remote(at, at, (self.name, "l", way, k), self.links.rep, self.links.shard)
+    def __init__(self, links, name, full, half, first=None):
+        self.links, self.name, self.full, self.half, self.first = links, name, full, half, first
+
+    def line(self, way, k, h):
+        at = self.full.at[(self.links.shard - way * k,) + self.links.where() + self.half[h]]
+        src = self.first.at[self.half[h]] if k == 0 and self.first is not None else at
+        return self.links.remote(src, at, (self.name, "l", way, k, h), self.links.rep, self.links.shard + way)
+
+    def came(self, way, k, h):
+        at = self.full.at[(self.links.shard - way * (k + 1),) + self.links.where() + self.half[h]]
+        return self.links.remote(at, at, (self.name, "l", way, k, h), self.links.rep, self.links.shard)
 
     def plane(self, way, k, h, step):
         links = self.links
@@ -516,19 +533,26 @@
         for way in WAYS:
             @pl.when(self.links.goes(way, 0))
             def _():
-                self.line(way, 0).start()
+                for h in range(2):
+                    self.line(way, 0, h).start()
+
+    def arrive(self, k):
+        links = self.links
+        for way in WAYS:
+            @pl.when(links.comes(way, k))
+            def _():
+                for h in range(2):
+                    self.came(way, k, h).wait_recv()
+                    if k + 1 < links.n_shard - 1:
+                        @pl.when(links.goes(way, k + 1))
+                        def _():
+                            self.line(way, k + 1, h).start()
 
     def event(self, k, step, then=None):
         links = self.links
         for way in WAYS:
             @pl.when(links.comes(way, k))
             def _():
-                if step == 0:
-                    self.came(way, k).wait_recv()
-                    if k + 1 < links.n_shard - 1:
-                        @pl.when(links.goes(way, k + 1))
-                        def _():
-                            self.line(way, k + 1).start()
                 for h in range(2):
                     if step > 0:
                         self.plane(way, k, h, step - 1).wait_recv()
@@ -543,7 +567,8 @@
             for k in range(links.n_shard - 1):
                 @pl.when(links.goes(way, k))
                 def _():
-                    self.line(way, k).wait_send()
+                    for h in range(2):
+                        self.line(way, k, h).wait_send()
 
                 @pl.when(links.comes(way, k))
                 def _():
@@ -556,7 +581,7 @@
     def __init__(self, links, name, refs, region, half, keep_sem):
         self.links, self.name, self.region, self.half = links, name, region, half
         self.part, self.bufs, self.zbuf, self.gpiece, self.mpiece, self.moment, self.sums, wholes = refs
-        self.whole = Gather(links, name + "m", wholes, region, half, self.mpiece.at[region])
+        self.whole = Gather(links, name + "m", wholes, half, self.mpiece)
         self.keep = lambda: pltpu.make_async_copy(
             self.gpiece.at[region], self.sums.at[links.where() + region], keep_sem
         )
@@ -726,8 +751,8 @@
 def layer_kernel(
     n_rep, n_shard, decay,
     tok_hbm, cot_hbm, seg_row, frequency, gain, w_query, w_key, w_value, w_outproj, m_query, m_key, m_value, m_outproj,
-    out, grad_tok, sums_in, sums_out, wholes_in, wholes_out, gain_out,
-    tok, cot, w_in, w_out, gain_full, xn, inv_ref, q, dattn, attn_t, attn, dqkv, dxn, row_acc, kx, vx, kxt, vxt, dk_acc, dv_acc,
+    out_hbm, grad_hbm, sums_in, sums_out, wholes_in, wholes_out, gain_out,
+    out, grad_tok,    tok, cot, w_in, w_out, gain_full, xn, inv_ref, q, dattn, attn_t, attn, dqkv, dxn, row_acc, kx, vx, kxt, vxt, dk_acc, dv_acc,
     bias, cosine, sine, inv_l, part_in, part_out, gain_acc, gain_come, gain_line, moment_in, moment_out,
     zbuf_in, gp_in, mp_in, zbuf_out, gp_out, mp_out, load_sem, keep_sem, send, recv, *bufs,
 ):
@@ -758,7 +783,7 @@
     half_cols = [[(both, pl.ds(c * chunk + h * (chunk // 2), chunk // 2)) for h in range(2)] for c in range(2)]
     half_in = [(both, pl.ds(h * chunk, chunk)) for h in range(2)]
     half_out = [(pl.ds(h * (own_out // 2), own_out // 2), both) for h in range(2)]
-    get_in, get_out = Gather(links, "wi", w_in, (both, both), half_in), Gather(links, "wo", w_out, (both, both), half_out)
+    get_in, get_out = Gather(links, "wi", w_in, half_in), Gather(links, "wo", w_out, half_out)
     refs_in = (part_in, bufs[:nb], zbuf_in, gp_in, mp_in, moment_in, sums_in, wholes_in)
     refs_out = (part_out, bufs[nb:], zbuf_out, gp_out, mp_out, moment_out, sums_out, wholes_out)
     sum_in = [Reduce(links, f"i{c}", refs_in, part_cols[c], half_cols[c], keep_sem.at[c]) for c in range(2)]
@@ -770,34 +795,49 @@
         pltpu.make_async_copy(ws[i].at[:, pl.ds(at, size)], dxn.at[pl.ds(0, own_in), pl.ds(to, size)], load_sem.at[n])
         for n, (i, at, to, size) in enumerate(places)
     ]
+    first = [
+        pltpu.make_async_copy(ws[i].at[span(rep, rows_in), pl.ds(at, size)], moment_in.at[:, pl.ds(to, size)], load_sem.at[9 + n])
+        for n, (i, at, to, size) in enumerate(places)
+    ] + [pltpu.make_async_copy(w_outproj.at[:, span(rep, cols_out)], moment_out, load_sem.at[15])]
     early = [pltpu.make_async_copy(a, b, load_sem.at[7 + i]) for i, (a, b) in enumerate(((tok_hbm, tok), (cot_hbm, cot)))]
-    for load in loads + early:
+    for load in first + loads + early:
         load.start()
+    gain_full[me] = gain[...].astype(B16).astype(F32)
     links.barrier()
 
     def gain_line_copy(way, k):
         at = gain_full.at[me - way * k]
-        return links.remote(gain if k == 0 else at, at, ("gf", way, k), rep, me + way)
+        return links.remote(at, at, ("gf", way, k), rep, me + way)
 
     def gain_came(way, k):
         at = gain_full.at[me - way * (k + 1)]
         return links.remote(at, at, ("gf", way, k), rep, me)
 
-    gain_full[me] = gain[...]
     for way in WAYS:
         @pl.when(links.goes(way, 0))
         def _():
             gain_line_copy(way, 0).start()
+    for load in first:
+        load.wait()
+    here = (me,) + links.where()
+    w_in[here] = moment_in[...].astype(B16)
+    get_in.start()
+    w_out[here] = moment_out[...].astype(B16)
     for load in loads:
         load.wait()
     for r in range(n_rep):
-        w_in[(me,) + bits_of(r, nb)] = dxn[r * rows_in : (r + 1) * rows_in, :all_in].astype(B16)
-    get_in.start()
+        @pl.when(rep != r)
+        def _():
+            w_in[(me,) + bits_of(r, nb)] = dxn[r * rows_in : (r + 1) * rows_in, :all_in].astype(B16)
+
     load_out = pltpu.make_async_copy(w_outproj, dxn.at[pl.ds(0, own_out), :], load_sem.at[6])
     load_out.start()
     load_out.wait()
     for r in range(n_rep):
-        w_out[(me,) + bits_of(r, nb)] = dxn[:own_out, r * cols_out : (r + 1) * cols_out].astype(B16)
+        @pl.when(rep != r)
+        def _():
+            w_out[(me,) + bits_of(r, nb)] = dxn[:own_out, r * cols_out : (r + 1) * cols_out].astype(B16)
+
     loads = [
         pltpu.make_async_copy(ms[i].at[span(rep, rows_in), pl.ds(at, size)], moment_in.at[:, pl.ds(to, size)], load_sem.at[n])
         for n, (i, at, to, size) in enumerate(places)
@@ -860,18 +900,20 @@
         tiles(all_in // TILE, columns)
 
     project(me, True)
-    items = [(get_in, k, k) for k in range(n_shard - 1)] + [(get_out, k, n_shard + k) for k in range(n_shard - 1)]
+    items = [(get_in, k, k) for k in range(n_shard - 1)] + [(get_out, k, n_shard - 1 + k) for k in range(n_shard - 1)]
 
     def gather_time(t):
+        for gather, k, at in items:
+            if t == (k if gather is get_in else k + 1):
+                gather.arrive(k)
         for gather, k, at in items:
             if 0 <= t - at <= nb:
                 gather.event(k, t - at, project if gather is get_in else None)
 
     first_phase = n_shard - 1 + nb
+    get_out.start()
     for t in range(first_phase):
         gather_time(t)
-        if t == 1:
-            get_out.start()
     later = list(range(first_phase, items[-1][2] + nb + 1))
 
     def tables():
@@ -986,7 +1028,7 @@
 
     def backward(p):
         for t in range(in_loop):
-            @pl.when(p == 1 + (t * (pairs - 1)) // in_loop)
+            @pl.when(p == 1 + (t * (pairs - 2)) // max(in_loop - 1, 1))
             def _():
                 reduce_time(sum_out, t)
 
@@ -1077,6 +1119,8 @@
         out[:, c] = (tok[:, c].astype(F32) + x).astype(B16)
 
     def gather_sums_time(who, t):
+        if t < n_shard - 1:
+            who.whole.arrive(t)
         for i in range(n_shard):
             if 0 <= t - i <= nb:
                 who.gather_event(i, t - i)
@@ -1095,15 +1139,15 @@
             then(reduce_time, sum_out, in_loop + u)
         if u < n_reduce:
             then(reduce_time, sum_in[0], u)
+        if u == n_reduce:
+            then(sum_in[0].finish, decay)
         if 0 <= u - 2 < n_reduce:
             then(reduce_time, sum_in[1], u - 2)
         if u == out_end + 1:
             then(sum_out.finish, decay)
-        if u == n_reduce + 1:
-            then(sum_in[0].finish, decay)
-        if u == n_reduce + 3:
+        if u == n_reduce + 2:
             then(sum_in[1].finish, decay)
-        for who, lag in ((sum_in[0], n_reduce + 2), (sum_in[1], n_reduce + 4), (sum_out, out_end + 2)):
+        for who, lag in ((sum_in[0], n_reduce + 1), (sum_in[1], n_reduce + 3), (sum_out, out_end + 2)):
             if 0 <= u - lag < n_gather:
                 then(gather_sums_time, who, u - lag)
         if 0 <= u - n_reduce - 3 < nb:
@@ -1120,15 +1164,20 @@
     sum_gain.send(0).start()
     advance()
     tiles(seq // rows, token_grad)
+    gone = [pltpu.make_async_copy(grad_tok, grad_hbm, load_sem.at[16]), pltpu.make_async_copy(out, out_hbm, load_sem.at[17])]
+    gone[0].start()
     advance()
     tiles(n_rep // 2, output)
     advance()
     tiles(n_rep // 2, lambda r: output(r + n_rep // 2))
+    gone[1].start()
     while todo:
         advance()
 
     for who in (get_in, get_out, sum_out, *sum_in):
         who.drain()
+    for copy in gone:
+        copy.wait()
     for way in WAYS:
         for k in range(n_shard - 1):
             @pl.when(links.goes(way, k))
@@ -1152,7 +1201,7 @@
     vmem, any_ = pl.BlockSpec(memory_space=pltpu.VMEM), pl.BlockSpec(memory_space=pl.ANY)
     V, D = pltpu.VMEM, pltpu.SemaphoreType.DMA
     n_sems = (
-        5 * 2 * (n_shard - 1) * (1 + 2 * nb) + 3 * (n_shard * (1 + 2 * (nb - 1)) + n_shard - 1 + 2 * nb) + nb + 3 * n_shard
+        5 * 2 * (n_shard - 1) * (2 + 2 * nb) + 3 * (n_shard * (1 + 2 * (nb - 1)) + n_shard - 1 + 2 * nb) + nb + 3 * n_shard
     )
     bufs = [V((n_shard,) + (2,) * (nb - 1 - j) + piece, B16) for piece in (piece_in, piece_out) for j in range(nb)]
     shape = jax.ShapeDtypeStruct
@@ -1168,8 +1217,10 @@
             shape((1, own_in), F32),
         ],
         in_specs=[any_] * 2 + [vmem] * 3 + [any_] * 8,
-        out_specs=[vmem] * 2 + [any_] * 4 + [vmem],
+        out_specs=[any_] * 6 + [vmem],
         scratch_shapes=[
+            V((seq, width), B16),
+            V((seq, width), B16),
             V((seq, width), B16),
             V((seq, width), B16),
             V((n_shard,) + bits + piece_in, B16),
@@ -1207,7 +1258,7 @@
             V((n_shard,) + piece_out, B16),
             V(piece_out, B16),
             V(piece_out, B16),
-            D((9,)),
+            D((18,)),
             D((3,)),
             D((n_sems,)),
             D((n_sems,)),
@@ -1217,7 +1268,7 @@
             collective_id=collective_id, has_side_effects=True, vmem_limit_bytes=67_043_328
         ),
         name="layer",
-    )(tok, cot, seg[None], frequency, lax.reduce_precision(gain, 8, 7)[None], *weights, *moments)
+    )(tok, cot, seg[None], frequency, gain[None], *weights, *moments)
 
 
 gain_rate = 0.2

time: 256 us -> 243 us (0.949)
  Pallas kernels: 253 us -> 240 us
    pallas_call x1, Pallas kernels: 58.6 us -> 49.5 us  [muon(): pl.pallas_call(muon_kernel, out_shape=own + own + [jax.ShapeDtypeStruct(p...]
    pallas_call x1, Pallas kernels: 186 us -> 183 us  [layer(): pl.pallas_call(functools.partial(layer_kernel, n_rep, n_shard, decay), ou...]
where the time goes in v6:
time: 243 us; the launch traced here: 242 us
  Pallas kernels  240 us (99%)
    pallas_call x1, Pallas kernels, layer(): pl.pallas_call(functools.partial(layer_kernel, n_rep, n_shard, decay), ou...  183 us
    pallas_call x1, Pallas kernels, muon(): pl.pallas_call(muon_kernel, out_shape=own + own + [jax.ShapeDtypeStruct(p...  49.5 us
    pallas_call x1, Pallas kernels, update(): pl.pallas_call(update_kernel, out_shape=[jax.ShapeDtypeStruct(s[::-1] if...  5.24 us

profile of v6, /device:TPU:0, one launch (start us, length us, event | category | flops | bytes accessed | tf_op | source)
XLA Modules:
  0.0 242.4 jit_solution(16581126472694027233)
XLA Ops:
  0.7 182.8 %layer.1 = (bf16[512,2048]{1,0:T(8,128)(2,1)}, bf16[512,2048]{1,0:T(8,128)(2,1)}, bf16[2,2,2,64,1536]{4,3,2,1,0:T(8,128)(2,1)}, bf16[2,2,2,256,256]{4,3,2,1,0:T(...) custom-call(bf16[512,2048]{1,0:T(8,128)(2,1)} %bitcast.15, ...), custom_call_target="tpu_custom_call" | custom-call | tf_op jit(solution)/shard_map/layer/pallas_call | solution.py:1208
  183.5 49.5 %muon.1 = (f32[512,1024]{1,0:T(8,128)}, f32[512,256]{1,0:T(8,128)}, f32[512,256]{1,0:T(8,128)}, f32[256,2048]{1,0:T(8,128)}, f32[512,1024]{1,0:T(8,128)}, /*inde...) custom-call(bf16[2048,1536]{1,0:T(8,128)(2,1)} %bitcast.14, ...), custom_call_target="tpu_custom_call" | custom-call | tf_op jit(solution)/shard_map/muon/pallas_call | solution.py:294
  233.1 2.8 %swap.1 = (bf16[256,1024]{1,0:T(8,128)(2,1)}, bf16[256,256]{1,0:T(8,128)(2,1)}, f32[8,128]{1,0:T(8,128)}) custom-call(bf16[1024,1024]{1,0:T(8,128)(2,1)} %get-tuple-element.57.h, bf16[256,256]{1,0:T(8,128)(2,1)} %get-tuple-element.58.hs, f32[8,128]{1,0:T(8,128)} %get-tuple-element.59.scal), custom_call_target="tpu_custom_call" | custom-call | tf_op jit(solution)/shard_map/swap/pallas_call | solution.py:351
  235.9 0.0 copy-start
  235.9 0.0 copy-start.1
  235.9 0.0 copy-start.2
  235.9 5.2 %update.1 = (f32[512,128]{1,0:T(8,128)}, f32[32,512]{1,0:T(8,128)}, f32[32,512]{1,0:T(8,128)}, f32[256,256]{1,0:T(8,128)}) custom-call(bf16[1024,1024]{1,0:T(8,128)(2,1)} %get-tuple-element.57.h, bf16[256,1024]{1,0:T(8,128)(2,1)} %get-tuple-element.60.h_pair, bf16[256,256]{1,0:T(8,128)(2,1)} %get-tuple-element.58.hs, ...), custom_call_target="tpu_custom_call" | custom-call | tf_op jit(solution)/shard_map/update/pallas_call | solution.py:446
  241.2 0.0 copy-done
  241.2 0.0 copy-done.1
  241.2 0.0 copy-done.2
  241.2 0.6 multiply_subtract_fusion
  241.8 0.6 copy.32
Async XLA Ops:
  235.9 5.3 %copy-start = (f32[512]{0:T(512)S(1)}, f32[512]{0:T(512)}, u32[]{:S(2)}) copy-start(f32[512]{0:T(512)} %param.17) | copy-start | bytes 6148
  235.9 5.3 %copy-start.1 = (f32[1,512]{1,0:T(1,128)S(1)}, f32[1,512]{1,0:T(1,128)}, u32[]{:S(2)}) copy-start(f32[1,512]{1,0:T(1,128)} %get-tuple-element.52) | copy-start | bytes 6148
  235.9 5.3 %copy-start.2 = (f32[512]{0:T(512)S(1)}, f32[512]{0:T(512)}, u32[]{:S(2)}) copy-start(f32[512]{0:T(512)} %param.22) | copy-start | bytes 6148

commit v7 on v6

--- a/solution.py
+++ b/solution.py
@@ -548,6 +548,16 @@
                         def _():
                             self.line(way, k + 1, h).start()
 
+    def times(self):
+        return self.links.n_shard + self.links.n_bits
+
+    def time(self, t):
+        if t < self.links.n_shard - 1:
+            self.arrive(t)
+        for k in range(self.links.n_shard - 1):
+            if 0 <= t - 1 - k <= self.links.n_bits:
+                self.event(k, t - 1 - k)
+
     def event(self, k, step, then=None):
         links = self.links
         for way in WAYS:
@@ -577,11 +587,61 @@
                             self.plane(way, k, h, step).wait_send()
 
 
+class Spread:
+    def __init__(self, links, name, full, half, first):
+        self.links, self.name, self.full, self.half, self.first = links, name, full, half, first
+
+    def line(self, k, h):
+        links = self.links
+        d = lax.rem(links.shard + 1 + k, links.n_shard)
+        into = self.full.at[(links.shard,) + links.where() + self.half[h]]
+        return links.remote(self.first.at[self.half[h]], into, (self.name, "l", k, h), links.rep, d)
+
+    def origin(self, k):
+        return lax.rem(self.links.shard + self.links.n_shard - 1 - k, self.links.n_shard)
+
+    def came(self, k, h):
+        links = self.links
+        at = self.full.at[(self.origin(k),) + links.where() + self.half[h]]
+        return links.remote(at, at, (self.name, "l", k, h), links.rep, links.shard)
+
+    def plane(self, k, h, step):
+        links = self.links
+        order = links.orders[h] + [0]
+        view = self.full.at[(self.origin(k),) + links.where(order[:step]) + self.half[h]]
+        return links.remote(view, view, (self.name, "p", k, h, step), links.flip(order[step]), links.shard)
+
+    def start(self):
+        for k in range(self.links.n_shard - 1):
+            for h in range(2):
+                self.line(k, h).start()
+
+    def times(self):
+        return self.links.n_bits + 1
+
+    def time(self, step):
+        for k in range(self.links.n_shard - 1):
+            for h in range(2):
+                if step == 0:
+                    self.came(k, h).wait_recv()
+                else:
+                    self.plane(k, h, step - 1).wait_recv()
+                if step < self.links.n_bits:
+                    self.plane(k, h, step).start()
+
+    def drain(self):
+        for k in range(self.links.n_shard - 1):
+            for h in range(2):
+                self.line(k, h).wait_send()
+                for step in range(self.links.n_bits):
+                    self.plane(k, h, step).wait_send()
+
+
 class Reduce:
-    def __init__(self, links, name, refs, region, half, keep_sem):
+    def __init__(self, links, name, refs, region, half, keep_sem, way_of_whole):
         self.links, self.name, self.region, self.half = links, name, region, half
         self.part, self.bufs, self.zbuf, self.gpiece, self.mpiece, self.moment, self.sums, wholes = refs
-        self.whole = Gather(links, name + "m", wholes, half, self.mpiece)
+        self.whole = way_of_whole(links, name + "m", wholes, half, self.mpiece)
         self.keep = lambda: pltpu.make_async_copy(
             self.gpiece.at[region], self.sums.at[links.where() + region], keep_sem
         )
@@ -674,10 +734,7 @@
             self.gather_sum(h, 0).start()
         self.keep().start()
 
-    def gather_event(self, i, step):
-        if i > 0:
-            self.whole.event(i - 1, step)
-            return
+    def gather_event(self, step):
         if step == 0:
             self.keep().wait()
         if step < self.links.n_bits:
@@ -685,6 +742,7 @@
                 self.gather_sum(h, step).wait_recv()
                 if step + 1 < self.links.n_bits:
                     self.gather_sum(h, step + 1).start()
+        self.whole.time(step)
 
     def drain(self):
         links = self.links
@@ -786,8 +844,8 @@
     get_in, get_out = Gather(links, "wi", w_in, half_in), Gather(links, "wo", w_out, half_out)
     refs_in = (part_in, bufs[:nb], zbuf_in, gp_in, mp_in, moment_in, sums_in, wholes_in)
     refs_out = (part_out, bufs[nb:], zbuf_out, gp_out, mp_out, moment_out, sums_out, wholes_out)
-    sum_in = [Reduce(links, f"i{c}", refs_in, part_cols[c], half_cols[c], keep_sem.at[c]) for c in range(2)]
-    sum_out = Reduce(links, "o", refs_out, (both, both), half_out, keep_sem.at[2])
+    sum_in = [Reduce(links, f"i{c}", refs_in, part_cols[c], half_cols[c], keep_sem.at[c], Spread) for c in range(2)]
+    sum_out = Reduce(links, "o", refs_out, (both, both), half_out, keep_sem.at[2], Gather)
     sum_gain = GainSum(links, gain_acc, gain_come, gain_line)
 
     ws, ms = (w_query, w_key, w_value), (m_query, m_key, m_value)
@@ -1022,7 +1080,7 @@
         for k in range(n_shard):
             sum_in[c].start(k)
 
-    n_reduce, n_gather = n_shard + nb - 1, n_shard + nb
+    n_reduce = n_shard + nb - 1
 
     in_loop = (2 * n_reduce) // 3
 
@@ -1119,11 +1177,7 @@
         out[:, c] = (tok[:, c].astype(F32) + x).astype(B16)
 
     def gather_sums_time(who, t):
-        if t < n_shard - 1:
-            who.whole.arrive(t)
-        for i in range(n_shard):
-            if 0 <= t - i <= nb:
-                who.gather_event(i, t - i)
+        who.gather_event(t)
 
     todo = []
 
@@ -1134,7 +1188,7 @@
         gain_out[...] = sum_gain.end()
 
     out_end = n_reduce - in_loop
-    for u in range(3 * n_gather + n_reduce):
+    for u in range(3 * (n_shard + nb) + n_reduce):
         if u < out_end:
             then(reduce_time, sum_out, in_loop + u)
         if u < n_reduce:
@@ -1148,11 +1202,11 @@
         if u == n_reduce + 2:
             then(sum_in[1].finish, decay)
         for who, lag in ((sum_in[0], n_reduce + 1), (sum_in[1], n_reduce + 3), (sum_out, out_end + 2)):
-            if 0 <= u - lag < n_gather:
+            if 0 <= u - lag < who.whole.times():
                 then(gather_sums_time, who, u - lag)
-        if 0 <= u - n_reduce - 3 < nb:
-            then(sum_gain.event, u - n_reduce - 3)
-        if u == n_reduce + nb + 4:
+        if 0 <= u - 3 < nb:
+            then(sum_gain.event, u - 3)
+        if u == n_reduce + nb:
             then(gain_end)
 
     def advance():

time: 243 us -> 236 us (0.971)
  Pallas kernels: 240 us -> 234 us
    pallas_call x1, Pallas kernels: 183 us -> 177 us  [layer(): pl.pallas_call(functools.partial(layer_kernel, n_rep, n_shard, decay), ou...]
where the time goes in v7:
time: 236 us
  Pallas kernels  234 us (99%)
    pallas_call x1, Pallas kernels, layer(): pl.pallas_call(functools.partial(layer_kernel, n_rep, n_shard, decay), ou...  177 us
    pallas_call x1, Pallas kernels, muon(): pl.pallas_call(muon_kernel, out_shape=own + own + [jax.ShapeDtypeStruct(p...  49.5 us
    pallas_call x1, Pallas kernels, update(): pl.pallas_call(update_kernel, out_shape=[jax.ShapeDtypeStruct(s[::-1] if...  5.24 us

profile of v7, /device:TPU:0, one launch (start us, length us, event | category | flops | bytes accessed | tf_op | source)
XLA Modules:
  0.0 236.2 jit_solution(1643363843269762849)
XLA Ops:
  0.7 176.7 %layer.1 = (bf16[512,2048]{1,0:T(8,128)(2,1)}, bf16[512,2048]{1,0:T(8,128)(2,1)}, bf16[2,2,2,64,1536]{4,3,2,1,0:T(8,128)(2,1)}, bf16[2,2,2,256,256]{4,3,2,1,0:T(...) custom-call(bf16[512,2048]{1,0:T(8,128)(2,1)} %bitcast.15, ...), custom_call_target="tpu_custom_call" | custom-call | tf_op jit(solution)/shard_map/layer/pallas_call | solution.py:1262
  177.3 49.5 %muon.1 = (f32[512,1024]{1,0:T(8,128)}, f32[512,256]{1,0:T(8,128)}, f32[512,256]{1,0:T(8,128)}, f32[256,2048]{1,0:T(8,128)}, f32[512,1024]{1,0:T(8,128)}, /*inde...) custom-call(bf16[2048,1536]{1,0:T(8,128)(2,1)} %bitcast.14, ...), custom_call_target="tpu_custom_call" | custom-call | tf_op jit(solution)/shard_map/muon/pallas_call | solution.py:294
  226.9 2.8 %swap.1 = (bf16[256,1024]{1,0:T(8,128)(2,1)}, bf16[256,256]{1,0:T(8,128)(2,1)}, f32[8,128]{1,0:T(8,128)}) custom-call(bf16[1024,1024]{1,0:T(8,128)(2,1)} %get-tuple-element.57.h, bf16[256,256]{1,0:T(8,128)(2,1)} %get-tuple-element.58.hs, f32[8,128]{1,0:T(8,128)} %get-tuple-element.59.scal), custom_call_target="tpu_custom_call" | custom-call | tf_op jit(solution)/shard_map/swap/pallas_call | solution.py:351
  229.7 0.0 copy-start
  229.7 0.0 copy-start.1
  229.7 0.0 copy-start.2
  229.7 5.2 %update.1 = (f32[512,128]{1,0:T(8,128)}, f32[32,512]{1,0:T(8,128)}, f32[32,512]{1,0:T(8,128)}, f32[256,256]{1,0:T(8,128)}) custom-call(bf16[1024,1024]{1,0:T(8,128)(2,1)} %get-tuple-element.57.h, bf16[256,1024]{1,0:T(8,128)(2,1)} %get-tuple-element.60.h_pair, bf16[256,256]{1,0:T(8,128)(2,1)} %get-tuple-element.58.hs, ...), custom_call_target="tpu_custom_call" | custom-call | tf_op jit(solution)/shard_map/update/pallas_call | solution.py:446
  235.0 0.0 copy-done
  235.0 0.0 copy-done.1
  235.0 0.0 copy-done.2
  235.0 0.6 multiply_subtract_fusion
  235.6 0.6 copy.32
Async XLA Ops:
  229.7 5.3 %copy-start = (f32[512]{0:T(512)S(1)}, f32[512]{0:T(512)}, u32[]{:S(2)}) copy-start(f32[512]{0:T(512)} %param.17) | copy-start | bytes 6148
  229.7 5.3 %copy-start.1 = (f32[1,512]{1,0:T(1,128)S(1)}, f32[1,512]{1,0:T(1,128)}, u32[]{:S(2)}) copy-start(f32[1,512]{1,0:T(1,128)} %get-tuple-element.52) | copy-start | bytes 6148
  229.7 5.3 %copy-start.2 = (f32[512]{0:T(512)S(1)}, f32[512]{0:T(512)}, u32[]{:S(2)}) copy-start(f32[512]{0:T(512)} %param.22) | copy-start | bytes 6148

commit v8 on v7

--- a/solution.py
+++ b/solution.py
@@ -841,7 +841,8 @@
     half_cols = [[(both, pl.ds(c * chunk + h * (chunk // 2), chunk // 2)) for h in range(2)] for c in range(2)]
     half_in = [(both, pl.ds(h * chunk, chunk)) for h in range(2)]
     half_out = [(pl.ds(h * (own_out // 2), own_out // 2), both) for h in range(2)]
-    get_in, get_out = Gather(links, "wi", w_in, half_in), Gather(links, "wo", w_out, half_out)
+    get_in = Gather(links, "wi", w_in, half_in)
+    get_out = Spread(links, "wo", w_out, half_out, w_out.at[(links.shard,) + links.where()])
     refs_in = (part_in, bufs[:nb], zbuf_in, gp_in, mp_in, moment_in, sums_in, wholes_in)
     refs_out = (part_out, bufs[nb:], zbuf_out, gp_out, mp_out, moment_out, sums_out, wholes_out)
     sum_in = [Reduce(links, f"i{c}", refs_in, part_cols[c], half_cols[c], keep_sem.at[c], Spread) for c in range(2)]
@@ -958,21 +959,22 @@
         tiles(all_in // TILE, columns)
 
     project(me, True)
-    items = [(get_in, k, k) for k in range(n_shard - 1)] + [(get_out, k, n_shard - 1 + k) for k in range(n_shard - 1)]
+    first_phase, lag = n_shard - 1 + nb, n_shard
 
     def gather_time(t):
-        for gather, k, at in items:
-            if t == (k if gather is get_in else k + 1):
-                gather.arrive(k)
-        for gather, k, at in items:
-            if 0 <= t - at <= nb:
-                gather.event(k, t - at, project if gather is get_in else None)
-
-    first_phase = n_shard - 1 + nb
-    get_out.start()
+        if t < n_shard - 1:
+            get_in.arrive(t)
+        for k in range(n_shard - 1):
+            if 0 <= t - k <= nb:
+                get_in.event(k, t - k, project)
+        if t == n_shard - 2:
+            get_out.start()
+        if 0 <= t - lag < get_out.times():
+            get_out.time(t - lag)
+
     for t in range(first_phase):
         gather_time(t)
-    later = list(range(first_phase, items[-1][2] + nb + 1))
+    later = list(range(first_phase, lag + get_out.times()))
 
     def tables():
         c, s = cosine[...], sine[...]

time: 236 us -> 235 us (level)
  no operation moved by 1% of the time
where the time goes in v8:
time: 235 us; the launch traced here: 234 us
  Pallas kernels  232 us (99%)
    pallas_call x1, Pallas kernels, layer(): pl.pallas_call(functools.partial(layer_kernel, n_rep, n_shard, decay), ou...  175 us
    pallas_call x1, Pallas kernels, muon(): pl.pallas_call(muon_kernel, out_shape=own + own + [jax.ShapeDtypeStruct(p...  49.5 us
    pallas_call x1, Pallas kernels, update(): pl.pallas_call(update_kernel, out_shape=[jax.ShapeDtypeStruct(s[::-1] if...  5.24 us

profile of v8, /device:TPU:0, one launch (start us, length us, event | category | flops | bytes accessed | tf_op | source)
XLA Modules:
  0.0 234.3 jit_solution(1759345191005358275)
XLA Ops:
  0.7 174.9 %layer.1 = (bf16[512,2048]{1,0:T(8,128)(2,1)}, bf16[512,2048]{1,0:T(8,128)(2,1)}, bf16[2,2,2,64,1536]{4,3,2,1,0:T(8,128)(2,1)}, bf16[2,2,2,256,256]{4,3,2,1,0:T(...) custom-call(bf16[512,2048]{1,0:T(8,128)(2,1)} %bitcast.15, ...), custom_call_target="tpu_custom_call" | custom-call | tf_op jit(solution)/shard_map/layer/pallas_call | solution.py:1264
  175.5 49.5 %muon.1 = (f32[512,1024]{1,0:T(8,128)}, f32[512,256]{1,0:T(8,128)}, f32[512,256]{1,0:T(8,128)}, f32[256,2048]{1,0:T(8,128)}, f32[512,1024]{1,0:T(8,128)}, /*inde...) custom-call(bf16[2048,1536]{1,0:T(8,128)(2,1)} %bitcast.14, ...), custom_call_target="tpu_custom_call" | custom-call | tf_op jit(solution)/shard_map/muon/pallas_call | solution.py:294
  225.1 2.8 %swap.1 = (bf16[256,1024]{1,0:T(8,128)(2,1)}, bf16[256,256]{1,0:T(8,128)(2,1)}, f32[8,128]{1,0:T(8,128)}) custom-call(bf16[1024,1024]{1,0:T(8,128)(2,1)} %get-tuple-element.57.h, bf16[256,256]{1,0:T(8,128)(2,1)} %get-tuple-element.58.hs, f32[8,128]{1,0:T(8,128)} %get-tuple-element.59.scal), custom_call_target="tpu_custom_call" | custom-call | tf_op jit(solution)/shard_map/swap/pallas_call | solution.py:351
  227.9 0.0 copy-start
  227.9 0.0 copy-start.1
  227.9 0.0 copy-start.2
  227.9 5.2 %update.1 = (f32[512,128]{1,0:T(8,128)}, f32[32,512]{1,0:T(8,128)}, f32[32,512]{1,0:T(8,128)}, f32[256,256]{1,0:T(8,128)}) custom-call(bf16[1024,1024]{1,0:T(8,128)(2,1)} %get-tuple-element.57.h, bf16[256,1024]{1,0:T(8,128)(2,1)} %get-tuple-element.60.h_pair, bf16[256,256]{1,0:T(8,128)(2,1)} %get-tuple-element.58.hs, ...), custom_call_target="tpu_custom_call" | custom-call | tf_op jit(solution)/shard_map/update/pallas_call | solution.py:446
  233.1 0.0 copy-done
  233.1 0.0 copy-done.1
  233.2 0.0 copy-done.2
  233.2 0.6 multiply_subtract_fusion
  233.8 0.6 copy.32
Async XLA Ops:
  227.9 5.3 %copy-start = (f32[512]{0:T(512)S(1)}, f32[512]{0:T(512)}, u32[]{:S(2)}) copy-start(f32[512]{0:T(512)} %param.17) | copy-start | bytes 6148
  227.9 5.3 %copy-start.1 = (f32[1,512]{1,0:T(1,128)S(1)}, f32[1,512]{1,0:T(1,128)}, u32[]{:S(2)}) copy-start(f32[1,512]{1,0:T(1,128)} %get-tuple-element.52) | copy-start | bytes 6148
  227.9 5.3 %copy-start.2 = (f32[512]{0:T(512)S(1)}, f32[512]{0:T(512)}, u32[]{:S(2)}) copy-start(f32[512]{0:T(512)} %param.22) | copy-start | bytes 6148
